TPU v7x, 256 devices: a whole 4x4x8 slice. The times are simulated.
256 devices in a mesh: ta: 32 (over z, x_hi, core), gz: 2 (over x_lo), gy: 4 (over y).
Axes of the slice: x: 4 (x_hi: 2, x_lo: 2; x = x_hi * 2 + x_lo), y: 4, z: 8, core: 2. Of those that a mesh axis runs over, the one named last changes fastest.
Arguments:
- lattice_links: float32 [2, 4, 18, 64, 16, 1024], P(None, None, None, 'ta', 'gz', 'gy'), may hold values from -1 to 1, as said below
- transform: float32 [2, 18, 64, 16, 1024], P(None, None, 'ta', 'gz', 'gy'), may hold values from -1 to 1, as said below
Outputs:
- fixed_transform: float32 [2, 18, 64, 16, 1024], P(None, None, 'ta', 'gz', 'gy')
- monitor: float32 [2, 2], replicated
Inputs may be any that keep to these rules, and one draw needn't show every extreme that they name: `lattice_links`: every site's matrix for every colour and direction is special unitary. `transform`: every site's matrix is special unitary.
All inputs are finite; a program needn't handle non-finite values.
Results may differ from a plain program's by a relative error of at most 0.0003.
Values sent between devices are 32-bit elements; how exact they have to be, the bound alone decides.
No kernel may reach another device: no remote copies, remote signals or barrier semaphores. Data moves between devices by JAX's collectives and lax.ppermute only.
A program may use at most 128 MiB of HBM per device.

v0:
```python
import functools

import jax
import jax.numpy as jnp
from jax import lax
from jax.sharding import Mesh
from jax.sharding import PartitionSpec as P

NX = 64
ITERS = 2
TA = ("ta_0", "ta_1", "ta_2")
TA_GZ_GY = ("ta_0", "ta_1", "ta_2", "gz", "gy")


OMEGA = 1.7
GUARD = 1e-12


def shifted(value, axis, steps):
    count = lax.axis_size(axis)
    pairs = [(source, (source + steps) % count) for source in range(count)]
    return lax.ppermute(value, axis, pairs)


def over_axes(shard, axes):
    return functools.reduce(lax.psum, axes, shard)


def split_matrix(values):
    lead = values.shape[1:]
    return (values[:9].reshape((3, 3) + lead), values[9:].reshape((3, 3) + lead))


def join_matrix(mat_re, mat_im):
    lead = mat_re.shape[2:]
    return jnp.concatenate([mat_re.reshape((9,) + lead), mat_im.reshape((9,) + lead)], 0)


def product(left_re, left_im, right_re, right_im):
    total_re = None
    total_im = None
    for inner in range(3):
        col_re = left_re[:, inner][:, None]
        col_im = left_im[:, inner][:, None]
        row_re = right_re[inner][None]
        row_im = right_im[inner][None]
        term_re = col_re * row_re - col_im * row_im
        term_im = col_re * row_im + col_im * row_re
        if total_re is None:
            total_re = term_re
            total_im = term_im
        else:
            total_re = total_re + term_re
            total_im = total_im + term_im
    return (total_re, total_im)


def adjoint(mat_re, mat_im):
    return (jnp.swapaxes(mat_re, 0, 1), -jnp.swapaxes(mat_im, 0, 1))


def along_x(values, offset, forward, half_len):
    column = jnp.arange(values.shape[-1], dtype=jnp.int32) % half_len
    if forward:
        stepped = jnp.where(
            column == half_len - 1, jnp.roll(values, half_len - 1, -1), jnp.roll(values, -1, -1)
        )
        return jnp.where(offset == 0, values, stepped)
    stepped = jnp.where(column == 0, jnp.roll(values, 1 - half_len, -1), jnp.roll(values, 1, -1))
    return jnp.where(offset == 0, stepped, values)


def rotation(mat_re, mat_im, row_one, row_two):
    vec_zero = mat_re[row_one, row_one] + mat_re[row_two, row_two]
    vec_one = -(mat_im[row_one, row_two] + mat_im[row_two, row_one])
    vec_two = mat_re[row_two, row_one] - mat_re[row_one, row_two]
    vec_three = -(mat_im[row_one, row_one] - mat_im[row_two, row_two])
    length = jnp.sqrt(
        vec_zero * vec_zero + vec_one * vec_one + vec_two * vec_two + vec_three * vec_three
    )
    step_zero = (1.0 - OMEGA) * length + OMEGA * vec_zero
    step_one = OMEGA * vec_one
    step_two = OMEGA * vec_two
    step_three = OMEGA * vec_three
    divisor = jnp.sqrt(
        step_zero * step_zero
        + step_one * step_one
        + step_two * step_two
        + step_three * step_three
        + GUARD
    )
    return (step_zero / divisor, step_one / divisor, step_two / divisor, step_three / divisor)


def rotate(mat_re, mat_im, quat, row_one, row_two):
    q_zero, q_one, q_two, q_three = quat
    upper_re, upper_im = (mat_re[row_one], mat_im[row_one])
    lower_re, lower_im = (mat_re[row_two], mat_im[row_two])

    def combine(left_pair, right_pair):
        left_re, left_im = (left_pair[0][None], left_pair[1][None])
        right_re, right_im = (right_pair[0][None], right_pair[1][None])
        new_re = left_re * upper_re - left_im * upper_im + right_re * lower_re - right_im * lower_im
        new_im = left_re * upper_im + left_im * upper_re + right_re * lower_im + right_im * lower_re
        return (new_re, new_im)

    top_re, top_im = combine((q_zero, q_three), (q_two, q_one))
    bottom_re, bottom_im = combine((-q_two, q_one), (q_zero, -q_three))
    rows_re = [mat_re[0], mat_re[1], mat_re[2]]
    rows_im = [mat_im[0], mat_im[1], mat_im[2]]
    rows_re[row_one] = top_re
    rows_im[row_one] = top_im
    rows_re[row_two] = bottom_re
    rows_im[row_two] = bottom_im
    return (jnp.stack(rows_re, 0), jnp.stack(rows_im, 0))


def relax(own, own_links, forward, backward):
    gauge_re, gauge_im = split_matrix(own)
    sum_re = None
    sum_im = None
    for direction in range(4):
        link_re, link_im = split_matrix(own_links[direction])
        next_re, next_im = adjoint(forward[direction][0], forward[direction][1])
        ahead_re, ahead_im = product(link_re, link_im, next_re, next_im)
        behind_re, behind_im = adjoint(backward[direction][0], backward[direction][1])
        if sum_re is None:
            sum_re = ahead_re + behind_re
            sum_im = ahead_im + behind_im
        else:
            sum_re = sum_re + ahead_re + behind_re
            sum_im = sum_im + ahead_im + behind_im
    mat_re, mat_im = product(gauge_re, gauge_im, sum_re, sum_im)
    for row_one, row_two in ((0, 1), (0, 2), (1, 2)):
        quat = rotation(mat_re, mat_im, row_one, row_two)
        mat_re, mat_im = rotate(mat_re, mat_im, quat, row_one, row_two)
        gauge_re, gauge_im = rotate(gauge_re, gauge_im, quat, row_one, row_two)
    return (join_matrix(gauge_re, gauge_im), mat_re, mat_im)


def measures(mat_re, mat_im):
    diag_sum = mat_re[0, 0] + mat_re[1, 1] + mat_re[2, 2]
    skew_re = 0.5 * (mat_re - jnp.swapaxes(mat_re, 0, 1))
    skew_im = 0.5 * (mat_im + jnp.swapaxes(mat_im, 0, 1))
    mean_im = (skew_im[0, 0] + skew_im[1, 1] + skew_im[2, 2]) / 3.0
    identity = jnp.eye(3, dtype=jnp.float32).reshape((3, 3) + (1,) * diag_sum.ndim)
    skew_im = skew_im - identity * mean_im[None, None]
    return (jnp.sum(diag_sum), jnp.sum(skew_re * skew_re + skew_im * skew_im))


def pass_time(face, stride):
    return shifted(face, TA, stride)


def pass_depth(face, stride):
    return shifted(face, "gz", stride)


def pass_rows(face, stride):
    return shifted(face, "gy", stride)


def upper_side(values, direction, half_len):
    if direction == 1:
        return jnp.concatenate([values[..., half_len:], pass_rows(values[..., :half_len], -1)], 3)
    if direction == 2:
        return jnp.concatenate([values[:, :, 1:], pass_depth(values[:, :, :1], -1)], 2)
    return jnp.concatenate([values[:, 1:], pass_time(values[:, :1], -1)], 1)


def lower_side(values, direction, half_len):
    if direction == 1:
        return jnp.concatenate([pass_rows(values[..., -half_len:], 1), values[..., :-half_len]], 3)
    if direction == 2:
        return jnp.concatenate([pass_depth(values[:, :, -1:], 1), values[:, :, :-1]], 2)
    return jnp.concatenate([pass_time(values[:, -1:], 1), values[:, :-1]], 1)


def global_totals(values):
    return over_axes(values, TA_GZ_GY)


def shards(lattice_links, transform):
    half_len = NX // 2
    slices = transform.shape[2]
    depth = transform.shape[3]
    row_len = transform.shape[4]
    t_index = jnp.arange(slices, dtype=jnp.int32)[:, None, None]
    z_index = jnp.arange(depth, dtype=jnp.int32)[None, :, None]
    y_index = (jnp.arange(row_len, dtype=jnp.int32) // half_len)[None, None, :]
    parity = t_index + z_index + y_index
    offsets = [parity % 2, (parity + 1) % 2]
    colours = [transform[0], transform[1]]
    volume = (
        slices * depth * row_len * 2 * lax.axis_size(TA) * lax.axis_size("gz") * lax.axis_size("gy")
    )
    summed_rows = []
    for sweep in range(ITERS):
        for colour in (0, 1):
            partner = 1 - colour
            offset = offsets[colour]
            part_re, part_im = split_matrix(colours[partner])
            forward = []
            backward = []
            for direction in range(4):
                if direction == 0:
                    forward.append(
                        (
                            along_x(part_re, offset, True, half_len),
                            along_x(part_im, offset, True, half_len),
                        )
                    )
                else:
                    forward.append(split_matrix(upper_side(colours[partner], direction, half_len)))
                link_re, link_im = split_matrix(lattice_links[partner, direction])
                prod_re, prod_im = product(part_re, part_im, link_re, link_im)
                if direction == 0:
                    backward.append(
                        (
                            along_x(prod_re, offset, False, half_len),
                            along_x(prod_im, offset, False, half_len),
                        )
                    )
                else:
                    backward.append(
                        split_matrix(lower_side(join_matrix(prod_re, prod_im), direction, half_len))
                    )
            colours[colour], mat_re, mat_im = relax(
                colours[colour], lattice_links[colour], forward, backward
            )
        func_sum, div_sum = measures(mat_re, mat_im)
        summed_rows.append(global_totals(jnp.stack([func_sum, div_sum])))
    sums = jnp.stack(summed_rows, 1)
    monitor = jnp.stack([1.0 - sums[0] / (12.0 * volume), sums[1] / (volume / 2.0)], 0)
    return (jnp.stack(colours, 0), monitor)


def solution(mesh):
    finer = Mesh(
        mesh.devices.reshape(8, 2, 2, mesh.shape["gz"], mesh.shape["gy"]),
        ("ta_0", "ta_1", "ta_2", "gz", "gy"),
    )
    return jax.shard_map(
        shards,
        mesh=finer,
        in_specs=(P(None, None, None, TA, "gz", "gy"), P(None, None, TA, "gz", "gy")),
        out_specs=(P(None, None, TA, "gz", "gy"), P()),
        check_vma=False,
    )
```

profile of v0, /device:TPU:1, one launch (start us, length us, event | category | flops | bytes accessed | tf_op | source)
XLA Modules:
  0.0 121.5 jit_solution(9450456494978134214)
XLA Ops:
  0.6 1.3 %slice_bitcast_fusion.223 = (f32[3,2,8,256]{3,2,1,0:T(8,128)S(1)}, f32[3,2,8,256]{3,2,1,0:T(8,128)S(1)}, f32[3,2,8,256]{3,2,1,0:T(8,128)S(1)}, f32[3,2,8,256]{3,...) fusion(f32[2,4,18,2,8,256]{5,4,3,2,1,0:T(8,128)} %param.2), kind=kLoop, calls=%fused_computation.706 | loop fusion | bytes 1867776 | tf_op jit(solution)/shard_map/mul | solution.py:47
  1.9 1.1 slice_bitcast_fusion.248
  3.1 0.2 subtract_add_fusion.19
  3.4 2.2 %collective-permute-start.1 = (f32[18,2,8,32]{3,2,1,0:T(8,128)S(1)}, f32[18,2,8,32]{3,2,1,0:T(8,128)S(1)}, u32[]{:S(2)}, u32[]{:S(2)}) collective-permute-start(f32[18,2,8,32]{3,2,1,0:T(8,128)S(1)} %fusion.37), channel_id=1, source_target_pairs={{0,1},{1,2},{2,3},{3,0},{4,5},{5,6},{6,7},{7,4},{8,9},{9,10},{10,1... | collective-permute-start | bytes 110600 | tf_op jit(solution)/shard_map/ppermute | solution.py:22
  5.9 1.3 %collective-permute-start.3 = (f32[18,2,1,256]{3,2,1,0:T(1,128)S(1)}, f32[18,2,1,256]{3,2,1,0:T(1,128)S(1)}, u32[]{:S(2)}, u32[]{:S(2)}) collective-permute-start(f32[18,2,1,256]{3,2,1,0:T(1,128)S(1)} %pad_maximum_fusion.43), channel_id=1, source_target_pairs={{0,4},{4,0},{1,5},{5,1},{2,6},{6,2},{3,7},{7,3},{8,12},{12,8},{9,1... | collective-permute-start | bytes 110600 | tf_op jit(solution)/shard_map/ppermute | solution.py:22
  7.2 3.6 %collective-permute-start.5 = (f32[18,1,8,256]{3,2,1,0:T(8,128)S(1)}, f32[18,1,8,256]{3,2,1,0:T(8,128)S(1)}, u32[]{:S(2)}, u32[]{:S(2)}) collective-permute-start(f32[18,1,8,256]{3,2,1,0:T(8,128)S(1)} %fusion.34), channel_id=1, source_target_pairs={{0,8},{8,16},{16,24},{24,32},{32,40},{40,48},{48,56},{56,64},{64,7... | collective-permute-start | bytes 442376 | tf_op jit(solution)/shard_map/ppermute | solution.py:22
  11.0 1.5 %collective-permute-start = (f32[18,2,8,32]{3,2,1,0:T(8,128)S(1)}, f32[18,2,8,32]{3,2,1,0:T(8,128)S(1)}, u32[]{:S(2)}, u32[]{:S(2)}) collective-permute-start(f32[18,2,8,32]{3,2,1,0:T(8,128)S(1)} %slice.2830), channel_id=1, source_target_pairs={{0,3},{1,0},{2,1},{3,2},{4,7},{5,4},{6,5},{7,6},{8,11},{9,8},{10,9... | collective-permute-start | bytes 110600 | tf_op jit(solution)/shard_map/ppermute | solution.py:22
  12.9 0.2 fusion.317
  15.2 2.6 %collective-permute-done.2 = f32[18,2,1,256]{3,2,1,0:T(1,128)S(1)} collective-permute-done((f32[18,2,1,256]{3,2,1,0:T(1,128)S(1)}, f32[18,2,1,256]{3,2,1,0:T(1,128)S(1)}, u32[]{:S(2)}, u32[]{:S(2)}) %collective-permute-start.2) | collective-permute-done | bytes 36896 | tf_op jit(solution)/shard_map/ppermute | solution.py:22
  18.0 1.0 collective-permute-done.4
  19.1 0.5 fusion.71
  19.6 0.6 fusion.81
  22.5 1.3 %collective-permute-start.6 = (f32[18,2,8,32]{3,2,1,0:T(8,128)S(1)}, f32[18,2,8,32]{3,2,1,0:T(8,128)S(1)}, u32[]{:S(2)}, u32[]{:S(2)}) collective-permute-start(f32[18,2,8,32]{3,2,1,0:T(8,128)S(1)} %fusion.42), channel_id=1, source_target_pairs={{0,3},{1,0},{2,1},{3,2},{4,7},{5,4},{6,5},{7,6},{8,11},{9,8},{10,9... | collective-permute-start | bytes 110600 | tf_op jit(solution)/shard_map/ppermute | solution.py:22
  23.9 5.3 %collective-permute-start.10 = (f32[18,1,8,256]{3,2,1,0:T(8,128)S(1)}, f32[18,1,8,256]{3,2,1,0:T(8,128)S(1)}, u32[]{:S(2)}, u32[]{:S(2)}) collective-permute-start(f32[18,1,8,256]{3,2,1,0:T(8,128)S(1)} %get-tuple-element.311), channel_id=1, source_target_pairs={{0,248},{8,0},{16,8},{24,16},{32,24},{40,32},{48,40},{56,48},{64,5... | collective-permute-start | bytes 442376 | tf_op jit(solution)/shard_map/ppermute | solution.py:22
  29.3 0.7 collective-permute-start.7
  30.2 1.2 %collective-permute-start.9 = (f32[18,2,1,256]{3,2,1,0:T(1,128)S(1)}, f32[18,2,1,256]{3,2,1,0:T(1,128)S(1)}, u32[]{:S(2)}, u32[]{:S(2)}) collective-permute-start(f32[18,2,1,256]{3,2,1,0:T(1,128)S(1)} %pad_maximum_fusion.42), channel_id=1, source_target_pairs={{0,4},{4,0},{1,5},{5,1},{2,6},{6,2},{3,7},{7,3},{8,12},{12,8},{9,1... | collective-permute-start | bytes 110600 | tf_op jit(solution)/shard_map/ppermute | solution.py:22
  31.7 4.0 %collective-permute-done.7 = f32[18,2,8,32]{3,2,1,0:T(8,128)S(1)} collective-permute-done((f32[18,2,8,32]{3,2,1,0:T(8,128)S(1)}, f32[18,2,8,32]{3,2,1,0:T(8,128)S(1)}, u32[]{:S(2)}, u32[]{:S(2)}) %collective-permute-start.7) | collective-permute-done | bytes 36896 | tf_op jit(solution)/shard_map/ppermute | solution.py:22
  36.3 0.5 fusion.95
  36.9 0.6 fusion.105
  39.4 0.2 subtract_add_fusion.7
  40.0 0.8 collective-permute-start.12
  40.9 1.3 %collective-permute-start.14 = (f32[18,2,1,256]{3,2,1,0:T(1,128)S(1)}, f32[18,2,1,256]{3,2,1,0:T(1,128)S(1)}, u32[]{:S(2)}, u32[]{:S(2)}) collective-permute-start(f32[18,2,1,256]{3,2,1,0:T(1,128)S(1)} %fusion.195), channel_id=1, source_target_pairs={{0,4},{4,0},{1,5},{5,1},{2,6},{6,2},{3,7},{7,3},{8,12},{12,8},{9,1... | collective-permute-start | bytes 110600 | tf_op jit(solution)/shard_map/ppermute | solution.py:22
  42.2 5.6 %collective-permute-start.16 = (f32[18,1,8,256]{3,2,1,0:T(8,128)S(1)}, f32[18,1,8,256]{3,2,1,0:T(8,128)S(1)}, u32[]{:S(2)}, u32[]{:S(2)}) collective-permute-start(f32[18,1,8,256]{3,2,1,0:T(8,128)S(1)} %get-tuple-element.297), channel_id=1, source_target_pairs={{0,248},{8,0},{16,8},{24,16},{32,24},{40,32},{48,40},{56,48},{64,5... | collective-permute-start | bytes 442376 | tf_op jit(solution)/shard_map/ppermute | solution.py:22
  48.1 1.4 %collective-permute-start.15 = (f32[18,2,1,256]{3,2,1,0:T(1,128)S(1)}, f32[18,2,1,256]{3,2,1,0:T(1,128)S(1)}, u32[]{:S(2)}, u32[]{:S(2)}) collective-permute-start(f32[18,2,1,256]{3,2,1,0:T(1,128)S(1)} %pad_maximum_fusion.41), channel_id=1, source_target_pairs={{0,4},{4,0},{1,5},{5,1},{2,6},{6,2},{3,7},{7,3},{8,12},{12,8},{9,1... | collective-permute-start | bytes 110600 | tf_op jit(solution)/shard_map/ppermute | solution.py:22
  49.5 0.6 fusion.210
  50.2 0.3 collective-permute-start.17
  50.8 3.8 %collective-permute-done.13 = f32[18,2,8,32]{3,2,1,0:T(8,128)S(1)} collective-permute-done((f32[18,2,8,32]{3,2,1,0:T(8,128)S(1)}, f32[18,2,8,32]{3,2,1,0:T(8,128)S(1)}, u32[]{:S(2)}, u32[]{:S(2)}) %collective-permute-start.13) | collective-permute-done | bytes 36896 | tf_op jit(solution)/shard_map/ppermute | solution.py:22
  55.2 0.6 fusion.119
  55.7 0.6 fusion.129
  58.1 0.2 subtract_add_fusion.2
  58.8 0.3 collective-permute-start.18
  59.2 1.2 collective-permute-start.20
  60.4 6.1 %collective-permute-start.22 = (f32[18,1,8,256]{3,2,1,0:T(8,128)S(1)}, f32[18,1,8,256]{3,2,1,0:T(8,128)S(1)}, u32[]{:S(2)}, u32[]{:S(2)}) collective-permute-start(f32[18,1,8,256]{3,2,1,0:T(8,128)S(1)} %get-tuple-element.283), channel_id=1, source_target_pairs={{0,248},{8,0},{16,8},{24,16},{32,24},{40,32},{48,40},{56,48},{64,5... | collective-permute-start | bytes 442376 | tf_op jit(solution)/shard_map/ppermute | solution.py:22
  66.6 1.4 %collective-permute-start.21 = (f32[18,2,1,256]{3,2,1,0:T(1,128)S(1)}, f32[18,2,1,256]{3,2,1,0:T(1,128)S(1)}, u32[]{:S(2)}, u32[]{:S(2)}) collective-permute-start(f32[18,2,1,256]{3,2,1,0:T(1,128)S(1)} %pad_maximum_fusion.40), channel_id=1, source_target_pairs={{0,4},{4,0},{1,5},{5,1},{2,6},{6,2},{3,7},{7,3},{8,12},{12,8},{9,1... | collective-permute-start | bytes 110600 | tf_op jit(solution)/shard_map/ppermute | solution.py:22
  68.3 4.9 %collective-permute-done.19 = f32[18,2,8,32]{3,2,1,0:T(8,128)S(1)} collective-permute-done((f32[18,2,8,32]{3,2,1,0:T(8,128)S(1)}, f32[18,2,8,32]{3,2,1,0:T(8,128)S(1)}, u32[]{:S(2)}, u32[]{:S(2)}) %collective-permute-start.19) | collective-permute-done | bytes 36896 | tf_op jit(solution)/shard_map/ppermute | solution.py:22
  73.8 0.6 fusion.143
  74.4 0.6 fusion.153
  75.7 0.7 fusion.207
  76.4 0.8 fusion.158
  77.2 1.3 %pad_maximum_fusion.46 = f32[2]{0:T(128)S(1)} fusion(f32[1]{0:T(128)} %bitcast.556, f32[1]{0:T(128)} %bitcast.547), kind=kLoop, calls=%fused_computation.1046 | loop fusion | flops 2 | bytes 16 | tf_op jit(solution)/shard_map/stack | solution.py:232
  78.5 1.4 %pad_maximum_fusion.47 = f32[2]{0:T(128)S(1)} fusion(f32[1]{0:T(128)} %bitcast.567, f32[1]{0:T(128)} %bitcast.558), kind=kLoop, calls=%fused_computation.1047 | loop fusion | flops 2 | bytes 16 | tf_op jit(solution)/shard_map/stack | solution.py:232
  80.0 11.7 %all-reduce = (f32[2]{0:T(128)S(1)}, f32[2]{0:T(128)S(1)}) all-reduce(f32[2]{0:T(128)S(1)} %pad_maximum_fusion.47, f32[2]{0:T(128)S(1)} %pad_maximum_fusion.46), channel_id=1, replica_groups=mesh['ta_0'=8,'ta_1'=2,'ta_2'=2,'gz'=2,'gy'=4] {'ta_0'}, use_global_device_ids=true, to_apply=%region_9.10 | all-reduce | flops 4 | bytes 32 | tf_op jit(solution)/shard_map/psum | solution.py:26
  91.6 5.3 %all-reduce.4 = (f32[2]{0:T(128)S(1)}, f32[2]{0:T(128)S(1)}) all-reduce(f32[2]{0:T(128)S(1)} %get-tuple-element.8, f32[2]{0:T(128)S(1)} %get-tuple-element.9), channel_id=1, replica_groups=mesh['ta_0'=8,'ta_1'=2,'ta_2'=2,'gz'=2,'gy'=4] {'ta_1'}, use_global_device_ids=true, to_apply=%region_10.11 | all-reduce | flops 4 | bytes 32 | tf_op jit(solution)/shard_map/psum | solution.py:26
  96.9 9.7 %all-reduce.3 = (f32[2]{0:T(128)S(1)}, f32[2]{0:T(128)S(1)}) all-reduce(f32[2]{0:T(128)S(1)} %get-tuple-element.16, f32[2]{0:T(128)S(1)} %get-tuple-element.17), channel_id=1, replica_groups=mesh['ta_0'=8,'ta_1'=2,'ta_2'=2,'gz'=2,'gy'=4] {'ta_2'}, use_global_device_ids=true, to_apply=%region_11.12 | all-reduce | flops 4 | bytes 32 | tf_op jit(solution)/shard_map/psum | solution.py:26
  106.6 3.8 %all-reduce.2 = (f32[2]{0:T(128)S(1)}, f32[2]{0:T(128)S(1)}) all-reduce(f32[2]{0:T(128)S(1)} %get-tuple-element.14, f32[2]{0:T(128)S(1)} %get-tuple-element.15), channel_id=1, replica_groups=mesh['ta_0'=8,'ta_1'=2,'ta_2'=2,'gz'=2,'gy'=4] {'gz'}, use_global_device_ids=true, to_apply=%region_12.13 | all-reduce | flops 4 | bytes 32 | tf_op jit(solution)/shard_map/psum | solution.py:26
  110.4 9.4 %all-reduce.1 = (f32[2,1]{0,1:T(1,128)S(1)}, f32[2,1]{0,1:T(1,128)S(1)}) all-reduce(f32[2,1]{0,1:T(1,128)S(1)} %bitcast.1982, f32[2,1]{0,1:T(1,128)S(1)} %bitcast.1983), channel_id=1, replica_groups=mesh['ta_0'=8,'ta_1'=2,'ta_2'=2,'gz'=2,'gy'=4] {'gy'}, use_global_device_ids=true, to_apply=%region_13.14 | all-reduce | flops 4 | bytes 32 | tf_op jit(solution)/shard_map/psum | solution.py:26
  119.9 0.7 copy.384
  120.6 0.9 pad_maximum_fusion.1
  (306 shorter events, 13.2 us)
Async XLA Ops:
  0.6 2.4 %copy-start.1 = (f32[2,18,2,8,256]{4,3,2,1,0:T(8,128)S(1)}, f32[2,18,2,8,256]{4,3,2,1,0:T(8,128)}, u32[]{:S(2)}) copy-start(f32[2,18,2,8,256]{4,3,2,1,0:T(8,128)} %param.3) | copy-start | bytes 1769476
  3.4 11.0 %collective-permute-start.1 = (f32[18,2,8,32]{3,2,1,0:T(8,128)S(1)}, f32[18,2,8,32]{3,2,1,0:T(8,128)S(1)}, u32[]{:S(2)}, u32[]{:S(2)}) collective-permute-start(f32[18,2,8,32]{3,2,1,0:T(8,128)S(1)} %fusion.37), channel_id=1, source_target_pairs={{0,1},{1,2},{2,3},{3,0},{4,5},{5,6},{6,7},{7,4},{8,9},{9,10},{10,1... | collective-permute-start | bytes 110600 | tf_op jit(solution)/shard_map/ppermute | solution.py:22
  5.6 7.3 %copy-start = (f32[2,4,18,2,8,256]{5,4,3,2,1,0:T(8,128)S(1)}, f32[2,4,18,2,8,256]{5,4,3,2,1,0:T(8,128)}, u32[]{:S(2)}) copy-start(f32[2,4,18,2,8,256]{5,4,3,2,1,0:T(8,128)} %param.2) | copy-start | bytes 7077892
  5.9 8.9 %collective-permute-start.3 = (f32[18,2,1,256]{3,2,1,0:T(1,128)S(1)}, f32[18,2,1,256]{3,2,1,0:T(1,128)S(1)}, u32[]{:S(2)}, u32[]{:S(2)}) collective-permute-start(f32[18,2,1,256]{3,2,1,0:T(1,128)S(1)} %pad_maximum_fusion.43), channel_id=1, source_target_pairs={{0,4},{4,0},{1,5},{5,1},{2,6},{6,2},{3,7},{7,3},{8,12},{12,8},{9,1... | collective-permute-start | bytes 110600 | tf_op jit(solution)/shard_map/ppermute | solution.py:22
  7.2 10.8 %collective-permute-start.5 = (f32[18,1,8,256]{3,2,1,0:T(8,128)S(1)}, f32[18,1,8,256]{3,2,1,0:T(8,128)S(1)}, u32[]{:S(2)}, u32[]{:S(2)}) collective-permute-start(f32[18,1,8,256]{3,2,1,0:T(8,128)S(1)} %fusion.34), channel_id=1, source_target_pairs={{0,8},{8,16},{16,24},{24,32},{32,40},{40,48},{48,56},{56,64},{64,7... | collective-permute-start | bytes 442376 | tf_op jit(solution)/shard_map/ppermute | solution.py:22
  10.9 8.1 %collective-permute-start.4 = (f32[18,1,8,256]{3,2,1,0:T(8,128)S(1)}, f32[18,1,8,256]{3,2,1,0:T(8,128)S(1)}, u32[]{:S(2)}, u32[]{:S(2)}) collective-permute-start(f32[18,1,8,256]{3,2,1,0:T(8,128)S(1)} %get-tuple-element.325), channel_id=1, source_target_pairs={{0,248},{8,0},{16,8},{24,16},{32,24},{40,32},{48,40},{56,48},{64,5... | collective-permute-start | bytes 442376 | tf_op jit(solution)/shard_map/ppermute | solution.py:22
  11.0 4.1 %collective-permute-start = (f32[18,2,8,32]{3,2,1,0:T(8,128)S(1)}, f32[18,2,8,32]{3,2,1,0:T(8,128)S(1)}, u32[]{:S(2)}, u32[]{:S(2)}) collective-permute-start(f32[18,2,8,32]{3,2,1,0:T(8,128)S(1)} %slice.2830), channel_id=1, source_target_pairs={{0,3},{1,0},{2,1},{3,2},{4,7},{5,4},{6,5},{7,6},{8,11},{9,8},{10,9... | collective-permute-start | bytes 110600 | tf_op jit(solution)/shard_map/ppermute | solution.py:22
  14.5 3.3 %collective-permute-start.2 = (f32[18,2,1,256]{3,2,1,0:T(1,128)S(1)}, f32[18,2,1,256]{3,2,1,0:T(1,128)S(1)}, u32[]{:S(2)}, u32[]{:S(2)}) collective-permute-start(f32[18,2,1,256]{3,2,1,0:T(1,128)S(1)} %slice.2849), channel_id=1, source_target_pairs={{0,4},{4,0},{1,5},{5,1},{2,6},{6,2},{3,7},{7,3},{8,12},{12,8},{9,1... | collective-permute-start | bytes 110600 | tf_op jit(solution)/shard_map/ppermute | solution.py:22
  22.5 9.0 %collective-permute-start.6 = (f32[18,2,8,32]{3,2,1,0:T(8,128)S(1)}, f32[18,2,8,32]{3,2,1,0:T(8,128)S(1)}, u32[]{:S(2)}, u32[]{:S(2)}) collective-permute-start(f32[18,2,8,32]{3,2,1,0:T(8,128)S(1)} %fusion.42), channel_id=1, source_target_pairs={{0,3},{1,0},{2,1},{3,2},{4,7},{5,4},{6,5},{7,6},{8,11},{9,8},{10,9... | collective-permute-start | bytes 110600 | tf_op jit(solution)/shard_map/ppermute | solution.py:22
  23.8 12.1 %collective-permute-start.8 = (f32[18,2,1,256]{3,2,1,0:T(1,128)S(1)}, f32[18,2,1,256]{3,2,1,0:T(1,128)S(1)}, u32[]{:S(2)}, u32[]{:S(2)}) collective-permute-start(f32[18,2,1,256]{3,2,1,0:T(1,128)S(1)} %fusion.196), channel_id=1, source_target_pairs={{0,4},{4,0},{1,5},{5,1},{2,6},{6,2},{3,7},{7,3},{8,12},{12,8},{9,1... | collective-permute-start | bytes 110600 | tf_op jit(solution)/shard_map/ppermute | solution.py:22
  23.9 12.2 %collective-permute-start.10 = (f32[18,1,8,256]{3,2,1,0:T(8,128)S(1)}, f32[18,1,8,256]{3,2,1,0:T(8,128)S(1)}, u32[]{:S(2)}, u32[]{:S(2)}) collective-permute-start(f32[18,1,8,256]{3,2,1,0:T(8,128)S(1)} %get-tuple-element.311), channel_id=1, source_target_pairs={{0,248},{8,0},{16,8},{24,16},{32,24},{40,32},{48,40},{56,48},{64,5... | collective-permute-start | bytes 442376 | tf_op jit(solution)/shard_map/ppermute | solution.py:22
  29.3 6.4 %collective-permute-start.7 = (f32[18,2,8,32]{3,2,1,0:T(8,128)S(1)}, f32[18,2,8,32]{3,2,1,0:T(8,128)S(1)}, u32[]{:S(2)}, u32[]{:S(2)}) collective-permute-start(f32[18,2,8,32]{3,2,1,0:T(8,128)S(1)} %fusion.32), channel_id=1, source_target_pairs={{0,1},{1,2},{2,3},{3,0},{4,5},{5,6},{6,7},{7,4},{8,9},{9,10},{10,1... | collective-permute-start | bytes 110600 | tf_op jit(solution)/shard_map/ppermute | solution.py:22
  30.2 5.8 %collective-permute-start.9 = (f32[18,2,1,256]{3,2,1,0:T(1,128)S(1)}, f32[18,2,1,256]{3,2,1,0:T(1,128)S(1)}, u32[]{:S(2)}, u32[]{:S(2)}) collective-permute-start(f32[18,2,1,256]{3,2,1,0:T(1,128)S(1)} %pad_maximum_fusion.42), channel_id=1, source_target_pairs={{0,4},{4,0},{1,5},{5,1},{2,6},{6,2},{3,7},{7,3},{8,12},{12,8},{9,1... | collective-permute-start | bytes 110600 | tf_op jit(solution)/shard_map/ppermute | solution.py:22
  31.5 4.7 %collective-permute-start.11 = (f32[18,1,8,256]{3,2,1,0:T(8,128)S(1)}, f32[18,1,8,256]{3,2,1,0:T(8,128)S(1)}, u32[]{:S(2)}, u32[]{:S(2)}) collective-permute-start(f32[18,1,8,256]{3,2,1,0:T(8,128)S(1)} %fusion.29), channel_id=1, source_target_pairs={{0,8},{8,16},{16,24},{24,32},{32,40},{40,48},{48,56},{56,64},{64,7... | collective-permute-start | bytes 442376 | tf_op jit(solution)/shard_map/ppermute | solution.py:22
  40.0 10.1 %collective-permute-start.12 = (f32[18,2,8,32]{3,2,1,0:T(8,128)S(1)}, f32[18,2,8,32]{3,2,1,0:T(8,128)S(1)}, u32[]{:S(2)}, u32[]{:S(2)}) collective-permute-start(f32[18,2,8,32]{3,2,1,0:T(8,128)S(1)} %fusion.40), channel_id=1, source_target_pairs={{0,3},{1,0},{2,1},{3,2},{4,7},{5,4},{6,5},{7,6},{8,11},{9,8},{10,9... | collective-permute-start | bytes 110600 | tf_op jit(solution)/shard_map/ppermute | solution.py:22
  40.9 9.8 %collective-permute-start.14 = (f32[18,2,1,256]{3,2,1,0:T(1,128)S(1)}, f32[18,2,1,256]{3,2,1,0:T(1,128)S(1)}, u32[]{:S(2)}, u32[]{:S(2)}) collective-permute-start(f32[18,2,1,256]{3,2,1,0:T(1,128)S(1)} %fusion.195), channel_id=1, source_target_pairs={{0,4},{4,0},{1,5},{5,1},{2,6},{6,2},{3,7},{7,3},{8,12},{12,8},{9,1... | collective-permute-start | bytes 110600 | tf_op jit(solution)/shard_map/ppermute | solution.py:22
  42.2 12.7 %collective-permute-start.16 = (f32[18,1,8,256]{3,2,1,0:T(8,128)S(1)}, f32[18,1,8,256]{3,2,1,0:T(8,128)S(1)}, u32[]{:S(2)}, u32[]{:S(2)}) collective-permute-start(f32[18,1,8,256]{3,2,1,0:T(8,128)S(1)} %get-tuple-element.297), channel_id=1, source_target_pairs={{0,248},{8,0},{16,8},{24,16},{32,24},{40,32},{48,40},{56,48},{64,5... | collective-permute-start | bytes 442376 | tf_op jit(solution)/shard_map/ppermute | solution.py:22
  47.9 6.7 %collective-permute-start.13 = (f32[18,2,8,32]{3,2,1,0:T(8,128)S(1)}, f32[18,2,8,32]{3,2,1,0:T(8,128)S(1)}, u32[]{:S(2)}, u32[]{:S(2)}) collective-permute-start(f32[18,2,8,32]{3,2,1,0:T(8,128)S(1)} %fusion.27), channel_id=1, source_target_pairs={{0,1},{1,2},{2,3},{3,0},{4,5},{5,6},{6,7},{7,4},{8,9},{9,10},{10,1... | collective-permute-start | bytes 110600 | tf_op jit(solution)/shard_map/ppermute | solution.py:22
  48.1 6.8 %collective-permute-start.15 = (f32[18,2,1,256]{3,2,1,0:T(1,128)S(1)}, f32[18,2,1,256]{3,2,1,0:T(1,128)S(1)}, u32[]{:S(2)}, u32[]{:S(2)}) collective-permute-start(f32[18,2,1,256]{3,2,1,0:T(1,128)S(1)} %pad_maximum_fusion.41), channel_id=1, source_target_pairs={{0,4},{4,0},{1,5},{5,1},{2,6},{6,2},{3,7},{7,3},{8,12},{12,8},{9,1... | collective-permute-start | bytes 110600 | tf_op jit(solution)/shard_map/ppermute | solution.py:22
  50.2 4.9 %collective-permute-start.17 = (f32[18,1,8,256]{3,2,1,0:T(8,128)S(1)}, f32[18,1,8,256]{3,2,1,0:T(8,128)S(1)}, u32[]{:S(2)}, u32[]{:S(2)}) collective-permute-start(f32[18,1,8,256]{3,2,1,0:T(8,128)S(1)} %fusion.24), channel_id=1, source_target_pairs={{0,8},{8,16},{16,24},{24,32},{32,40},{40,48},{48,56},{56,64},{64,7... | collective-permute-start | bytes 442376 | tf_op jit(solution)/shard_map/ppermute | solution.py:22
  58.8 9.2 %collective-permute-start.18 = (f32[18,2,8,32]{3,2,1,0:T(8,128)S(1)}, f32[18,2,8,32]{3,2,1,0:T(8,128)S(1)}, u32[]{:S(2)}, u32[]{:S(2)}) collective-permute-start(f32[18,2,8,32]{3,2,1,0:T(8,128)S(1)} %fusion.43), channel_id=1, source_target_pairs={{0,3},{1,0},{2,1},{3,2},{4,7},{5,4},{6,5},{7,6},{8,11},{9,8},{10,9... | collective-permute-start | bytes 110600 | tf_op jit(solution)/shard_map/ppermute | solution.py:22
  59.2 14.2 %collective-permute-start.20 = (f32[18,2,1,256]{3,2,1,0:T(1,128)S(1)}, f32[18,2,1,256]{3,2,1,0:T(1,128)S(1)}, u32[]{:S(2)}, u32[]{:S(2)}) collective-permute-start(f32[18,2,1,256]{3,2,1,0:T(1,128)S(1)} %fusion.197), channel_id=1, source_target_pairs={{0,4},{4,0},{1,5},{5,1},{2,6},{6,2},{3,7},{7,3},{8,12},{12,8},{9,1... | collective-permute-start | bytes 110600 | tf_op jit(solution)/shard_map/ppermute | solution.py:22
  60.4 13.3 %collective-permute-start.22 = (f32[18,1,8,256]{3,2,1,0:T(8,128)S(1)}, f32[18,1,8,256]{3,2,1,0:T(8,128)S(1)}, u32[]{:S(2)}, u32[]{:S(2)}) collective-permute-start(f32[18,1,8,256]{3,2,1,0:T(8,128)S(1)} %get-tuple-element.283), channel_id=1, source_target_pairs={{0,248},{8,0},{16,8},{24,16},{32,24},{40,32},{48,40},{56,48},{64,5... | collective-permute-start | bytes 442376 | tf_op jit(solution)/shard_map/ppermute | solution.py:22
  66.5 6.7 %collective-permute-start.19 = (f32[18,2,8,32]{3,2,1,0:T(8,128)S(1)}, f32[18,2,8,32]{3,2,1,0:T(8,128)S(1)}, u32[]{:S(2)}, u32[]{:S(2)}) collective-permute-start(f32[18,2,8,32]{3,2,1,0:T(8,128)S(1)} %fusion.22), channel_id=1, source_target_pairs={{0,1},{1,2},{2,3},{3,0},{4,5},{5,6},{6,7},{7,4},{8,9},{9,10},{10,1... | collective-permute-start | bytes 110600 | tf_op jit(solution)/shard_map/ppermute | solution.py:22
  66.6 6.9 %collective-permute-start.21 = (f32[18,2,1,256]{3,2,1,0:T(1,128)S(1)}, f32[18,2,1,256]{3,2,1,0:T(1,128)S(1)}, u32[]{:S(2)}, u32[]{:S(2)}) collective-permute-start(f32[18,2,1,256]{3,2,1,0:T(1,128)S(1)} %pad_maximum_fusion.40), channel_id=1, source_target_pairs={{0,4},{4,0},{1,5},{5,1},{2,6},{6,2},{3,7},{7,3},{8,12},{12,8},{9,1... | collective-permute-start | bytes 110600 | tf_op jit(solution)/shard_map/ppermute | solution.py:22
  68.1 5.6 %collective-permute-start.23 = (f32[18,1,8,256]{3,2,1,0:T(8,128)S(1)}, f32[18,1,8,256]{3,2,1,0:T(8,128)S(1)}, u32[]{:S(2)}, u32[]{:S(2)}) collective-permute-start(f32[18,1,8,256]{3,2,1,0:T(8,128)S(1)} %fusion.19), channel_id=1, source_target_pairs={{0,8},{8,16},{16,24},{24,32},{32,40},{40,48},{48,56},{56,64},{64,7... | collective-permute-start | bytes 442376 | tf_op jit(solution)/shard_map/ppermute | solution.py:22
where the time goes:
time: 124 us; the launch traced here: 121 us
  blocking collectives  39.8 us (32%)
  starting transfers between devices  36.2 us (29%)
  other arithmetic  18.8 us (15%)
  waiting for transfers between devices  16.5 us (13%)
  local copies, waits for them, and re-layouts  7.44 us (6%)
  between operations  2.72 us (2%)
    psum x5, blocking collectives, over_axes(): return functools.reduce(lax.psum, axes, shard)  39.8 us
    ppermute x24, starting transfers between devices, shifted(): return lax.ppermute(value, axis, pairs)  36.2 us
    ppermute x24, waiting for transfers between devices, shifted(): return lax.ppermute(value, axis, pairs)  16.5 us
    mul x55, local copies, waits for them, and re-layouts, product(): term_re = col_re * row_re - col_im * row_im  3.18 us
    another operation x2, other arithmetic, shards(): summed_rows.append(global_totals(jnp.stack([func_sum, div_sum])))  2.74 us
  transfers between devices with their start and end apart: 24, of which 6 were waited for; matrix products, arithmetic and copies ran while one was open for 5% of the time, Pallas kernels for 0%

commit v1 on v0

v1 whole, which is shorter than its diff:
```python
import functools

import jax
import jax.numpy as jnp
from jax import lax
from jax.experimental import pallas as pl
from jax.experimental.pallas import tpu as pltpu
from jax.sharding import Mesh
from jax.sharding import PartitionSpec as P

NX = 64
ITERS = 2
OMEGA = 1.7
GUARD = 1e-12
TA = ("tz", "tx", "tc")
F32 = jnp.float32
R3 = range(3)


def re(i, j):
    return 3 * i + j


def im(i, j):
    return 9 + 3 * i + j


def half(h):
    return pl.ds(128 * h, 128)


def times_adjoint(acc, left, right):
    out = list(acc)
    for k in R3:
        lr = [left(re(i, k)) for i in R3]
        li = [left(im(i, k)) for i in R3]
        rr = [right(re(j, k)) for j in R3]
        ri = [right(im(j, k)) for j in R3]
        for i in R3:
            for j in R3:
                tr = lr[i] * rr[j] + li[i] * ri[j]
                ti = li[i] * rr[j] - lr[i] * ri[j]
                a, b = re(i, j), im(i, j)
                out[a] = tr if out[a] is None else out[a] + tr
                out[b] = ti if out[b] is None else out[b] + ti
    return out


def times(left, right):
    out = [None] * 18
    for k in R3:
        lr = [left(re(i, k)) for i in R3]
        li = [left(im(i, k)) for i in R3]
        rr = [right(re(k, j)) for j in R3]
        ri = [right(im(k, j)) for j in R3]
        for i in R3:
            for j in R3:
                tr = lr[i] * rr[j] - li[i] * ri[j]
                ti = lr[i] * ri[j] + li[i] * rr[j]
                a, b = re(i, j), im(i, j)
                out[a] = tr if out[a] is None else out[a] + tr
                out[b] = ti if out[b] is None else out[b] + ti
    return out


def plus_adjoint(acc, mat):
    out = list(acc)
    for i in R3:
        for j in R3:
            out[re(i, j)] = out[re(i, j)] + mat[re(j, i)]
            out[im(i, j)] = out[im(i, j)] - mat[im(j, i)]
    return out


def rotation(a, p, q):
    v0 = a[re(p, p)] + a[re(q, q)]
    v1 = -(a[im(p, q)] + a[im(q, p)])
    v2 = a[re(q, p)] - a[re(p, q)]
    v3 = -(a[im(p, p)] - a[im(q, q)])
    length = jnp.sqrt(v0 * v0 + v1 * v1 + v2 * v2 + v3 * v3)
    s0 = (1.0 - OMEGA) * length + OMEGA * v0
    s1, s2, s3 = OMEGA * v1, OMEGA * v2, OMEGA * v3
    inverse = lax.rsqrt(s0 * s0 + s1 * s1 + s2 * s2 + s3 * s3 + GUARD)
    return s0 * inverse, s1 * inverse, s2 * inverse, s3 * inverse


def rotate(m, quat, p, q):
    q0, q1, q2, q3 = quat
    out = list(m)
    for j in R3:
        ur, ui = m[re(p, j)], m[im(p, j)]
        lr, li = m[re(q, j)], m[im(q, j)]
        out[re(p, j)] = q0 * ur - q3 * ui + q2 * lr - q1 * li
        out[im(p, j)] = q0 * ui + q3 * ur + q2 * li + q1 * lr
        out[re(q, j)] = q0 * lr + q3 * li - q2 * ur - q1 * ui
        out[im(q, j)] = q0 * li - q3 * lr - q2 * ui + q1 * ur
    return out


def relax(g, w):
    a = times(lambda c: g[c], lambda c: w[c])
    for p, q in ((0, 1), (0, 2), (1, 2)):
        quat = rotation(a, p, q)
        a = rotate(a, quat, p, q)
        g = rotate(g, quat, p, q)
    return g, a


def measures(a):
    func = a[re(0, 0)] + a[re(1, 1)] + a[re(2, 2)]
    off = None
    for i, j in ((0, 1), (0, 2), (1, 2)):
        dr = a[re(i, j)] - a[re(j, i)]
        di = a[im(i, j)] + a[im(j, i)]
        term = dr * dr + di * di
        off = term if off is None else off + term
    mean = (a[im(0, 0)] + a[im(1, 1)] + a[im(2, 2)]) / 3.0
    div = 0.5 * off
    for i in R3:
        d = a[im(i, i)] - mean
        div = div + d * d
    return func, div


def unit(c):
    return 1.0 if c in (0, 4, 8) else 0.0


def crossing(links, h, is_unit):
    return lambda c: jnp.where(is_unit, F32(unit(c)), links[3, c, 1, :, half(h)])


def iotas():
    return (
        lax.broadcasted_iota(jnp.int32, (8, 128), 0),
        lax.broadcasted_iota(jnp.int32, (8, 128), 1),
    )


def pack_links(links, upz, upy):
    row, lane = iotas()
    for c in range(18):
        upz[c] = jnp.full((8, 128), unit(c), F32)
        for t in range(2):
            for h in range(2):
                r = 4 + 2 * t + h
                upz[c, r : r + 1, :] = links[2, c, t, 7:8, half(h)]
        high0 = pltpu.roll(links[1, c, 0, :, half(1)], 96, 1)
        high1 = links[1, c, 1, :, half(1)]
        upy[c] = jnp.where(lane < 64, F32(unit(c)), jnp.where(lane < 96, high0, high1))


def pack_sides(g, upz, upy, zp, yp, scr):
    row, lane = iotas()
    for c in range(18):
        for t in range(2):
            for h in range(2):
                r = 2 * t + h
                scr[c, r : r + 1, :] = g[c, t, 0:1, half(h)]
                scr[c, 4 + r : 5 + r, :] = g[c, t, 7:8, half(h)]
    out = times(lambda c: scr[c], lambda c: upz[c])
    for c in range(18):
        zp[c] = out[c]
    side = []
    for c in range(18):
        low1 = pltpu.roll(g[c, 1, :, half(0)], 32, 1)
        high0 = pltpu.roll(g[c, 0, :, half(1)], 96, 1)
        side.append(
            jnp.where(
                lane < 64,
                jnp.where(lane < 32, g[c, 0, :, half(0)], low1),
                jnp.where(lane < 96, high0, g[c, 1, :, half(1)]),
            )
        )
    out = times(lambda c: side[c], lambda c: upy[c])
    for c in range(18):
        yp[c] = out[c]


def first_kernel(links0, links1, g, tp, fp, zp, yp, upz0, upy0, upz1, upy1, scr):
    core = lax.axis_index("tc")
    pack_links(links1, upz1, upy1)
    for h in range(2):
        for out, s, is_unit in ((fp, core, core == 0), (tp, 1 - core, core == 1)):
            face = times(lambda c: g[c, s, :, half(h)], crossing(links1, h, is_unit))
            for c in range(18):
                out[c, :, half(h)] = face[c]
    pack_sides(g, upz1, upy1, zp, yp, scr)
    pack_links(links0, upz0, upy0)


def near_kernel(colour, last, own, other, gp, g, zh, ya, yb, th, *refs):
    if last:
        gn, wf, sums, w_scr, y_scr = refs
    else:
        gn, wf, tp, sums, w_scr, y_scr = refs
    core = lax.axis_index("tc")
    odd_row = lax.axis_index("gy") % 2
    row, lane = iotas()
    column = lane % 32
    parity = (row + lane // 32) % 2
    from_a = (lane // 64) == odd_row
    for c in range(18):
        y_scr[c] = jnp.where(from_a, ya[c], yb[c])
    for s in range(2):
        stays = parity == (s + colour) % 2
        behind = []
        for h in range(2):
            behind.append(
                times(lambda c: gp[c, s, :, half(h)], lambda c: other[1, c, s, :, half(h)])
            )
        low, high = [], []
        for c in range(18):
            r0 = pltpu.roll(behind[0][c], 32, 1)
            r1 = pltpu.roll(behind[1][c], 32, 1)
            halo = pltpu.roll(y_scr[c], 64 - 32 * s, 1)
            low.append(jnp.where(lane < 32, halo, r0))
            high.append(jnp.where(lane < 32, r0, r1))
        for h, mat in ((0, low), (1, high)):
            zero = [jnp.zeros((8, 128), F32)] * 18
            acc = plus_adjoint(zero, mat)
            for c in range(18):
                w_scr[c, s, :, half(h)] = acc[c]
        for h in range(2):
            acc = [w_scr[c, s, :, half(h)] for c in range(18)]

            def tile(c):
                return gp[c, s, :, half(h)]

            def ahead_x(c):
                v = tile(c)
                step = jnp.where(column == 31, pltpu.roll(v, 31, 1), pltpu.roll(v, 127, 1))
                return jnp.where(stays, v, step)

            acc = times_adjoint(acc, lambda c: own[0, c, s, :, half(h)], ahead_x)

            def ahead_y(c):
                a = pltpu.roll(gp[c, s, :, half(1)], 96, 1)
                if h == 0:
                    return jnp.where(lane >= 96, a, pltpu.roll(tile(c), 96, 1))
                return jnp.where(lane >= 96, pltpu.roll(y_scr[c], 96 - 32 * s, 1), a)

            acc = times_adjoint(acc, lambda c: own[1, c, s, :, half(h)], ahead_y)
            r = 2 * s + h

            def ahead_z(c):
                halo = jnp.broadcast_to(zh[c, r : r + 1, :], (8, 128))
                return jnp.where(row == 7, halo, pltpu.roll(tile(c), 7, 0))

            acc = times_adjoint(acc, lambda c: own[2, c, s, :, half(h)], ahead_z)
            back = times(tile, lambda c: other[0, c, s, :, half(h)])
            shifted = []
            for v in back:
                step = jnp.where(column == 0, pltpu.roll(v, 97, 1), pltpu.roll(v, 1, 1))
                shifted.append(jnp.where(stays, step, v))
            acc = plus_adjoint(acc, shifted)
            back = times(tile, lambda c: other[2, c, s, :, half(h)])
            shifted = []
            for c, v in enumerate(back):
                halo = jnp.broadcast_to(zh[c, 4 + r : 5 + r, :], (8, 128))
                shifted.append(jnp.where(row == 0, halo, pltpu.roll(v, 1, 0)))
            acc = plus_adjoint(acc, shifted)
            if s == 0:
                acc = times_adjoint(
                    acc,
                    lambda c: own[3, c, 0, :, half(h)],
                    lambda c: gp[c, 1, :, half(h)],
                )
            else:
                back = times(
                    lambda c: gp[c, 0, :, half(h)], lambda c: other[3, c, 0, :, half(h)]
                )
                acc = plus_adjoint(acc, back)
            for c in range(18):
                w_scr[c, s, :, half(h)] = acc[c]
    near = 1 - core
    total = [jnp.zeros((8, 128), F32)] * 2
    for h in range(2):
        for c in range(18):
            wf[c, :, half(h)] = w_scr[c, core, :, half(h)]
        link = crossing(own, h, core == 1)
        acc = [w_scr[c, near, :, half(h)] for c in range(18)]
        acc = times_adjoint(acc, link, lambda c: th[c, :, half(h)])
        new, mat = relax([g[c, near, :, half(h)] for c in range(18)], acc)
        for c in range(18):
            gn[c, :, half(h)] = new[c]
        if not last:
            face = times(lambda c: new[c], link)
            for c in range(18):
                tp[c, :, half(h)] = face[c]
        if colour == 1:
            total = [a + b for a, b in zip(total, measures(mat))]
    sums[0] = total[0]
    sums[1] = total[1]


def far_kernel(colour, last, own, g, gn, wf, fh, near_sums, *refs):
    if last:
        g0, out, sums = refs
    else:
        upz, upy, out, fp, zp, yp, sums, scr = refs
    core = lax.axis_index("tc")
    total = [near_sums[0], near_sums[1]]
    for h in range(2):
        link = crossing(own, h, core == 0)
        acc = [wf[c, :, half(h)] for c in range(18)]
        acc = times_adjoint(acc, link, lambda c: fh[c, :, half(h)])
        new, mat = relax([g[c, core, :, half(h)] for c in range(18)], acc)
        if last:
            for c in range(18):
                out[1, c, core, :, half(h)] = new[c]
        else:
            for c in range(18):
                out[c, core, :, half(h)] = new[c]
            face = times(lambda c: new[c], link)
            for c in range(18):
                fp[c, :, half(h)] = face[c]
        if colour == 1:
            total = [a + b for a, b in zip(total, measures(mat))]
    if last:
        for c in range(18):
            out[1, c, 1 - core] = gn[c]
            for s in range(2):
                out[0, c, s] = g0[c, s]
    else:
        for c in range(18):
            out[c, 1 - core] = gn[c]
        pack_sides(out, upz, upy, zp, yp, scr)
    if colour == 1:
        for k in range(2):
            rows = jnp.sum(total[k], axis=0, keepdims=True)
            sums[k] = jnp.broadcast_to(jnp.sum(rows, axis=1, keepdims=True), (8, 128))
    else:
        sums[0] = total[0]
        sums[1] = total[1]


def final_kernel(volume, parts, monitor):
    total = parts[0]
    for k in range(1, parts.shape[0]):
        total = total + parts[k]
    row, lane = iotas()
    func = jnp.where(lane[:4] == 0, total[0:1], total[2:3])
    div = jnp.where(lane[:4] == 0, total[1:2], total[3:4])
    both = jnp.where(row[:4] == 0, 1.0 - func / (12.0 * volume), div / (volume / 2.0))
    monitor[...] = both[:2, :2]


def call(body, outs, scratch, args, flops, name):
    return pl.pallas_call(
        body,
        out_shape=[jax.ShapeDtypeStruct(o, F32) for o in outs],
        in_specs=[pl.BlockSpec(memory_space=pltpu.VMEM)] * len(args),
        out_specs=[pl.BlockSpec(memory_space=pltpu.VMEM)] * len(outs),
        scratch_shapes=[pltpu.VMEM(s, F32) for s in scratch],
        compiler_params=pltpu.CompilerParams(vmem_limit_bytes=24 * 2**20),
        cost_estimate=pl.CostEstimate(flops=flops, bytes_accessed=0, transcendentals=0),
        name=name,
    )(*args)


def swap(value, axis, partner):
    count = lax.axis_size(axis)
    return lax.ppermute(value, axis, [(i, partner(i) % count) for i in range(count)])


def even_odd(i):
    return i ^ 1


def odd_even(i):
    return i + 1 if i % 2 else i - 1


def gathered(values, axes):
    count = 1
    for axis in axes:
        count *= lax.axis_size(axis)
    parts = jnp.broadcast_to(values, (count,) + values.shape)
    return lax.all_to_all(parts, axes, 0, 0, tiled=True)


FACE = (18, 8, 256)
SIDE = (18, 8, 128)
FIELD = (18, 2, 8, 256)


def shards(lattice_links, transform):
    links = [lattice_links[0], lattice_links[1]]
    g = [transform[0], transform[1]]
    packed = [None, None]
    tp, fp, zp, yp, *sides = call(
        first_kernel,
        [FACE, FACE, SIDE, SIDE] + [SIDE] * 4,
        [SIDE],
        [links[0], links[1], g[1]],
        10**7,
        "first",
    )
    packed[0] = sides[:2]
    packed[1] = sides[2:]
    volume = 2 * transform.shape[2] * transform.shape[3] * transform.shape[4]
    for axis in TA + ("gz", "gy"):
        volume *= lax.axis_size(axis)
    kept = []
    for sweep in range(ITERS):
        for colour in (0, 1):
            last = sweep == ITERS - 1 and colour == 1
            other = 1 - colour
            fh = swap(fp, TA, odd_even)
            zh = swap(zp, "gz", even_odd)
            ya = swap(yp, "gy", even_odd)
            yb = swap(yp, "gy", odd_even)
            th = swap(tp, "tc", even_odd)
            outs = [FACE, FACE] + ([] if last else [FACE]) + [(2, 8, 128)]
            gn, wf, *rest = call(
                functools.partial(near_kernel, colour, last),
                outs,
                [FIELD, SIDE],
                [links[colour], links[other], g[other], g[colour], zh, ya, yb, th],
                3 * 10**7,
                f"near_{sweep}_{colour}",
            )
            sums = rest[-1]
            args = [links[colour], g[colour], gn, wf, fh, sums]
            if last:
                out, sums = call(
                    functools.partial(far_kernel, colour, last),
                    [(2,) + FIELD, (2, 8, 128)],
                    [],
                    args + [g[0]],
                    10**7,
                    f"far_{sweep}_{colour}",
                )
            else:
                tp = rest[0]
                g[colour], fp, zp, yp, sums = call(
                    functools.partial(far_kernel, colour, last),
                    [FIELD, FACE, SIDE, SIDE, (2, 8, 128)],
                    [SIDE],
                    args + list(packed[colour]),
                    10**7,
                    f"far_{sweep}_{colour}",
                )
        kept.append(sums[:, 0, :])
    parts = gathered(jnp.concatenate(kept, 0), ("tx", "gz", "gy"))
    parts = gathered(jnp.sum(parts, 0), ("tz", "tc"))
    (monitor,) = call(
        functools.partial(final_kernel, volume), [(2, 2)], [], [parts], 10**3, "final"
    )
    return (out, monitor)


def solution(mesh):
    finer = Mesh(
        mesh.devices.reshape(8, 2, 2, mesh.shape["gz"], mesh.shape["gy"]),
        ("tz", "tx", "tc", "gz", "gy"),
    )
    return jax.shard_map(
        shards,
        mesh=finer,
        in_specs=(P(None, None, None, TA, "gz", "gy"), P(None, None, TA, "gz", "gy")),
        out_specs=(P(None, None, TA, "gz", "gy"), P()),
        check_vma=False,
    )
```

time: 124 us -> 84.4 us (0.68); the launches traced: 121 us -> 84.2 us
  other arithmetic: 18.8 us -> 0.04 us
  blocking collectives: 39.8 us -> 25 us
  Pallas kernels: 0 us -> 10.9 us
  starting transfers between devices: 36.2 us -> 29.6 us
  local copies, waits for them, and re-layouts: 7.44 us -> 2.95 us
  between operations: 2.72 us -> 0.71 us
  waiting for transfers between devices: 16.5 us -> 15 us
    psum x5 -> x0, blocking collectives: 39.8 us -> none  [over_axes(): return functools.reduce(lax.psum, axes, shard)]
    all_to_all x0 -> x2, blocking collectives: none -> 25 us  [gathered(): return lax.all_to_all(parts, axes, 0, 0, tiled=True)]
    pallas_call x0 -> x10, Pallas kernels: none -> 10.9 us  [call(): pl.pallas_call(body, out_shape=[jax.ShapeDtypeStruct(o, F32) for o in out...]
    add x32 -> x0, other arithmetic: 7.12 us -> none  [the longest x12 2.25 us: product(): total_re = total_re + term_re]
    ppermute x24 -> x20, starting transfers between devices: 36.2 us -> 29.6 us  [swap(): lax.ppermute(value, axis, [(i, partner(i) % count) for i in range(count)])]
    another operation x19 -> x0, other arithmetic: 3.87 us -> none  [the longest x2 2.74 us: shards(): summed_rows.append(global_totals(jnp.stack([func_sum, div_sum])))]
    slice x55 -> x1, local copies, waits for them, and re-layouts: 3.43 us -> 0.01 us  [shards(): kept.append(sums[:, 0, :])]
    mul x55 -> x0, local copies, waits for them, and re-layouts: 3.18 us -> none  [product(): term_re = col_re * row_re - col_im * row_im]
  transfers between devices with their start and end apart: 24 -> 20, of which waited for: 6 -> 8; matrix products, arithmetic and copies ran while one was open for 5% -> 0% of each run, Pallas kernels for 0% -> 9%
where the time goes in v1:
time: 84.4 us; the launch traced here: 84.2 us
  starting transfers between devices  29.6 us (35%)
  blocking collectives  25 us (30%)
  waiting for transfers between devices  15 us (18%)
  Pallas kernels  10.9 us (13%)
  local copies, waits for them, and re-layouts  2.95 us (3%)
    ppermute x20, starting transfers between devices, swap(): lax.ppermute(value, axis, [(i, partner(i) % count) for i in range(count)])  29.6 us
    all_to_all x2, blocking collectives, gathered(): return lax.all_to_all(parts, axes, 0, 0, tiled=True)  25 us
    ppermute x20, waiting for transfers between devices, swap(): lax.ppermute(value, axis, [(i, partner(i) % count) for i in range(count)])  15 us
    pallas_call x10, Pallas kernels, call(): pl.pallas_call(body, out_shape=[jax.ShapeDtypeStruct(o, F32) for o in out...  10.9 us
    squeeze x1, local copies, waits for them, and re-layouts, shards(): links = [lattice_links[0], lattice_links[1]]  1.83 us
  transfers between devices with their start and end apart: 20, of which 8 were waited for; matrix products, arithmetic and copies ran while one was open for 0% of the time, Pallas kernels for 9%

profile of v1, /device:TPU:1, one launch (start us, length us, event | category | flops | bytes accessed | tf_op | source)
XLA Modules:
  0.0 84.2 jit_solution(3906584699654951156)
XLA Ops:
  0.6 1.1 %slice_bitcast_fusion.2 = (f32[18,2,8,256]{3,2,1,0:T(8,128)S(1)}, f32[18,2,8,256]{3,2,1,0:T(8,128)S(1)}) fusion(f32[2,18,2,8,256]{4,3,2,1,0:T(8,128)} %param.3), kind=kLoop, calls=%fused_computation.2 | loop fusion | bytes 1179648 | tf_op jit(solution)/shard_map/squeeze | solution.py:390
  1.7 1.8 %slice_bitcast_fusion = (f32[4,18,2,8,256]{4,3,2,1,0:T(8,128)S(1)}, f32[4,18,2,8,256]{4,3,2,1,0:T(8,128)S(1)}) fusion(f32[2,4,18,2,8,256]{5,4,3,2,1,0:T(8,128)} %param.2), kind=kLoop, calls=%fused_computation | loop fusion | bytes 4718592 | tf_op jit(solution)/shard_map/squeeze | solution.py:389
  3.6 0.3 first.1
  3.9 3.3 %collective-permute-start.3 = (f32[18,8,256]{2,1,0:T(8,128)S(1)}, f32[18,8,256]{2,1,0:T(8,128)S(1)}, u32[]{:S(2)}, u32[]{:S(2)}) collective-permute-start(f32[18,8,256]{2,1,0:T(8,128)S(1)} %get-tuple-element.42), channel_id=1, source_target_pairs={{0,8},{8,0},{1,9},{9,1},{2,10},{10,2},{3,11},{11,3},{4,12},{12,4},... | collective-permute-start | bytes 442376 | tf_op jit(solution)/shard_map/ppermute | solution.py:364
  7.2 1.0 %collective-permute-start.4 = (f32[18,8,256]{2,1,0:T(8,128)S(1)}, f32[18,8,256]{2,1,0:T(8,128)S(1)}, u32[]{:S(2)}, u32[]{:S(2)}) collective-permute-start(f32[18,8,256]{2,1,0:T(8,128)S(1)} %get-tuple-element.45), channel_id=1, source_target_pairs={{0,248},{8,16},{16,8},{24,32},{32,24},{40,48},{48,40},{56,64},{64,... | collective-permute-start | bytes 442376 | tf_op jit(solution)/shard_map/ppermute | solution.py:364
  8.2 0.3 collective-permute-start
  8.5 2.7 %collective-permute-start.2 = (f32[18,8,128]{2,1,0:T(8,128)S(1)}, f32[18,8,128]{2,1,0:T(8,128)S(1)}, u32[]{:S(2)}, u32[]{:S(2)}) collective-permute-start(f32[18,8,128]{2,1,0:T(8,128)S(1)} %get-tuple-element.41), channel_id=1, source_target_pairs={{0,3},{1,2},{2,1},{3,0},{4,7},{5,6},{6,5},{7,4},{8,11},{9,10},{10,... | collective-permute-start | bytes 221192 | tf_op jit(solution)/shard_map/ppermute | solution.py:364
  11.2 2.2 %collective-permute-done.zh = f32[18,8,128]{2,1,0:T(8,128)S(1)} collective-permute-done((f32[18,8,128]{2,1,0:T(8,128)S(1)}, f32[18,8,128]{2,1,0:T(8,128)S(1)}, u32[]{:S(2)}, u32[]{:S(2)}) %collective-permute-start) | collective-permute-done | bytes 73760 | tf_op jit(solution)/shard_map/ppermute | solution.py:364
  13.4 0.0 collective-permute-done.2.yb
  13.4 1.3 %collective-permute-done.1.ya = f32[18,8,128]{2,1,0:T(8,128)S(1)} collective-permute-done((f32[18,8,128]{2,1,0:T(8,128)S(1)}, f32[18,8,128]{2,1,0:T(8,128)S(1)}, u32[]{:S(2)}, u32[]{:S(2)}) %collective-permute-start.1) | collective-permute-done | bytes 73760 | tf_op jit(solution)/shard_map/ppermute | solution.py:364
  14.7 0.0 collective-permute-done.3.th
  14.7 1.5 %near_0_0.1 = (f32[18,8,256]{2,1,0:T(8,128)S(1)}, f32[18,8,256]{2,1,0:T(8,128)S(1)}, f32[18,8,256]{2,1,0:T(8,128)S(1)}, f32[2,8,128]{2,1,0:T(8,128)S(1)}) custom-call(f32[4,18,2,8,256]{4,3,2,1,0:T(8,128)S(1)} %get-tuple-element.78.links0.own.other, f32[4,18,2,8,256]{4,3,2,1,0:T(8,128)S(1)} %get-tuple-element.79.links1.other.own, ...), custom_call_target="tpu_custom_call" | custom-call | flops 30000000 | tf_op jit(solution)/shard_map/near_0_0/pallas_call | solution.py:350
  16.3 7.2 %collective-permute-start.8 = (f32[18,8,256]{2,1,0:T(8,128)S(1)}, f32[18,8,256]{2,1,0:T(8,128)S(1)}, u32[]{:S(2)}, u32[]{:S(2)}) collective-permute-start(f32[18,8,256]{2,1,0:T(8,128)S(1)} %get-tuple-element.52), channel_id=1, source_target_pairs={{0,8},{8,0},{1,9},{9,1},{2,10},{10,2},{3,11},{11,3},{4,12},{12,4},... | collective-permute-start | bytes 442376 | tf_op jit(solution)/shard_map/ppermute | solution.py:364
  23.5 1.0 %far_0_0.1 = (f32[18,2,8,256]{3,2,1,0:T(8,128)S(1)}, f32[18,8,256]{2,1,0:T(8,128)S(1)}, f32[18,8,128]{2,1,0:T(8,128)S(1)}, f32[18,8,128]{2,1,0:T(8,128)S(1)}, f32[2,8,128]{2,1,0:T(8,128)}) custom-call(f32[4,18,2,8,256]{4,3,2,1,0:T(8,128)S(1)} %get-tuple-element.78.links0.own.other, f32[18,2,8,256]{3,2,1,0:T(8,128)S(1)} %get-tuple-element.80.g, ...), custom_call_target="tpu_custom_call" | custom-call | flops 10000000 | tf_op jit(solution)/shard_map/far_0_0/pallas_call | solution.py:350
  24.5 0.0 collective-permute-start.9
  24.5 1.2 %collective-permute-start.5 = (f32[18,8,128]{2,1,0:T(8,128)S(1)}, f32[18,8,128]{2,1,0:T(8,128)S(1)}, u32[]{:S(2)}, u32[]{:S(2)}) collective-permute-start(f32[18,8,128]{2,1,0:T(8,128)S(1)} %get-tuple-element.50), channel_id=1, source_target_pairs={{0,4},{4,0},{1,5},{5,1},{2,6},{6,2},{3,7},{7,3},{8,12},{12,8},{9,1... | collective-permute-start | bytes 221192 | tf_op jit(solution)/shard_map/ppermute | solution.py:364
  25.7 0.9 %collective-permute-start.7 = (f32[18,8,128]{2,1,0:T(8,128)S(1)}, f32[18,8,128]{2,1,0:T(8,128)S(1)}, u32[]{:S(2)}, u32[]{:S(2)}) collective-permute-start(f32[18,8,128]{2,1,0:T(8,128)S(1)} %get-tuple-element.51), channel_id=1, source_target_pairs={{0,3},{1,2},{2,1},{3,0},{4,7},{5,6},{6,5},{7,4},{8,11},{9,10},{10,... | collective-permute-start | bytes 221192 | tf_op jit(solution)/shard_map/ppermute | solution.py:364
  26.6 2.4 %collective-permute-done.5.zh = f32[18,8,128]{2,1,0:T(8,128)S(1)} collective-permute-done((f32[18,8,128]{2,1,0:T(8,128)S(1)}, f32[18,8,128]{2,1,0:T(8,128)S(1)}, u32[]{:S(2)}, u32[]{:S(2)}) %collective-permute-start.5) | collective-permute-done | bytes 73760 | tf_op jit(solution)/shard_map/ppermute | solution.py:364
  29.0 1.1 %collective-permute-done.7.yb = f32[18,8,128]{2,1,0:T(8,128)S(1)} collective-permute-done((f32[18,8,128]{2,1,0:T(8,128)S(1)}, f32[18,8,128]{2,1,0:T(8,128)S(1)}, u32[]{:S(2)}, u32[]{:S(2)}) %collective-permute-start.7) | collective-permute-done | bytes 73760 | tf_op jit(solution)/shard_map/ppermute | solution.py:364
  30.1 0.0 collective-permute-done.6.ya
  30.1 0.0 collective-permute-done.8.th
  30.1 1.6 %near_0_1.1 = (f32[18,8,256]{2,1,0:T(8,128)S(1)}, f32[18,8,256]{2,1,0:T(8,128)S(1)}, f32[18,8,256]{2,1,0:T(8,128)S(1)}, f32[2,8,128]{2,1,0:T(8,128)S(1)}) custom-call(f32[4,18,2,8,256]{4,3,2,1,0:T(8,128)S(1)} %get-tuple-element.79.links1.other.own, f32[4,18,2,8,256]{4,3,2,1,0:T(8,128)S(1)} %get-tuple-element.78.links0.own.other, ...), custom_call_target="tpu_custom_call" | custom-call | flops 30000000 | tf_op jit(solution)/shard_map/near_0_1/pallas_call | solution.py:350
  31.7 2.2 %collective-permute-start.13 = (f32[18,8,256]{2,1,0:T(8,128)S(1)}, f32[18,8,256]{2,1,0:T(8,128)S(1)}, u32[]{:S(2)}, u32[]{:S(2)}) collective-permute-start(f32[18,8,256]{2,1,0:T(8,128)S(1)} %get-tuple-element.62), channel_id=1, source_target_pairs={{0,8},{8,0},{1,9},{9,1},{2,10},{10,2},{3,11},{11,3},{4,12},{12,4},... | collective-permute-start | bytes 442376 | tf_op jit(solution)/shard_map/ppermute | solution.py:364
  34.0 0.6 far_0_1.1
  34.5 3.2 %collective-permute-start.14 = (f32[18,8,256]{2,1,0:T(8,128)S(1)}, f32[18,8,256]{2,1,0:T(8,128)S(1)}, u32[]{:S(2)}, u32[]{:S(2)}) collective-permute-start(f32[18,8,256]{2,1,0:T(8,128)S(1)} %get-tuple-element.65), channel_id=1, source_target_pairs={{0,248},{8,16},{16,8},{24,32},{32,24},{40,48},{48,40},{56,64},{64,... | collective-permute-start | bytes 442376 | tf_op jit(solution)/shard_map/ppermute | solution.py:364
  37.7 0.0 collective-permute-start.10
  37.7 1.7 %collective-permute-start.12 = (f32[18,8,128]{2,1,0:T(8,128)S(1)}, f32[18,8,128]{2,1,0:T(8,128)S(1)}, u32[]{:S(2)}, u32[]{:S(2)}) collective-permute-start(f32[18,8,128]{2,1,0:T(8,128)S(1)} %get-tuple-element.61), channel_id=1, source_target_pairs={{0,3},{1,2},{2,1},{3,0},{4,7},{5,6},{6,5},{7,4},{8,11},{9,10},{10,... | collective-permute-start | bytes 221192 | tf_op jit(solution)/shard_map/ppermute | solution.py:364
  39.5 0.0 collective-permute-start.11
  39.5 3.4 %collective-permute-done.10.zh = f32[18,8,128]{2,1,0:T(8,128)S(1)} collective-permute-done((f32[18,8,128]{2,1,0:T(8,128)S(1)}, f32[18,8,128]{2,1,0:T(8,128)S(1)}, u32[]{:S(2)}, u32[]{:S(2)}) %collective-permute-start.10) | collective-permute-done | bytes 73760 | tf_op jit(solution)/shard_map/ppermute | solution.py:364
  42.9 0.0 collective-permute-done.12.yb
  42.9 0.1 collective-permute-done.11.ya
  43.0 0.0 collective-permute-done.13.th
  43.0 1.5 %near_1_0.1 = (f32[18,8,256]{2,1,0:T(8,128)S(1)}, f32[18,8,256]{2,1,0:T(8,128)S(1)}, f32[18,8,256]{2,1,0:T(8,128)S(1)}, f32[2,8,128]{2,1,0:T(8,128)S(1)}) custom-call(f32[4,18,2,8,256]{4,3,2,1,0:T(8,128)S(1)} %get-tuple-element.78.links0.own.other, f32[4,18,2,8,256]{4,3,2,1,0:T(8,128)S(1)} %get-tuple-element.79.links1.other.own, ...), custom_call_target="tpu_custom_call" | custom-call | flops 30000000 | tf_op jit(solution)/shard_map/near_1_0/pallas_call | solution.py:350
  44.5 0.0 collective-permute-done.14.fh
  44.5 1.1 %far_1_0.1 = (f32[18,2,8,256]{3,2,1,0:T(8,128)S(1)}, f32[18,8,256]{2,1,0:T(8,128)S(1)}, f32[18,8,128]{2,1,0:T(8,128)S(1)}, f32[18,8,128]{2,1,0:T(8,128)S(1)}, f32[2,8,128]{2,1,0:T(8,128)}) custom-call(f32[4,18,2,8,256]{4,3,2,1,0:T(8,128)S(1)} %get-tuple-element.78.links0.own.other, f32[18,2,8,256]{3,2,1,0:T(8,128)S(1)} %get-tuple-element.49.gp.g, ...), custom_call_target="tpu_custom_call" | custom-call | flops 10000000 | tf_op jit(solution)/shard_map/far_1_0/pallas_call | solution.py:350
  45.6 1.7 %collective-permute-start.17 = (f32[18,8,128]{2,1,0:T(8,128)S(1)}, f32[18,8,128]{2,1,0:T(8,128)S(1)}, u32[]{:S(2)}, u32[]{:S(2)}) collective-permute-start(f32[18,8,128]{2,1,0:T(8,128)S(1)} %get-tuple-element.69), channel_id=1, source_target_pairs={{0,3},{1,2},{2,1},{3,0},{4,7},{5,6},{6,5},{7,4},{8,11},{9,10},{10,... | collective-permute-start | bytes 221192 | tf_op jit(solution)/shard_map/ppermute | solution.py:364
  47.2 2.3 %collective-permute-start.18 = (f32[18,8,256]{2,1,0:T(8,128)S(1)}, f32[18,8,256]{2,1,0:T(8,128)S(1)}, u32[]{:S(2)}, u32[]{:S(2)}) collective-permute-start(f32[18,8,256]{2,1,0:T(8,128)S(1)} %get-tuple-element.70), channel_id=1, source_target_pairs={{0,8},{8,0},{1,9},{9,1},{2,10},{10,2},{3,11},{11,3},{4,12},{12,4},... | collective-permute-start | bytes 442376 | tf_op jit(solution)/shard_map/ppermute | solution.py:364
  49.6 1.7 %collective-permute-start.15 = (f32[18,8,128]{2,1,0:T(8,128)S(1)}, f32[18,8,128]{2,1,0:T(8,128)S(1)}, u32[]{:S(2)}, u32[]{:S(2)}) collective-permute-start(f32[18,8,128]{2,1,0:T(8,128)S(1)} %get-tuple-element.68), channel_id=1, source_target_pairs={{0,4},{4,0},{1,5},{5,1},{2,6},{6,2},{3,7},{7,3},{8,12},{12,8},{9,1... | collective-permute-start | bytes 221192 | tf_op jit(solution)/shard_map/ppermute | solution.py:364
  51.3 2.6 %collective-permute-done.15.zh = f32[18,8,128]{2,1,0:T(8,128)S(1)} collective-permute-done((f32[18,8,128]{2,1,0:T(8,128)S(1)}, f32[18,8,128]{2,1,0:T(8,128)S(1)}, u32[]{:S(2)}, u32[]{:S(2)}) %collective-permute-start.15) | collective-permute-done | bytes 73760 | tf_op jit(solution)/shard_map/ppermute | solution.py:364
  54.0 0.0 collective-permute-done.17.yb
  54.0 0.0 collective-permute-done.16.ya
  54.0 0.0 collective-permute-done.18.th
  54.0 1.6 %near_1_1.1 = (f32[18,8,256]{2,1,0:T(8,128)S(1)}, f32[18,8,256]{2,1,0:T(8,128)S(1)}, f32[2,8,128]{2,1,0:T(8,128)S(1)}) custom-call(f32[4,18,2,8,256]{4,3,2,1,0:T(8,128)S(1)} %get-tuple-element.79.links1.other.own, f32[4,18,2,8,256]{4,3,2,1,0:T(8,128)S(1)} %get-tuple-element.78.links0.own.other, f32[18,2,8,256]{3,2,1,0:T(8,128)S(1)} %get-tuple-element.67.gp.refs_0_, ...), custom_call_target="tpu_custom_call" | custom-call | flops 30000000 | tf_op jit(solution)/shard_map/near_1_1/pallas_call | solution.py:350
  55.5 1.8 %collective-permute-done.19.fh = f32[18,8,256]{2,1,0:T(8,128)S(1)} collective-permute-done((f32[18,8,256]{2,1,0:T(8,128)S(1)}, f32[18,8,256]{2,1,0:T(8,128)S(1)}, u32[]{:S(2)}, u32[]{:S(2)}) %collective-permute-start.19) | collective-permute-done | bytes 147488 | tf_op jit(solution)/shard_map/ppermute | solution.py:364
  57.4 1.1 %far_1_1.1 = (f32[2,18,2,8,256]{4,3,2,1,0:T(8,128)}, f32[2,8,128]{2,1,0:T(8,128)S(1)}) custom-call(f32[4,18,2,8,256]{4,3,2,1,0:T(8,128)S(1)} %get-tuple-element.79.links1.other.own, f32[18,2,8,256]{3,2,1,0:T(8,128)S(1)} %get-tuple-element.59.gp.g, f32[18,8,256]{2,1,0:T(8,128)S(1)} %get-tuple-element.71.gn, f32[18,8,256]{2,1,0:T(8,128)S(1)} %get-tuple-element.72.wf, ...), custom_call_target="tpu_custom_call" | custom-call | flops 10000000 | tf_op jit(solution)/shard_map/far_1_1/pallas_call | solution.py:350
  58.6 12.2 %all_to_all.10 = f32[16,4,128]{2,1,0:T(4,128)S(1)} all-to-all(f32[16,4,128]{2,1,0:T(4,128)S(1)} %broadcast_in_dim.6), channel_id=1, replica_groups=mesh['tz'=8,'tx'=2,'tc'=2,'gz'=2,'gy'=4] {'tx','gz','gy'}, dimensions={0} | all-to-all | bytes 65536 | tf_op jit(solution)/shard_map/all_to_all | solution.py:380
  70.8 12.8 %all_to_all.11.parts = f32[16,4,128]{2,1,0:T(4,128)S(1)} all-to-all(f32[16,4,128]{2,1,0:T(4,128)S(1)} %broadcast_in_dim.7), channel_id=1, replica_groups=mesh['tz'=8,'tx'=2,'tc'=2,'gz'=2,'gy'=4] {'tz','tc'}, dimensions={0} | all-to-all | bytes 65536 | tf_op jit(solution)/shard_map/all_to_all | solution.py:380
  83.7 0.6 final.1
  (13 shorter events, 0.1 us)
Async XLA Ops:
  3.9 10.9 %collective-permute-start.3 = (f32[18,8,256]{2,1,0:T(8,128)S(1)}, f32[18,8,256]{2,1,0:T(8,128)S(1)}, u32[]{:S(2)}, u32[]{:S(2)}) collective-permute-start(f32[18,8,256]{2,1,0:T(8,128)S(1)} %get-tuple-element.42), channel_id=1, source_target_pairs={{0,8},{8,0},{1,9},{9,1},{2,10},{10,2},{3,11},{11,3},{4,12},{12,4},... | collective-permute-start | bytes 442376 | tf_op jit(solution)/shard_map/ppermute | solution.py:364
  7.2 16.3 %collective-permute-start.4 = (f32[18,8,256]{2,1,0:T(8,128)S(1)}, f32[18,8,256]{2,1,0:T(8,128)S(1)}, u32[]{:S(2)}, u32[]{:S(2)}) collective-permute-start(f32[18,8,256]{2,1,0:T(8,128)S(1)} %get-tuple-element.45), channel_id=1, source_target_pairs={{0,248},{8,16},{16,8},{24,32},{32,24},{40,48},{48,40},{56,64},{64,... | collective-permute-start | bytes 442376 | tf_op jit(solution)/shard_map/ppermute | solution.py:364
  8.2 5.2 %collective-permute-start = (f32[18,8,128]{2,1,0:T(8,128)S(1)}, f32[18,8,128]{2,1,0:T(8,128)S(1)}, u32[]{:S(2)}, u32[]{:S(2)}) collective-permute-start(f32[18,8,128]{2,1,0:T(8,128)S(1)} %get-tuple-element.40), channel_id=1, source_target_pairs={{0,4},{4,0},{1,5},{5,1},{2,6},{6,2},{3,7},{7,3},{8,12},{12,8},{9,1... | collective-permute-start | bytes 221192 | tf_op jit(solution)/shard_map/ppermute | solution.py:364
  8.5 4.9 %collective-permute-start.2 = (f32[18,8,128]{2,1,0:T(8,128)S(1)}, f32[18,8,128]{2,1,0:T(8,128)S(1)}, u32[]{:S(2)}, u32[]{:S(2)}) collective-permute-start(f32[18,8,128]{2,1,0:T(8,128)S(1)} %get-tuple-element.41), channel_id=1, source_target_pairs={{0,3},{1,2},{2,1},{3,0},{4,7},{5,6},{6,5},{7,4},{8,11},{9,10},{10,... | collective-permute-start | bytes 221192 | tf_op jit(solution)/shard_map/ppermute | solution.py:364
  11.2 3.5 %collective-permute-start.1 = (f32[18,8,128]{2,1,0:T(8,128)S(1)}, f32[18,8,128]{2,1,0:T(8,128)S(1)}, u32[]{:S(2)}, u32[]{:S(2)}) collective-permute-start(f32[18,8,128]{2,1,0:T(8,128)S(1)} %get-tuple-element.41), channel_id=1, source_target_pairs={{0,1},{1,0},{2,3},{3,2},{4,5},{5,4},{6,7},{7,6},{8,9},{9,8},{10,11... | collective-permute-start | bytes 221192 | tf_op jit(solution)/shard_map/ppermute | solution.py:364
  16.3 13.8 %collective-permute-start.8 = (f32[18,8,256]{2,1,0:T(8,128)S(1)}, f32[18,8,256]{2,1,0:T(8,128)S(1)}, u32[]{:S(2)}, u32[]{:S(2)}) collective-permute-start(f32[18,8,256]{2,1,0:T(8,128)S(1)} %get-tuple-element.52), channel_id=1, source_target_pairs={{0,8},{8,0},{1,9},{9,1},{2,10},{10,2},{3,11},{11,3},{4,12},{12,4},... | collective-permute-start | bytes 442376 | tf_op jit(solution)/shard_map/ppermute | solution.py:364
  24.5 9.4 %collective-permute-start.9 = (f32[18,8,256]{2,1,0:T(8,128)S(1)}, f32[18,8,256]{2,1,0:T(8,128)S(1)}, u32[]{:S(2)}, u32[]{:S(2)}) collective-permute-start(f32[18,8,256]{2,1,0:T(8,128)S(1)} %get-tuple-element.55), channel_id=1, source_target_pairs={{0,248},{8,16},{16,8},{24,32},{32,24},{40,48},{48,40},{56,64},{64,... | collective-permute-start | bytes 442376 | tf_op jit(solution)/shard_map/ppermute | solution.py:364
  24.5 4.5 %collective-permute-start.5 = (f32[18,8,128]{2,1,0:T(8,128)S(1)}, f32[18,8,128]{2,1,0:T(8,128)S(1)}, u32[]{:S(2)}, u32[]{:S(2)}) collective-permute-start(f32[18,8,128]{2,1,0:T(8,128)S(1)} %get-tuple-element.50), channel_id=1, source_target_pairs={{0,4},{4,0},{1,5},{5,1},{2,6},{6,2},{3,7},{7,3},{8,12},{12,8},{9,1... | collective-permute-start | bytes 221192 | tf_op jit(solution)/shard_map/ppermute | solution.py:364
  25.7 4.4 %collective-permute-start.7 = (f32[18,8,128]{2,1,0:T(8,128)S(1)}, f32[18,8,128]{2,1,0:T(8,128)S(1)}, u32[]{:S(2)}, u32[]{:S(2)}) collective-permute-start(f32[18,8,128]{2,1,0:T(8,128)S(1)} %get-tuple-element.51), channel_id=1, source_target_pairs={{0,3},{1,2},{2,1},{3,0},{4,7},{5,6},{6,5},{7,4},{8,11},{9,10},{10,... | collective-permute-start | bytes 221192 | tf_op jit(solution)/shard_map/ppermute | solution.py:364
  26.6 3.5 %collective-permute-start.6 = (f32[18,8,128]{2,1,0:T(8,128)S(1)}, f32[18,8,128]{2,1,0:T(8,128)S(1)}, u32[]{:S(2)}, u32[]{:S(2)}) collective-permute-start(f32[18,8,128]{2,1,0:T(8,128)S(1)} %get-tuple-element.51), channel_id=1, source_target_pairs={{0,1},{1,0},{2,3},{3,2},{4,5},{5,4},{6,7},{7,6},{8,9},{9,8},{10,11... | collective-permute-start | bytes 221192 | tf_op jit(solution)/shard_map/ppermute | solution.py:364
  31.7 11.3 %collective-permute-start.13 = (f32[18,8,256]{2,1,0:T(8,128)S(1)}, f32[18,8,256]{2,1,0:T(8,128)S(1)}, u32[]{:S(2)}, u32[]{:S(2)}) collective-permute-start(f32[18,8,256]{2,1,0:T(8,128)S(1)} %get-tuple-element.62), channel_id=1, source_target_pairs={{0,8},{8,0},{1,9},{9,1},{2,10},{10,2},{3,11},{11,3},{4,12},{12,4},... | collective-permute-start | bytes 442376 | tf_op jit(solution)/shard_map/ppermute | solution.py:364
  34.5 10.0 %collective-permute-start.14 = (f32[18,8,256]{2,1,0:T(8,128)S(1)}, f32[18,8,256]{2,1,0:T(8,128)S(1)}, u32[]{:S(2)}, u32[]{:S(2)}) collective-permute-start(f32[18,8,256]{2,1,0:T(8,128)S(1)} %get-tuple-element.65), channel_id=1, source_target_pairs={{0,248},{8,16},{16,8},{24,32},{32,24},{40,48},{48,40},{56,64},{64,... | collective-permute-start | bytes 442376 | tf_op jit(solution)/shard_map/ppermute | solution.py:364
  37.7 5.2 %collective-permute-start.10 = (f32[18,8,128]{2,1,0:T(8,128)S(1)}, f32[18,8,128]{2,1,0:T(8,128)S(1)}, u32[]{:S(2)}, u32[]{:S(2)}) collective-permute-start(f32[18,8,128]{2,1,0:T(8,128)S(1)} %get-tuple-element.60), channel_id=1, source_target_pairs={{0,4},{4,0},{1,5},{5,1},{2,6},{6,2},{3,7},{7,3},{8,12},{12,8},{9,1... | collective-permute-start | bytes 221192 | tf_op jit(solution)/shard_map/ppermute | solution.py:364
  37.7 5.2 %collective-permute-start.12 = (f32[18,8,128]{2,1,0:T(8,128)S(1)}, f32[18,8,128]{2,1,0:T(8,128)S(1)}, u32[]{:S(2)}, u32[]{:S(2)}) collective-permute-start(f32[18,8,128]{2,1,0:T(8,128)S(1)} %get-tuple-element.61), channel_id=1, source_target_pairs={{0,3},{1,2},{2,1},{3,0},{4,7},{5,6},{6,5},{7,4},{8,11},{9,10},{10,... | collective-permute-start | bytes 221192 | tf_op jit(solution)/shard_map/ppermute | solution.py:364
  39.5 3.5 %collective-permute-start.11 = (f32[18,8,128]{2,1,0:T(8,128)S(1)}, f32[18,8,128]{2,1,0:T(8,128)S(1)}, u32[]{:S(2)}, u32[]{:S(2)}) collective-permute-start(f32[18,8,128]{2,1,0:T(8,128)S(1)} %get-tuple-element.61), channel_id=1, source_target_pairs={{0,1},{1,0},{2,3},{3,2},{4,5},{5,4},{6,7},{7,6},{8,9},{9,8},{10,11... | collective-permute-start | bytes 221192 | tf_op jit(solution)/shard_map/ppermute | solution.py:364
  45.6 8.4 %collective-permute-start.17 = (f32[18,8,128]{2,1,0:T(8,128)S(1)}, f32[18,8,128]{2,1,0:T(8,128)S(1)}, u32[]{:S(2)}, u32[]{:S(2)}) collective-permute-start(f32[18,8,128]{2,1,0:T(8,128)S(1)} %get-tuple-element.69), channel_id=1, source_target_pairs={{0,3},{1,2},{2,1},{3,0},{4,7},{5,6},{6,5},{7,4},{8,11},{9,10},{10,... | collective-permute-start | bytes 221192 | tf_op jit(solution)/shard_map/ppermute | solution.py:364
  47.2 6.7 %collective-permute-start.16 = (f32[18,8,128]{2,1,0:T(8,128)S(1)}, f32[18,8,128]{2,1,0:T(8,128)S(1)}, u32[]{:S(2)}, u32[]{:S(2)}) collective-permute-start(f32[18,8,128]{2,1,0:T(8,128)S(1)} %get-tuple-element.69), channel_id=1, source_target_pairs={{0,1},{1,0},{2,3},{3,2},{4,5},{5,4},{6,7},{7,6},{8,9},{9,8},{10,11... | collective-permute-start | bytes 221192 | tf_op jit(solution)/shard_map/ppermute | solution.py:364
  47.2 6.7 %collective-permute-start.18 = (f32[18,8,256]{2,1,0:T(8,128)S(1)}, f32[18,8,256]{2,1,0:T(8,128)S(1)}, u32[]{:S(2)}, u32[]{:S(2)}) collective-permute-start(f32[18,8,256]{2,1,0:T(8,128)S(1)} %get-tuple-element.70), channel_id=1, source_target_pairs={{0,8},{8,0},{1,9},{9,1},{2,10},{10,2},{3,11},{11,3},{4,12},{12,4},... | collective-permute-start | bytes 442376 | tf_op jit(solution)/shard_map/ppermute | solution.py:364
  49.6 4.4 %collective-permute-start.15 = (f32[18,8,128]{2,1,0:T(8,128)S(1)}, f32[18,8,128]{2,1,0:T(8,128)S(1)}, u32[]{:S(2)}, u32[]{:S(2)}) collective-permute-start(f32[18,8,128]{2,1,0:T(8,128)S(1)} %get-tuple-element.68), channel_id=1, source_target_pairs={{0,4},{4,0},{1,5},{5,1},{2,6},{6,2},{3,7},{7,3},{8,12},{12,8},{9,1... | collective-permute-start | bytes 221192 | tf_op jit(solution)/shard_map/ppermute | solution.py:364
  51.3 6.1 %collective-permute-start.19 = (f32[18,8,256]{2,1,0:T(8,128)S(1)}, f32[18,8,256]{2,1,0:T(8,128)S(1)}, u32[]{:S(2)}, u32[]{:S(2)}) collective-permute-start(f32[18,8,256]{2,1,0:T(8,128)S(1)} %get-tuple-element.73), channel_id=1, source_target_pairs={{0,248},{8,16},{16,8},{24,32},{32,24},{40,48},{48,40},{56,64},{64,... | collective-permute-start | bytes 442376 | tf_op jit(solution)/shard_map/ppermute | solution.py:364

commit v2 on v1

v2 whole, which is shorter than its diff:
```python
import functools

import jax
import jax.numpy as jnp
from jax import lax
from jax.experimental import pallas as pl
from jax.experimental.pallas import tpu as pltpu
from jax.sharding import Mesh
from jax.sharding import PartitionSpec as P


ITERS = 2
OMEGA = 1.7
GUARD = 1e-12
TA = ("tz", "tx", "tc")
AXES = TA + ("gz", "gy")
F32 = jnp.float32
R3 = range(3)
PAIRS = ((0, 1), (0, 2), (1, 2))
ROWS = (0, 1, 2, 3, 4, 5, 9, 10, 11, 12, 13, 14)
TWO_ROWS, WHOLE, TURN = range(3)


def re(i, j):
    return 3 * i + j


def im(i, j):
    return 9 + 3 * i + j


def half(h):
    return pl.ds(128 * h, 128)


def times_adjoint(acc, left, right):
    out = list(acc)
    for k in R3:
        lr = [left(re(i, k)) for i in R3]
        li = [left(im(i, k)) for i in R3]
        rr = [right(re(j, k)) for j in R3]
        ri = [right(im(j, k)) for j in R3]
        for i in R3:
            for j in R3:
                tr = lr[i] * rr[j] + li[i] * ri[j]
                ti = li[i] * rr[j] - lr[i] * ri[j]
                a, b = re(i, j), im(i, j)
                out[a] = tr if out[a] is None else out[a] + tr
                out[b] = ti if out[b] is None else out[b] + ti
    return out


def times(left, right):
    out = [None] * 18
    for k in R3:
        lr = [left(re(i, k)) for i in R3]
        li = [left(im(i, k)) for i in R3]
        rr = [right(re(k, j)) for j in R3]
        ri = [right(im(k, j)) for j in R3]
        for i in R3:
            for j in R3:
                tr = lr[i] * rr[j] - li[i] * ri[j]
                ti = lr[i] * ri[j] + li[i] * rr[j]
                a, b = re(i, j), im(i, j)
                out[a] = tr if out[a] is None else out[a] + tr
                out[b] = ti if out[b] is None else out[b] + ti
    return out


def plus_adjoint(acc, mat):
    out = list(acc)
    for i in R3:
        for j in R3:
            out[re(i, j)] = out[re(i, j)] + mat[re(j, i)]
            out[im(i, j)] = out[im(i, j)] - mat[im(j, i)]
    return out


def rotation(a, p, q):
    v0 = a[re(p, p)] + a[re(q, q)]
    v1 = -(a[im(p, q)] + a[im(q, p)])
    v2 = a[re(q, p)] - a[re(p, q)]
    v3 = -(a[im(p, p)] - a[im(q, q)])
    length = jnp.sqrt(v0 * v0 + v1 * v1 + v2 * v2 + v3 * v3)
    s0 = (1.0 - OMEGA) * length + OMEGA * v0
    s1, s2, s3 = OMEGA * v1, OMEGA * v2, OMEGA * v3
    inverse = lax.rsqrt(s0 * s0 + s1 * s1 + s2 * s2 + s3 * s3 + GUARD)
    return s0 * inverse, s1 * inverse, s2 * inverse, s3 * inverse


def rotate(m, quat, p, q):
    q0, q1, q2, q3 = quat
    out = list(m)
    for j in R3:
        ur, ui = m[re(p, j)], m[im(p, j)]
        lr, li = m[re(q, j)], m[im(q, j)]
        out[re(p, j)] = q0 * ur - q3 * ui + q2 * lr - q1 * li
        out[im(p, j)] = q0 * ui + q3 * ur + q2 * li + q1 * lr
        out[re(q, j)] = q0 * lr + q3 * li - q2 * ur - q1 * ui
        out[im(q, j)] = q0 * li - q3 * lr - q2 * ui + q1 * ur
    return out


def relax(g, w):
    a = times(lambda c: g[c], lambda c: w[c])
    turn = []
    for p, q in PAIRS:
        quat = rotation(a, p, q)
        a = rotate(a, quat, p, q)
        g = rotate(g, quat, p, q)
        turn += quat
    return g, a, turn


def turned(mat, turn):
    for k, (p, q) in enumerate(PAIRS):
        mat = rotate(mat, turn[4 * k : 4 * k + 4], p, q)
    return mat


def third_row(rows):
    a = [None] * 18
    for c, v in zip(ROWS, rows):
        a[c] = v
    for j in R3:
        k, m = (j + 1) % 3, (j + 2) % 3
        ur, ui, xr, xi = a[re(0, k)], a[im(0, k)], a[re(1, m)], a[im(1, m)]
        vr, vi, yr, yi = a[re(0, m)], a[im(0, m)], a[re(1, k)], a[im(1, k)]
        a[re(2, j)] = (ur * xr - ui * xi) - (vr * yr - vi * yi)
        a[im(2, j)] = (vr * yi + vi * yr) - (ur * xi + ui * xr)
    return a


def behind(mode, sent, link, before):
    if mode == TURN:
        return turned([before[c] for c in range(18)], [sent(c) for c in range(12)])
    if mode == TWO_ROWS:
        full = third_row([sent(k) for k in range(12)])
        return times_adjoint([None] * 18, lambda c: full[c], link)
    return times_adjoint([None] * 18, sent, link)


def measures(a):
    func = a[re(0, 0)] + a[re(1, 1)] + a[re(2, 2)]
    off = None
    for i, j in PAIRS:
        dr = a[re(i, j)] - a[re(j, i)]
        di = a[im(i, j)] + a[im(j, i)]
        term = dr * dr + di * di
        off = term if off is None else off + term
    mean = (a[im(0, 0)] + a[im(1, 1)] + a[im(2, 2)]) / 3.0
    div = 0.5 * off
    for i in R3:
        d = a[im(i, i)] - mean
        div = div + d * d
    return func, div


def unit(c):
    return 1.0 if c in (0, 4, 8) else 0.0


def crossing(links, h, is_unit):
    return lambda c: jnp.where(is_unit, F32(unit(c)), links[3, c, 1, :, half(h)])


def iotas():
    return (
        lax.broadcasted_iota(jnp.int32, (8, 128), 0),
        lax.broadcasted_iota(jnp.int32, (8, 128), 1),
    )


def slices(core):
    return core, 1 - core


def pack_links(core, links, upz, upy):
    _, lane = iotas()
    for c in range(18):
        upz[c] = jnp.full((8, 128), unit(c), F32)
        for k, s in enumerate(slices(core)):
            for h in range(2):
                r = 4 + 2 * k + h
                upz[c, r : r + 1, :] = links[2, c, s, 7:8, half(h)]
        high0 = pltpu.roll(links[1, c, core, :, half(1)], 96, 1)
        high1 = links[1, c, 1 - core, :, half(1)]
        upy[c] = jnp.where(lane < 64, F32(unit(c)), jnp.where(lane < 96, high0, high1))


def pack_rows(c, k, value, h, scr):
    scr[c, 2 * k + h : 2 * k + h + 1, :] = value[0:1, :]
    scr[c, 4 + 2 * k + h : 5 + 2 * k + h, :] = value[7:8, :]


def pack_z(core, g, upz, zp, scr):
    for c in range(18):
        for k, s in enumerate(slices(core)):
            for h in range(2):
                pack_rows(c, k, g[c, s, :, half(h)], h, scr)
    out = times(lambda c: scr[c], lambda c: upz[c])
    for k, c in enumerate(ROWS if zp.shape[0] == 12 else range(18)):
        zp[k] = out[c]


def row_ends(value):
    _, lane = iotas()
    low1 = pltpu.roll(value(1, 0), 32, 1)
    high0 = pltpu.roll(value(0, 1), 96, 1)
    return jnp.where(
        lane < 64,
        jnp.where(lane < 32, value(0, 0), low1),
        jnp.where(lane < 96, high0, value(1, 1)),
    )


def send_rows(ends, lowp, highp):
    _, lane = iotas()
    for k in range(lowp.shape[0]):
        a, b = ends[2 * k], ends[2 * k + 1]
        lowp[k] = jnp.where(lane < 64, a, pltpu.roll(b, 64, 1))
        highp[k] = jnp.where(lane < 64, pltpu.roll(a, 64, 1), b)


def received_rows(c, yu, yd):
    _, lane = iotas()
    u, d = yu[c // 2], yd[c // 2]
    if c % 2:
        return jnp.where(lane < 64, pltpu.roll(u, 64, 1), d)
    return jnp.where(lane < 64, u, pltpu.roll(d, 64, 1))


def pack_y(core, g, upy, lowp, highp):
    ends = [
        row_ends(lambda k, h: g[c, slices(core)[k], :, half(h)]) for c in range(18)
    ]
    out = times(lambda c: ends[c], lambda c: upy[c])
    if lowp.shape[0] == 6:
        out = [out[c] for c in ROWS]
    send_rows(out, lowp, highp)


def first_kernel(
    links_hbm, g_hbm, links, g, tp, fp, zp, lowp, highp, upz0, upy0, upz1, upy1, scr, sems
):
    copies = []
    for colour in (1, 0):
        copies.append((g_hbm.at[colour], g.at[colour]))
        for mu in (3, 2, 1, 0):
            copies.append((links_hbm.at[colour, mu], links.at[colour, mu]))
    copies = [pltpu.make_async_copy(a, b, sems.at[k]) for k, (a, b) in enumerate(copies)]
    for copy in copies:
        copy.start()
    core = lax.axis_index("tc")
    far, near = slices(core)
    for copy in copies[:2]:
        copy.wait()
    for h in range(2):
        face = times(lambda c: g[1, c, far, :, half(h)], crossing(links.at[1], h, core == 0))
        for k, c in enumerate(ROWS):
            fp[k, :, half(h)] = face[c]
        face = times(lambda c: g[1, c, near, :, half(h)], crossing(links.at[1], h, core == 1))
        for c in range(18):
            tp[c, :, half(h)] = face[c]
    for copy in copies[2:4]:
        copy.wait()
    pack_links(core, links.at[1], upz1, upy1)
    pack_z(core, g.at[1], upz1, zp, scr)
    pack_y(core, g.at[1], upy1, lowp, highp)
    for copy in copies[4:]:
        copy.wait()
    pack_links(core, links.at[0], upz0, upy0)


def local_kernel(colour, first, links, gp, w):
    own, other = links.at[colour], links.at[1 - colour]
    if first:
        gp = gp.at[1 - colour]
    row, lane = iotas()
    column = lane % 32
    parity = (row + lane // 32) % 2
    for s in range(2):
        stays = parity == (s + colour) % 2
        behind = []
        for h in range(2):
            behind.append(
                times(lambda c: gp[c, s, :, half(h)], lambda c: other[1, c, s, :, half(h)])
            )
        low, high = [], []
        for c in range(18):
            r0 = pltpu.roll(behind[0][c], 32, 1)
            r1 = pltpu.roll(behind[1][c], 32, 1)
            low.append(jnp.where(lane < 32, 0.0, r0))
            high.append(jnp.where(lane < 32, r0, r1))
        for h, mat in ((0, low), (1, high)):
            acc = plus_adjoint([jnp.zeros((8, 128), F32)] * 18, mat)
            for c in range(18):
                w[c, s, :, half(h)] = acc[c]
        for h in range(2):
            acc = [w[c, s, :, half(h)] for c in range(18)]

            def tile(c):
                return gp[c, s, :, half(h)]

            def ahead_x(c):
                v = tile(c)
                step = jnp.where(column == 31, pltpu.roll(v, 31, 1), pltpu.roll(v, 127, 1))
                return jnp.where(stays, v, step)

            acc = times_adjoint(acc, lambda c: own[0, c, s, :, half(h)], ahead_x)

            def ahead_y(c):
                a = pltpu.roll(gp[c, s, :, half(1)], 96, 1)
                if h == 0:
                    return jnp.where(lane >= 96, a, pltpu.roll(tile(c), 96, 1))
                return jnp.where(lane >= 96, 0.0, a)

            acc = times_adjoint(acc, lambda c: own[1, c, s, :, half(h)], ahead_y)

            def ahead_z(c):
                return jnp.where(row == 7, 0.0, pltpu.roll(tile(c), 7, 0))

            acc = times_adjoint(acc, lambda c: own[2, c, s, :, half(h)], ahead_z)
            back = times(tile, lambda c: other[0, c, s, :, half(h)])
            shifted = []
            for v in back:
                step = jnp.where(column == 0, pltpu.roll(v, 97, 1), pltpu.roll(v, 1, 1))
                shifted.append(jnp.where(stays, step, v))
            acc = plus_adjoint(acc, shifted)
            back = times(tile, lambda c: other[2, c, s, :, half(h)])
            acc = plus_adjoint(acc, [jnp.where(row == 0, 0.0, pltpu.roll(v, 1, 0)) for v in back])
            if s == 0:
                acc = times_adjoint(
                    acc,
                    lambda c: own[3, c, 0, :, half(h)],
                    lambda c: gp[c, 1, :, half(h)],
                )
            else:
                back = times(
                    lambda c: gp[c, 0, :, half(h)], lambda c: other[3, c, 0, :, half(h)]
                )
                acc = plus_adjoint(acc, back)
            for c in range(18):
                w[c, s, :, half(h)] = acc[c]


def near_kernel(step, links, g, w, upz, upy, zh, yu, yd, th, *refs):
    refs = list(refs)
    before = [refs.pop(0), refs.pop(0)] if step.mode == TURN else [None, None]
    gn, wf = refs.pop(0), refs.pop(0)
    kept = [refs.pop(0), refs.pop(0)] if step.keeps else [None, None]
    tp = None if step.last else refs.pop(0)
    qn = refs.pop(0) if step.sends == TURN else None
    sums = refs.pop(0) if step.colour == 1 else None
    z_scr, y_scr = refs
    own = links.at[step.colour]
    if step.first:
        g = g.at[step.colour]
    core = lax.axis_index("tc")
    far, near = slices(core)
    row, lane = iotas()
    part = behind(
        step.mode, lambda c: zh[c], lambda c: pltpu.roll(upz[c], 4, 0), before[0]
    )
    for c in range(18):
        z_scr[c] = part[c]
        if kept[0] is not None:
            kept[0][c] = part[c]
    part = behind(
        step.mode,
        lambda c: received_rows(c, yu, yd),
        lambda c: pltpu.roll(upy[c], 64, 1),
        before[1],
    )
    for c in range(18):
        v = part[c]
        if kept[1] is not None:
            kept[1][c] = v
        for k in range(2):
            y_scr[c, k, :, half(0)] = jnp.where(lane < 32, pltpu.roll(v, 64 - 32 * k, 1), 0.0)
            y_scr[c, k, :, half(1)] = jnp.where(lane < 96, 0.0, pltpu.roll(v, 96 - 32 * k, 1))

    def with_sides(k, s, h):
        side = []
        for c in range(18):
            r = 2 * k + h
            up = jnp.broadcast_to(z_scr[c, r : r + 1, :], (8, 128))
            down = jnp.broadcast_to(z_scr[c, 4 + r : 5 + r, :], (8, 128))
            edge = jnp.where(row == 7, up, jnp.where(row == 0, down, 0.0))
            side.append(edge + y_scr[c, k, :, half(h)])
        return plus_adjoint([w[c, s, :, half(h)] for c in range(18)], side)

    total = None
    for h in range(2):
        acc = with_sides(0, far, h)
        for c in range(18):
            wf[c, :, half(h)] = acc[c]
        link = crossing(own, h, core == 1)
        acc = with_sides(1, near, h)
        acc = times_adjoint(acc, link, lambda c: th[c, :, half(h)])
        new, mat, turn = relax([g[c, near, :, half(h)] for c in range(18)], acc)
        for c in range(18):
            gn[c, :, half(h)] = new[c]
        if tp is not None:
            face = times(lambda c: new[c], link)
            for c in range(18):
                tp[c, :, half(h)] = face[c]
        if qn is not None:
            for k in range(12):
                qn[k, :, half(h)] = turn[k]
        if sums is not None:
            now = measures(mat)
            total = now if total is None else [a + b for a, b in zip(total, now)]
    if sums is not None:
        sums[0] = total[0]
        sums[1] = total[1]


def far_kernel(step, links, g, gn, wf, fh, *refs):
    refs = list(refs)
    before = refs.pop(0) if step.mode == TURN else None
    near_sums = refs.pop(0) if step.colour == 1 else None
    line = refs.pop(0) if step.colour == 1 and step.number > 1 else None
    g0 = refs.pop(0) if step.last else None
    upz = refs.pop(0) if step.sends == WHOLE else None
    upy = refs.pop(0) if step.sends == WHOLE else None
    qn = refs.pop(0) if step.sends == TURN else None
    out = refs.pop(0)
    kept = refs.pop(0) if step.keeps else None
    fp, zp, lowp, highp = [None] * 4 if step.last else [refs.pop(0) for _ in range(4)]
    sums = refs.pop(0) if step.colour == 1 else None
    own = links.at[step.colour]
    if step.first:
        g = g.at[step.colour]
    core = lax.axis_index("tc")
    far, near = slices(core)
    total = None if sums is None else [near_sums[0], near_sums[1]]
    to = out.at[1] if step.last else out
    for h in range(2):
        link = crossing(own, h, core == 0)
        part = behind(
            step.mode,
            lambda c: fh[c, :, half(h)],
            link,
            None if before is None else [before[c, :, half(h)] for c in range(18)],
        )
        if kept is not None:
            for c in range(18):
                kept[c, :, half(h)] = part[c]
        acc = plus_adjoint([wf[c, :, half(h)] for c in range(18)], part)
        new, mat, turn = relax([g[c, far, :, half(h)] for c in range(18)], acc)
        for c in range(18):
            to[c, far, :, half(h)] = new[c]
        if step.sends == WHOLE:
            face = times(lambda c: new[c], link)
            for c in range(18):
                fp[c, :, half(h)] = face[c]
        if step.sends == TURN:
            for k in range(12):
                fp[k, :, half(h)] = turn[k]
                pack_rows(k, 0, turn[k], h, zp)
                pack_rows(k, 1, qn[k, :, half(h)], h, zp)
        if sums is not None:
            total = [a + b for a, b in zip(total, measures(mat))]
    for c in range(18):
        to[c, near] = gn[c]
    if step.last:
        for c in range(18):
            for s in range(2):
                out[0, c, s] = g0[c, s]
    else:
        if step.sends == WHOLE:
            pack_z(core, out, upz, zp, refs.pop(0))
            pack_y(core, out, upy, lowp, highp)
        else:
            ends = [row_ends(lambda j, h: (fp, qn)[j][k, :, half(h)]) for k in range(12)]
            send_rows(ends, lowp, highp)
    if sums is not None:
        lane = lax.broadcasted_iota(jnp.int32, (1, 128), 1)
        line = jnp.zeros((1, 128), F32) if line is None else line[...]
        for k in range(2):
            rows = jnp.sum(total[k], axis=0, keepdims=True)
            value = jnp.sum(rows, axis=1, keepdims=True)
            line = jnp.where(lane == ITERS * k + step.number // 2, value, line)
        sums[...] = line


def final_kernel(volume, parts, monitor):
    total = jnp.sum(parts[...], axis=0)
    both = jnp.concatenate([total, pltpu.roll(total, 128 - ITERS, 1)], axis=0)
    row = lax.broadcasted_iota(jnp.int32, (2, 128), 0)
    both = jnp.where(row == 0, 1.0 - both / (12.0 * volume), both / (volume / 2.0))
    monitor[...] = both[:, :ITERS]


def call(body, outs, scratch, args, flops, space=pltpu.VMEM):
    return pl.pallas_call(
        body,
        out_shape=[jax.ShapeDtypeStruct(o, F32) for o in outs],
        in_specs=[pl.BlockSpec(memory_space=space)] * len(args),
        out_specs=[pl.BlockSpec(memory_space=pltpu.VMEM)] * len(outs),
        scratch_shapes=[s if not isinstance(s, tuple) else pltpu.VMEM(s, F32) for s in scratch],
        compiler_params=pltpu.CompilerParams(vmem_limit_bytes=24 * 2**20),
        cost_estimate=pl.CostEstimate(flops=flops, bytes_accessed=0, transcendentals=0),
    )(*args)


def swap(value, axis, partner):
    count = lax.axis_size(axis)
    return lax.ppermute(value, axis, [(i, partner(i) % count) for i in range(count)])


def even_odd(i):
    return i ^ 1


def odd_even(i):
    return i + 1 if i % 2 else i - 1


FACE = (18, 8, 256)
SIDE = (18, 8, 128)
FIELD = (18, 2, 8, 256)
FACE_12 = (12, 8, 256)
SIDE_12 = (12, 8, 128)
ROW = (9, 8, 128)
ROW_12 = (6, 8, 128)
SUMS = (2, 8, 128)
SENT = {WHOLE: [FACE, SIDE, ROW, ROW], TURN: [FACE_12, SIDE_12, ROW_12, ROW_12]}


class Step:
    def __init__(self, number):
        self.number = number
        self.colour = number % 2
        self.first = number < 2
        self.last = number == 2 * ITERS - 1
        self.mode = TWO_ROWS if number == 0 else WHOLE if number == 1 else TURN
        self.keeps = number < 2 * ITERS - 2
        self.sends = None if self.last else WHOLE if number == 0 else TURN


def shards(lattice_links, transform):
    volume = 2 * transform.shape[2] * transform.shape[3] * transform.shape[4]
    for axis in AXES:
        volume *= lax.axis_size(axis)
    links, start, tp, fp, zp, lowp, highp, *sides = call(
        first_kernel,
        [lattice_links.shape, transform.shape, FACE, FACE_12, SIDE_12, ROW_12, ROW_12]
        + [SIDE] * 4,
        [SIDE, pltpu.SemaphoreType.DMA((10,))],
        [pltpu.with_memory_space_constraint(v, pltpu.HBM) for v in (lattice_links, transform)],
        10**7,
        pltpu.HBM,
    )
    g = [start, start]
    packed = [sides[:2], sides[2:]]
    kept_far, kept_side = [None, None], [None, None]
    th = swap(tp, "tc", even_odd)
    line = None
    for step in map(Step, range(2 * ITERS)):
        colour = step.colour
        fh = swap(fp, TA, odd_even)
        yu = swap(lowp, "gy", lambda i: i - 1)
        yd = swap(highp, "gy", lambda i: i + 1)
        zh = swap(zp, "gz", even_odd)
        (w,) = call(
            functools.partial(local_kernel, colour, step.number == 0),
            [FIELD],
            [],
            [links, g[1 - colour]],
            3 * 10**7,
        )
        outs = [FACE, FACE]
        outs += [SIDE, SIDE] if step.keeps else []
        outs += [] if step.last else [FACE]
        outs += [FACE_12] if step.sends == TURN else []
        outs += [SUMS] if colour == 1 else []
        args = [links, g[colour], w, *packed[colour], zh, yu, yd, th]
        args += kept_side[colour] if step.mode == TURN else []
        gn, wf, *rest = call(functools.partial(near_kernel, step), outs, [SIDE, FIELD], args, 10**7)
        if step.keeps:
            kept_side[colour] = [rest.pop(0), rest.pop(0)]
        if not step.last:
            th = swap(rest.pop(0), "tc", even_odd)
        args = [links, g[colour], gn, wf, fh]
        args += [kept_far[colour]] if step.mode == TURN else []
        args += [rest.pop()] if colour == 1 else []
        args += [line] if line is not None and colour == 1 else []
        args += [g[0]] if step.last else []
        args += packed[colour] if step.sends == WHOLE else []
        args += [rest.pop()] if step.sends == TURN else []
        outs = [(2,) + FIELD] if step.last else [FIELD]
        outs += [FACE] if step.keeps else []
        if not step.last:
            outs += SENT[step.sends]
        outs += [(1, 128)] if colour == 1 else []
        out, *rest = call(
            functools.partial(far_kernel, step),
            outs,
            [SIDE] if step.sends == WHOLE else [],
            args,
            10**7,
        )
        g[colour] = out
        if step.keeps:
            kept_far[colour] = rest.pop(0)
        if not step.last:
            fp, zp, lowp, highp, *rest = rest
        if colour == 1:
            (line,) = rest
    count = 1
    for axis in AXES:
        count *= lax.axis_size(axis)
    parts = jnp.broadcast_to(line[None], (count, 1, 128))
    parts = lax.all_to_all(parts, AXES, 0, 0, tiled=True)
    (monitor,) = call(functools.partial(final_kernel, volume), [(2, ITERS)], [], [parts], 10**3)
    return (out, monitor)


def solution(mesh):
    finer = Mesh(
        mesh.devices.reshape(8, 2, 2, mesh.shape["gz"], mesh.shape["gy"]),
        AXES,
    )
    return jax.shard_map(
        shards,
        mesh=finer,
        in_specs=(P(None, None, None, TA, "gz", "gy"), P(None, None, TA, "gz", "gy")),
        out_specs=(P(None, None, TA, "gz", "gy"), P()),
        check_vma=False,
    )
```

time: 84.4 us -> 73.7 us (0.87)
  waiting for transfers between devices: 15 us -> 5.66 us
  starting transfers between devices: 29.6 us -> 33.3 us
  blocking collectives: 25 us -> 21.5 us
  local copies, waits for them, and re-layouts: 2.95 us -> 0.07 us
  Pallas kernels: 10.9 us -> 12.3 us
    ppermute x20, waiting for transfers between devices: 15 us -> 5.66 us  [swap(): lax.ppermute(value, axis, [(i, partner(i) % count) for i in range(count)])]
    ppermute x20, starting transfers between devices: 29.6 us -> 33.3 us  [swap(): lax.ppermute(value, axis, [(i, partner(i) % count) for i in range(count)])]
    all_to_all x2 -> x1, blocking collectives: 25 us -> 21.5 us  [shards(): parts = lax.all_to_all(parts, AXES, 0, 0, tiled=True)]
    squeeze x3 -> x0, local copies, waits for them, and re-layouts: 2.93 us -> none  [the longest x1 1.83 us: shards(): links = [lattice_links[0], lattice_links[1]]]
    pallas_call x10 -> x14, Pallas kernels: 10.9 us -> 12.3 us  [call(): pl.pallas_call(body, out_shape=[jax.ShapeDtypeStruct(o, F32) for o in out...]
  transfers between devices with their start and end apart: 20 -> 20, of which waited for: 8 -> 4; matrix products, arithmetic and copies ran while one was open for 0% -> 0% of each run, Pallas kernels for 9% -> 11%
where the time goes in v2:
time: 73.7 us; the launch traced here: 73.6 us
  starting transfers between devices  33.3 us (45%)
  blocking collectives  21.5 us (29%)
  Pallas kernels  12.3 us (17%)
  waiting for transfers between devices  5.66 us (8%)
  between operations  0.77 us (1%)
    ppermute x20, starting transfers between devices, swap(): lax.ppermute(value, axis, [(i, partner(i) % count) for i in range(count)])  33.3 us
    all_to_all x1, blocking collectives, shards(): parts = lax.all_to_all(parts, AXES, 0, 0, tiled=True)  21.5 us
    pallas_call x14, Pallas kernels, call(): pl.pallas_call(body, out_shape=[jax.ShapeDtypeStruct(o, F32) for o in out...  12.3 us
    ppermute x20, waiting for transfers between devices, swap(): lax.ppermute(value, axis, [(i, partner(i) % count) for i in range(count)])  5.66 us
  transfers between devices with their start and end apart: 20, of which 4 were waited for; matrix products, arithmetic and copies ran while one was open for 0% of the time, Pallas kernels for 11%

profile of v2, /device:TPU:1, one launch (start us, length us, event | category | flops | bytes accessed | tf_op | source)
XLA Modules:
  0.0 73.6 jit_solution(9034657432703119928)
XLA Ops:
  0.6 2.0 %shard_map.41 = (f32[2,4,18,2,8,256]{5,4,3,2,1,0:T(8,128)S(1)}, f32[2,18,2,8,256]{4,3,2,1,0:T(8,128)S(1)}, f32[18,8,256]{2,1,0:T(8,128)S(1)}, f32[12,8,256]{2,1,...) custom-call(f32[2,4,18,2,8,256]{5,4,3,2,1,0:T(8,128)} %links_hbm.1, ...), custom_call_target="tpu_custom_call" | custom-call | flops 10000000 | tf_op jit(solution)/shard_map/pallas_call | solution.py:497
  2.6 3.3 %collective-permute-start.3 = (f32[18,8,256]{2,1,0:T(8,128)S(1)}, f32[18,8,256]{2,1,0:T(8,128)S(1)}, u32[]{:S(2)}, u32[]{:S(2)}) collective-permute-start(f32[18,8,256]{2,1,0:T(8,128)S(1)} %get-tuple-element.59), channel_id=1, source_target_pairs={{0,8},{8,0},{1,9},{9,1},{2,10},{10,2},{3,11},{11,3},{4,12},{12,4},... | collective-permute-start | bytes 442376 | tf_op jit(solution)/shard_map/ppermute | solution.py:510
  5.9 2.2 %collective-permute-start.1 = (f32[6,8,128]{2,1,0:T(8,128)S(1)}, f32[6,8,128]{2,1,0:T(8,128)S(1)}, u32[]{:S(2)}, u32[]{:S(2)}) collective-permute-start(f32[6,8,128]{2,1,0:T(8,128)S(1)} %get-tuple-element.57), channel_id=1, source_target_pairs={{0,3},{1,0},{2,1},{3,2},{4,7},{5,4},{6,5},{7,6},{8,11},{9,8},{10,9... | collective-permute-start | bytes 73736 | tf_op jit(solution)/shard_map/ppermute | solution.py:510
  8.1 0.0 collective-permute-start.2
  8.1 3.0 %collective-permute-start.4 = (f32[12,8,256]{2,1,0:T(8,128)S(1)}, f32[12,8,256]{2,1,0:T(8,128)S(1)}, u32[]{:S(2)}, u32[]{:S(2)}) collective-permute-start(f32[12,8,256]{2,1,0:T(8,128)S(1)} %get-tuple-element.62), channel_id=1, source_target_pairs={{0,248},{8,16},{16,8},{24,32},{32,24},{40,48},{48,40},{56,64},{64,... | collective-permute-start | bytes 294920 | tf_op jit(solution)/shard_map/ppermute | solution.py:510
  11.1 1.2 %shard_map.42.w = f32[18,2,8,256]{3,2,1,0:T(8,128)S(1)} custom-call(f32[2,4,18,2,8,256]{5,4,3,2,1,0:T(8,128)S(1)} %get-tuple-element.52.links, f32[2,18,2,8,256]{4,3,2,1,0:T(8,128)S(1)} %get-tuple-element.53.gp.g), custom_call_target="tpu_custom_call" | custom-call | flops 30000000 | tf_op jit(solution)/shard_map/pallas_call | solution.py:497
  12.3 0.0 collective-permute-done.1.yu
  12.3 0.0 collective-permute-done.2.yd
  12.3 0.0 collective-permute-done.3.th
  12.4 0.6 shard_map.43
  12.9 5.2 %collective-permute-start.8 = (f32[18,8,256]{2,1,0:T(8,128)S(1)}, f32[18,8,256]{2,1,0:T(8,128)S(1)}, u32[]{:S(2)}, u32[]{:S(2)}) collective-permute-start(f32[18,8,256]{2,1,0:T(8,128)S(1)} %get-tuple-element.69), channel_id=1, source_target_pairs={{0,8},{8,0},{1,9},{9,1},{2,10},{10,2},{3,11},{11,3},{4,12},{12,4},... | collective-permute-start | bytes 442376 | tf_op jit(solution)/shard_map/ppermute | solution.py:510
  18.2 0.0 collective-permute-done.4.fh
  18.2 0.6 shard_map.44
  18.7 0.1 collective-permute-start.5
  18.8 0.4 collective-permute-start.9
  19.2 3.0 %collective-permute-start.6 = (f32[9,8,128]{2,1,0:T(8,128)S(1)}, f32[9,8,128]{2,1,0:T(8,128)S(1)}, u32[]{:S(2)}, u32[]{:S(2)}) collective-permute-start(f32[9,8,128]{2,1,0:T(8,128)S(1)} %get-tuple-element.67), channel_id=1, source_target_pairs={{0,3},{1,0},{2,1},{3,2},{4,7},{5,4},{6,5},{7,6},{8,11},{9,8},{10,9... | collective-permute-start | bytes 110600 | tf_op jit(solution)/shard_map/ppermute | solution.py:510
  22.2 1.2 %shard_map.45.w = f32[18,2,8,256]{3,2,1,0:T(8,128)S(1)} custom-call(f32[2,4,18,2,8,256]{5,4,3,2,1,0:T(8,128)S(1)} %get-tuple-element.52.links, f32[18,2,8,256]{3,2,1,0:T(8,128)S(1)} %get-tuple-element.63.gp.g), custom_call_target="tpu_custom_call" | custom-call | flops 30000000 | tf_op jit(solution)/shard_map/pallas_call | solution.py:497
  23.3 0.0 collective-permute-done.6.yu
  23.3 3.1 %collective-permute-done.7.yd = f32[9,8,128]{2,1,0:T(8,128)S(1)} collective-permute-done((f32[9,8,128]{2,1,0:T(8,128)S(1)}, f32[9,8,128]{2,1,0:T(8,128)S(1)}, u32[]{:S(2)}, u32[]{:S(2)}) %collective-permute-start.7) | collective-permute-done | bytes 36896 | tf_op jit(solution)/shard_map/ppermute | solution.py:510
  26.5 0.0 collective-permute-done.5.zh
  26.5 0.0 collective-permute-done.8.th
  26.5 0.6 shard_map.46
  27.1 6.9 %collective-permute-start.13 = (f32[18,8,256]{2,1,0:T(8,128)S(1)}, f32[18,8,256]{2,1,0:T(8,128)S(1)}, u32[]{:S(2)}, u32[]{:S(2)}) collective-permute-start(f32[18,8,256]{2,1,0:T(8,128)S(1)} %get-tuple-element.79), channel_id=1, source_target_pairs={{0,8},{8,0},{1,9},{9,1},{2,10},{10,2},{3,11},{11,3},{4,12},{12,4},... | collective-permute-start | bytes 442376 | tf_op jit(solution)/shard_map/ppermute | solution.py:510
  34.0 0.4 shard_map.47
  34.4 0.6 collective-permute-start.10
  35.0 0.0 collective-permute-start.14
  35.0 0.0 collective-permute-start.11
  35.0 1.5 %collective-permute-start.12 = (f32[6,8,128]{2,1,0:T(8,128)S(1)}, f32[6,8,128]{2,1,0:T(8,128)S(1)}, u32[]{:S(2)}, u32[]{:S(2)}) collective-permute-start(f32[6,8,128]{2,1,0:T(8,128)S(1)} %get-tuple-element.78), channel_id=1, source_target_pairs={{0,1},{1,2},{2,3},{3,0},{4,5},{5,6},{6,7},{7,4},{8,9},{9,10},{10,1... | collective-permute-start | bytes 73736 | tf_op jit(solution)/shard_map/ppermute | solution.py:510
  36.5 1.2 %shard_map.48.w = f32[18,2,8,256]{3,2,1,0:T(8,128)S(1)} custom-call(f32[2,4,18,2,8,256]{5,4,3,2,1,0:T(8,128)S(1)} %get-tuple-element.52.links, f32[18,2,8,256]{3,2,1,0:T(8,128)S(1)} %get-tuple-element.75.gp.g), custom_call_target="tpu_custom_call" | custom-call | flops 30000000 | tf_op jit(solution)/shard_map/pallas_call | solution.py:497
  37.6 0.3 collective-permute-done.11.yu
  38.0 0.9 %collective-permute-done.12.yd = f32[6,8,128]{2,1,0:T(8,128)S(1)} collective-permute-done((f32[6,8,128]{2,1,0:T(8,128)S(1)}, f32[6,8,128]{2,1,0:T(8,128)S(1)}, u32[]{:S(2)}, u32[]{:S(2)}) %collective-permute-start.12) | collective-permute-done | bytes 24608 | tf_op jit(solution)/shard_map/ppermute | solution.py:510
  38.9 0.0 collective-permute-done.10.zh
  38.9 0.0 collective-permute-done.13.th
  38.9 0.5 shard_map.49
  39.4 4.1 %collective-permute-start.18 = (f32[18,8,256]{2,1,0:T(8,128)S(1)}, f32[18,8,256]{2,1,0:T(8,128)S(1)}, u32[]{:S(2)}, u32[]{:S(2)}) collective-permute-start(f32[18,8,256]{2,1,0:T(8,128)S(1)} %get-tuple-element.91), channel_id=1, source_target_pairs={{0,8},{8,0},{1,9},{9,1},{2,10},{10,2},{3,11},{11,3},{4,12},{12,4},... | collective-permute-start | bytes 442376 | tf_op jit(solution)/shard_map/ppermute | solution.py:510
  43.6 0.4 shard_map.50
  43.9 0.4 collective-permute-start.19
  44.4 1.2 %collective-permute-start.15 = (f32[12,8,128]{2,1,0:T(8,128)S(1)}, f32[12,8,128]{2,1,0:T(8,128)S(1)}, u32[]{:S(2)}, u32[]{:S(2)}) collective-permute-start(f32[12,8,128]{2,1,0:T(8,128)S(1)} %get-tuple-element.88), channel_id=1, source_target_pairs={{0,4},{4,0},{1,5},{5,1},{2,6},{6,2},{3,7},{7,3},{8,12},{12,8},{9,1... | collective-permute-start | bytes 147464 | tf_op jit(solution)/shard_map/ppermute | solution.py:510
  45.5 0.0 collective-permute-start.16
  45.5 1.5 %collective-permute-start.17 = (f32[6,8,128]{2,1,0:T(8,128)S(1)}, f32[6,8,128]{2,1,0:T(8,128)S(1)}, u32[]{:S(2)}, u32[]{:S(2)}) collective-permute-start(f32[6,8,128]{2,1,0:T(8,128)S(1)} %get-tuple-element.90), channel_id=1, source_target_pairs={{0,1},{1,2},{2,3},{3,0},{4,5},{5,6},{6,7},{7,4},{8,9},{9,10},{10,1... | collective-permute-start | bytes 73736 | tf_op jit(solution)/shard_map/ppermute | solution.py:510
  47.0 1.2 %shard_map.51.w = f32[18,2,8,256]{3,2,1,0:T(8,128)S(1)} custom-call(f32[2,4,18,2,8,256]{5,4,3,2,1,0:T(8,128)S(1)} %get-tuple-element.52.links, f32[18,2,8,256]{3,2,1,0:T(8,128)S(1)} %get-tuple-element.87.gp.refs_3_), custom_call_target="tpu_custom_call" | custom-call | flops 30000000 | tf_op jit(solution)/shard_map/pallas_call | solution.py:497
  48.2 0.0 collective-permute-done.16.yu
  48.2 1.2 %collective-permute-done.17.yd = f32[6,8,128]{2,1,0:T(8,128)S(1)} collective-permute-done((f32[6,8,128]{2,1,0:T(8,128)S(1)}, f32[6,8,128]{2,1,0:T(8,128)S(1)}, u32[]{:S(2)}, u32[]{:S(2)}) %collective-permute-start.17) | collective-permute-done | bytes 24608 | tf_op jit(solution)/shard_map/ppermute | solution.py:510
  49.4 0.5 shard_map.52
  50.0 1.2 %shard_map.53 = (f32[2,18,2,8,256]{4,3,2,1,0:T(8,128)}, f32[1,128]{1,0:T(1,128)S(1)}) custom-call(f32[2,4,18,2,8,256]{5,4,3,2,1,0:T(8,128)S(1)} %get-tuple-element.52.links, f32[18,2,8,256]{3,2,1,0:T(8,128)S(1)} %get-tuple-element.75.gp.g, f32[18,8,256]{2,1,0:T(8,128)S(1)} %get-tuple-element.94.gn, f32[18,8,256]{2,1,0:T(8,128)S(1)} %get-tuple-element.95.wf, ...), custom_call_target="tpu_custom_call" | custom-call | flops 10000000 | tf_op jit(solution)/shard_map/pallas_call | solution.py:497
  51.1 0.1 broadcast_in_dim.9
  51.2 21.5 %all_to_all.5.parts = f32[256,1,128]{2,1,0:T(1,128)S(1)} all-to-all(f32[256,1,128]{2,1,0:T(1,128)S(1)} %broadcast_in_dim.9), channel_id=1, replica_groups=mesh['tz'=8,'tx'=2,'tc'=2,'gz'=2,'gy'=4] {'tz','tx','tc','gz','gy'}, dimensions={0} | all-to-all | bytes 262144 | tf_op jit(solution)/shard_map/all_to_all | solution.py:616
  72.7 0.9 %shard_map.54 = f32[2,2]{1,0:T(2,128)} custom-call(f32[256,1,128]{2,1,0:T(1,128)S(1)} %all_to_all.5.parts), custom_call_target="tpu_custom_call" | custom-call | flops 1000 | tf_op jit(solution)/shard_map/pallas_call | solution.py:497
  (8 shorter events, 0.0 us)
Async XLA Ops:
  2.6 9.7 %collective-permute-start.3 = (f32[18,8,256]{2,1,0:T(8,128)S(1)}, f32[18,8,256]{2,1,0:T(8,128)S(1)}, u32[]{:S(2)}, u32[]{:S(2)}) collective-permute-start(f32[18,8,256]{2,1,0:T(8,128)S(1)} %get-tuple-element.59), channel_id=1, source_target_pairs={{0,8},{8,0},{1,9},{9,1},{2,10},{10,2},{3,11},{11,3},{4,12},{12,4},... | collective-permute-start | bytes 442376 | tf_op jit(solution)/shard_map/ppermute | solution.py:510
  5.9 6.4 %collective-permute-start = (f32[12,8,128]{2,1,0:T(8,128)S(1)}, f32[12,8,128]{2,1,0:T(8,128)S(1)}, u32[]{:S(2)}, u32[]{:S(2)}) collective-permute-start(f32[12,8,128]{2,1,0:T(8,128)S(1)} %get-tuple-element.56), channel_id=1, source_target_pairs={{0,4},{4,0},{1,5},{5,1},{2,6},{6,2},{3,7},{7,3},{8,12},{12,8},{9,1... | collective-permute-start | bytes 147464 | tf_op jit(solution)/shard_map/ppermute | solution.py:510
  5.9 6.4 %collective-permute-start.1 = (f32[6,8,128]{2,1,0:T(8,128)S(1)}, f32[6,8,128]{2,1,0:T(8,128)S(1)}, u32[]{:S(2)}, u32[]{:S(2)}) collective-permute-start(f32[6,8,128]{2,1,0:T(8,128)S(1)} %get-tuple-element.57), channel_id=1, source_target_pairs={{0,3},{1,0},{2,1},{3,2},{4,7},{5,4},{6,5},{7,6},{8,11},{9,8},{10,9... | collective-permute-start | bytes 73736 | tf_op jit(solution)/shard_map/ppermute | solution.py:510
  8.1 4.2 %collective-permute-start.2 = (f32[6,8,128]{2,1,0:T(8,128)S(1)}, f32[6,8,128]{2,1,0:T(8,128)S(1)}, u32[]{:S(2)}, u32[]{:S(2)}) collective-permute-start(f32[6,8,128]{2,1,0:T(8,128)S(1)} %get-tuple-element.58), channel_id=1, source_target_pairs={{0,1},{1,2},{2,3},{3,0},{4,5},{5,6},{6,7},{7,4},{8,9},{9,10},{10,1... | collective-permute-start | bytes 73736 | tf_op jit(solution)/shard_map/ppermute | solution.py:510
  8.1 10.0 %collective-permute-start.4 = (f32[12,8,256]{2,1,0:T(8,128)S(1)}, f32[12,8,256]{2,1,0:T(8,128)S(1)}, u32[]{:S(2)}, u32[]{:S(2)}) collective-permute-start(f32[12,8,256]{2,1,0:T(8,128)S(1)} %get-tuple-element.62), channel_id=1, source_target_pairs={{0,248},{8,16},{16,8},{24,32},{32,24},{40,48},{48,40},{56,64},{64,... | collective-permute-start | bytes 294920 | tf_op jit(solution)/shard_map/ppermute | solution.py:510
  12.9 13.6 %collective-permute-start.8 = (f32[18,8,256]{2,1,0:T(8,128)S(1)}, f32[18,8,256]{2,1,0:T(8,128)S(1)}, u32[]{:S(2)}, u32[]{:S(2)}) collective-permute-start(f32[18,8,256]{2,1,0:T(8,128)S(1)} %get-tuple-element.69), channel_id=1, source_target_pairs={{0,8},{8,0},{1,9},{9,1},{2,10},{10,2},{3,11},{11,3},{4,12},{12,4},... | collective-permute-start | bytes 442376 | tf_op jit(solution)/shard_map/ppermute | solution.py:510
  18.7 7.7 %collective-permute-start.5 = (f32[18,8,128]{2,1,0:T(8,128)S(1)}, f32[18,8,128]{2,1,0:T(8,128)S(1)}, u32[]{:S(2)}, u32[]{:S(2)}) collective-permute-start(f32[18,8,128]{2,1,0:T(8,128)S(1)} %get-tuple-element.66), channel_id=1, source_target_pairs={{0,4},{4,0},{1,5},{5,1},{2,6},{6,2},{3,7},{7,3},{8,12},{12,8},{9,1... | collective-permute-start | bytes 221192 | tf_op jit(solution)/shard_map/ppermute | solution.py:510
  18.8 15.2 %collective-permute-start.9 = (f32[18,8,256]{2,1,0:T(8,128)S(1)}, f32[18,8,256]{2,1,0:T(8,128)S(1)}, u32[]{:S(2)}, u32[]{:S(2)}) collective-permute-start(f32[18,8,256]{2,1,0:T(8,128)S(1)} %get-tuple-element.72), channel_id=1, source_target_pairs={{0,248},{8,16},{16,8},{24,32},{32,24},{40,48},{48,40},{56,64},{64,... | collective-permute-start | bytes 442376 | tf_op jit(solution)/shard_map/ppermute | solution.py:510
  19.2 4.1 %collective-permute-start.6 = (f32[9,8,128]{2,1,0:T(8,128)S(1)}, f32[9,8,128]{2,1,0:T(8,128)S(1)}, u32[]{:S(2)}, u32[]{:S(2)}) collective-permute-start(f32[9,8,128]{2,1,0:T(8,128)S(1)} %get-tuple-element.67), channel_id=1, source_target_pairs={{0,3},{1,0},{2,1},{3,2},{4,7},{5,4},{6,5},{7,6},{8,11},{9,8},{10,9... | collective-permute-start | bytes 110600 | tf_op jit(solution)/shard_map/ppermute | solution.py:510
  22.2 4.3 %collective-permute-start.7 = (f32[9,8,128]{2,1,0:T(8,128)S(1)}, f32[9,8,128]{2,1,0:T(8,128)S(1)}, u32[]{:S(2)}, u32[]{:S(2)}) collective-permute-start(f32[9,8,128]{2,1,0:T(8,128)S(1)} %get-tuple-element.68), channel_id=1, source_target_pairs={{0,1},{1,2},{2,3},{3,0},{4,5},{5,6},{6,7},{7,4},{8,9},{9,10},{10,1... | collective-permute-start | bytes 110600 | tf_op jit(solution)/shard_map/ppermute | solution.py:510
  27.1 11.8 %collective-permute-start.13 = (f32[18,8,256]{2,1,0:T(8,128)S(1)}, f32[18,8,256]{2,1,0:T(8,128)S(1)}, u32[]{:S(2)}, u32[]{:S(2)}) collective-permute-start(f32[18,8,256]{2,1,0:T(8,128)S(1)} %get-tuple-element.79), channel_id=1, source_target_pairs={{0,8},{8,0},{1,9},{9,1},{2,10},{10,2},{3,11},{11,3},{4,12},{12,4},... | collective-permute-start | bytes 442376 | tf_op jit(solution)/shard_map/ppermute | solution.py:510
  34.4 4.5 %collective-permute-start.10 = (f32[12,8,128]{2,1,0:T(8,128)S(1)}, f32[12,8,128]{2,1,0:T(8,128)S(1)}, u32[]{:S(2)}, u32[]{:S(2)}) collective-permute-start(f32[12,8,128]{2,1,0:T(8,128)S(1)} %get-tuple-element.76), channel_id=1, source_target_pairs={{0,4},{4,0},{1,5},{5,1},{2,6},{6,2},{3,7},{7,3},{8,12},{12,8},{9,1... | collective-permute-start | bytes 147464 | tf_op jit(solution)/shard_map/ppermute | solution.py:510
  35.0 8.6 %collective-permute-start.14 = (f32[12,8,256]{2,1,0:T(8,128)S(1)}, f32[12,8,256]{2,1,0:T(8,128)S(1)}, u32[]{:S(2)}, u32[]{:S(2)}) collective-permute-start(f32[12,8,256]{2,1,0:T(8,128)S(1)} %get-tuple-element.84), channel_id=1, source_target_pairs={{0,248},{8,16},{16,8},{24,32},{32,24},{40,48},{48,40},{56,64},{64,... | collective-permute-start | bytes 294920 | tf_op jit(solution)/shard_map/ppermute | solution.py:510
  35.0 3.0 %collective-permute-start.11 = (f32[6,8,128]{2,1,0:T(8,128)S(1)}, f32[6,8,128]{2,1,0:T(8,128)S(1)}, u32[]{:S(2)}, u32[]{:S(2)}) collective-permute-start(f32[6,8,128]{2,1,0:T(8,128)S(1)} %get-tuple-element.77), channel_id=1, source_target_pairs={{0,3},{1,0},{2,1},{3,2},{4,7},{5,4},{6,5},{7,6},{8,11},{9,8},{10,9... | collective-permute-start | bytes 73736 | tf_op jit(solution)/shard_map/ppermute | solution.py:510
  35.0 3.9 %collective-permute-start.12 = (f32[6,8,128]{2,1,0:T(8,128)S(1)}, f32[6,8,128]{2,1,0:T(8,128)S(1)}, u32[]{:S(2)}, u32[]{:S(2)}) collective-permute-start(f32[6,8,128]{2,1,0:T(8,128)S(1)} %get-tuple-element.78), channel_id=1, source_target_pairs={{0,1},{1,2},{2,3},{3,0},{4,5},{5,6},{6,7},{7,4},{8,9},{9,10},{10,1... | collective-permute-start | bytes 73736 | tf_op jit(solution)/shard_map/ppermute | solution.py:510
  39.4 10.0 %collective-permute-start.18 = (f32[18,8,256]{2,1,0:T(8,128)S(1)}, f32[18,8,256]{2,1,0:T(8,128)S(1)}, u32[]{:S(2)}, u32[]{:S(2)}) collective-permute-start(f32[18,8,256]{2,1,0:T(8,128)S(1)} %get-tuple-element.91), channel_id=1, source_target_pairs={{0,8},{8,0},{1,9},{9,1},{2,10},{10,2},{3,11},{11,3},{4,12},{12,4},... | collective-permute-start | bytes 442376 | tf_op jit(solution)/shard_map/ppermute | solution.py:510
  43.9 6.0 %collective-permute-start.19 = (f32[12,8,256]{2,1,0:T(8,128)S(1)}, f32[12,8,256]{2,1,0:T(8,128)S(1)}, u32[]{:S(2)}, u32[]{:S(2)}) collective-permute-start(f32[12,8,256]{2,1,0:T(8,128)S(1)} %get-tuple-element.96), channel_id=1, source_target_pairs={{0,248},{8,16},{16,8},{24,32},{32,24},{40,48},{48,40},{56,64},{64,... | collective-permute-start | bytes 294920 | tf_op jit(solution)/shard_map/ppermute | solution.py:510
  44.4 5.0 %collective-permute-start.15 = (f32[12,8,128]{2,1,0:T(8,128)S(1)}, f32[12,8,128]{2,1,0:T(8,128)S(1)}, u32[]{:S(2)}, u32[]{:S(2)}) collective-permute-start(f32[12,8,128]{2,1,0:T(8,128)S(1)} %get-tuple-element.88), channel_id=1, source_target_pairs={{0,4},{4,0},{1,5},{5,1},{2,6},{6,2},{3,7},{7,3},{8,12},{12,8},{9,1... | collective-permute-start | bytes 147464 | tf_op jit(solution)/shard_map/ppermute | solution.py:510
  45.5 2.7 %collective-permute-start.16 = (f32[6,8,128]{2,1,0:T(8,128)S(1)}, f32[6,8,128]{2,1,0:T(8,128)S(1)}, u32[]{:S(2)}, u32[]{:S(2)}) collective-permute-start(f32[6,8,128]{2,1,0:T(8,128)S(1)} %get-tuple-element.89), channel_id=1, source_target_pairs={{0,3},{1,0},{2,1},{3,2},{4,7},{5,4},{6,5},{7,6},{8,11},{9,8},{10,9... | collective-permute-start | bytes 73736 | tf_op jit(solution)/shard_map/ppermute | solution.py:510
  45.5 3.9 %collective-permute-start.17 = (f32[6,8,128]{2,1,0:T(8,128)S(1)}, f32[6,8,128]{2,1,0:T(8,128)S(1)}, u32[]{:S(2)}, u32[]{:S(2)}) collective-permute-start(f32[6,8,128]{2,1,0:T(8,128)S(1)} %get-tuple-element.90), channel_id=1, source_target_pairs={{0,1},{1,2},{2,3},{3,0},{4,5},{5,6},{6,7},{7,4},{8,9},{9,10},{10,1... | collective-permute-start | bytes 73736 | tf_op jit(solution)/shard_map/ppermute | solution.py:510

commit v3 on v2

--- a/solution.py
+++ b/solution.py
@@ -240,14 +240,14 @@
     send_rows(out, lowp, highp)
 
 
-def first_kernel(
-    links_hbm, g_hbm, links, g, tp, fp, zp, lowp, highp, upz0, upy0, upz1, upy1, scr, sems
-):
-    copies = []
-    for colour in (1, 0):
-        copies.append((g_hbm.at[colour], g.at[colour]))
-        for mu in (3, 2, 1, 0):
-            copies.append((links_hbm.at[colour, mu], links.at[colour, mu]))
+def first_kernel(links_hbm, g_hbm, tp, fp, zp, lowp, highp, upz, upy, scr, links, g, sems):
+    right = pl.ds(128, 128)
+    copies = [
+        (g_hbm.at[1], g),
+        (links_hbm.at[1, 3, :, 1], links.at[3, :, 1]),
+        (links_hbm.at[1, 2], links.at[2]),
+        (links_hbm.at[1, 1, :, :, :, right], links.at[1, :, :, :, right]),
+    ]
     copies = [pltpu.make_async_copy(a, b, sems.at[k]) for k, (a, b) in enumerate(copies)]
     for copy in copies:
         copy.start()
@@ -256,23 +256,30 @@
     for copy in copies[:2]:
         copy.wait()
     for h in range(2):
-        face = times(lambda c: g[1, c, far, :, half(h)], crossing(links.at[1], h, core == 0))
+        face = times(lambda c: g[c, far, :, half(h)], crossing(links, h, core == 0))
         for k, c in enumerate(ROWS):
             fp[k, :, half(h)] = face[c]
-        face = times(lambda c: g[1, c, near, :, half(h)], crossing(links.at[1], h, core == 1))
+        face = times(lambda c: g[c, near, :, half(h)], crossing(links, h, core == 1))
         for c in range(18):
             tp[c, :, half(h)] = face[c]
-    for copy in copies[2:4]:
+    for copy in copies[2:]:
         copy.wait()
-    pack_links(core, links.at[1], upz1, upy1)
-    pack_z(core, g.at[1], upz1, zp, scr)
-    pack_y(core, g.at[1], upy1, lowp, highp)
-    for copy in copies[4:]:
-        copy.wait()
-    pack_links(core, links.at[0], upz0, upy0)
-
-
-def local_kernel(colour, first, links, gp, w):
+    pack_links(core, links, upz, upy)
+    pack_z(core, g, upz, zp, scr)
+    pack_y(core, g, upy, lowp, highp)
+
+
+def local_kernel(step, links, gp, *refs):
+    refs = list(refs)
+    w = refs.pop(0)
+    colour = step.colour
+    if step.number == 0:
+        pack_links(lax.axis_index("tc"), links.at[0], *refs)
+    if step.last:
+        out, sem = refs
+        copy = pltpu.make_async_copy(gp, out.at[1 - colour], sem)
+        copy.start()
+    first = step.number == 0
     own, other = links.at[colour], links.at[1 - colour]
     if first:
         gp = gp.at[1 - colour]
@@ -304,8 +311,8 @@
 
             def ahead_x(c):
                 v = tile(c)
-                step = jnp.where(column == 31, pltpu.roll(v, 31, 1), pltpu.roll(v, 127, 1))
-                return jnp.where(stays, v, step)
+                moved = jnp.where(column == 31, pltpu.roll(v, 31, 1), pltpu.roll(v, 127, 1))
+                return jnp.where(stays, v, moved)
 
             acc = times_adjoint(acc, lambda c: own[0, c, s, :, half(h)], ahead_x)
 
@@ -324,8 +331,8 @@
             back = times(tile, lambda c: other[0, c, s, :, half(h)])
             shifted = []
             for v in back:
-                step = jnp.where(column == 0, pltpu.roll(v, 97, 1), pltpu.roll(v, 1, 1))
-                shifted.append(jnp.where(stays, step, v))
+                moved = jnp.where(column == 0, pltpu.roll(v, 97, 1), pltpu.roll(v, 1, 1))
+                shifted.append(jnp.where(stays, moved, v))
             acc = plus_adjoint(acc, shifted)
             back = times(tile, lambda c: other[2, c, s, :, half(h)])
             acc = plus_adjoint(acc, [jnp.where(row == 0, 0.0, pltpu.roll(v, 1, 0)) for v in back])
@@ -342,6 +349,8 @@
                 acc = plus_adjoint(acc, back)
             for c in range(18):
                 w[c, s, :, half(h)] = acc[c]
+    if step.last:
+        copy.wait()
 
 
 def near_kernel(step, links, g, w, upz, upy, zh, yu, yd, th, *refs):
@@ -421,7 +430,6 @@
     before = refs.pop(0) if step.mode == TURN else None
     near_sums = refs.pop(0) if step.colour == 1 else None
     line = refs.pop(0) if step.colour == 1 and step.number > 1 else None
-    g0 = refs.pop(0) if step.last else None
     upz = refs.pop(0) if step.sends == WHOLE else None
     upy = refs.pop(0) if step.sends == WHOLE else None
     qn = refs.pop(0) if step.sends == TURN else None
@@ -435,7 +443,6 @@
     core = lax.axis_index("tc")
     far, near = slices(core)
     total = None if sums is None else [near_sums[0], near_sums[1]]
-    to = out.at[1] if step.last else out
     for h in range(2):
         link = crossing(own, h, core == 0)
         part = behind(
@@ -450,7 +457,10 @@
         acc = plus_adjoint([wf[c, :, half(h)] for c in range(18)], part)
         new, mat, turn = relax([g[c, far, :, half(h)] for c in range(18)], acc)
         for c in range(18):
-            to[c, far, :, half(h)] = new[c]
+            if step.last:
+                out[c, :, half(h)] = new[c]
+            else:
+                out[c, far, :, half(h)] = new[c]
         if step.sends == WHOLE:
             face = times(lambda c: new[c], link)
             for c in range(18):
@@ -462,13 +472,9 @@
                 pack_rows(k, 1, qn[k, :, half(h)], h, zp)
         if sums is not None:
             total = [a + b for a, b in zip(total, measures(mat))]
-    for c in range(18):
-        to[c, near] = gn[c]
-    if step.last:
+    if not step.last:
         for c in range(18):
-            for s in range(2):
-                out[0, c, s] = g0[c, s]
-    else:
+            out[c, near] = gn[c]
         if step.sends == WHOLE:
             pack_z(core, out, upz, zp, refs.pop(0))
             pack_y(core, out, upy, lowp, highp)
@@ -485,23 +491,43 @@
         sums[...] = line
 
 
-def final_kernel(volume, parts, monitor):
-    total = jnp.sum(parts[...], axis=0)
+def final_kernel(volume, parts, gn, gf, begun, out, monitor, scr, sems):
+    copies = [
+        pltpu.make_async_copy(part, out.at[1, :, s], sems.at[k])
+        for k, (part, s) in enumerate(zip((gf, gn), slices(lax.axis_index("tc"))))
+    ]
+    for copy in copies:
+        copy.start()
+    total = parts[0]
+    for k in range(1, parts.shape[0]):
+        total = total + parts[k]
+    total = jnp.sum(total, axis=0, keepdims=True)
     both = jnp.concatenate([total, pltpu.roll(total, 128 - ITERS, 1)], axis=0)
     row = lax.broadcasted_iota(jnp.int32, (2, 128), 0)
     both = jnp.where(row == 0, 1.0 - both / (12.0 * volume), both / (volume / 2.0))
-    monitor[...] = both[:, :ITERS]
-
-
-def call(body, outs, scratch, args, flops, space=pltpu.VMEM):
+    scr[...] = both[:, :ITERS]
+    copies.append(pltpu.make_async_copy(scr, monitor, sems.at[2]))
+    copies[2].start()
+    for copy in copies:
+        copy.wait()
+
+
+def call(body, outs, scratch, args, flops, hbm=False, hbm_outs=(), aliases={}):
     return pl.pallas_call(
         body,
         out_shape=[jax.ShapeDtypeStruct(o, F32) for o in outs],
-        in_specs=[pl.BlockSpec(memory_space=space)] * len(args),
-        out_specs=[pl.BlockSpec(memory_space=pltpu.VMEM)] * len(outs),
+        in_specs=[
+            pl.BlockSpec(memory_space=pltpu.HBM if hbm or k in aliases else pltpu.VMEM)
+            for k in range(len(args))
+        ],
+        out_specs=[
+            pl.BlockSpec(memory_space=pltpu.HBM if k in hbm_outs else pltpu.VMEM)
+            for k in range(len(outs))
+        ],
         scratch_shapes=[s if not isinstance(s, tuple) else pltpu.VMEM(s, F32) for s in scratch],
         compiler_params=pltpu.CompilerParams(vmem_limit_bytes=24 * 2**20),
         cost_estimate=pl.CostEstimate(flops=flops, bytes_accessed=0, transcendentals=0),
+        input_output_aliases=aliases,
     )(*args)
 
 
@@ -544,19 +570,18 @@
     volume = 2 * transform.shape[2] * transform.shape[3] * transform.shape[4]
     for axis in AXES:
         volume *= lax.axis_size(axis)
-    links, start, tp, fp, zp, lowp, highp, *sides = call(
+    tp, fp, zp, lowp, highp, *side = call(
         first_kernel,
-        [lattice_links.shape, transform.shape, FACE, FACE_12, SIDE_12, ROW_12, ROW_12]
-        + [SIDE] * 4,
-        [SIDE, pltpu.SemaphoreType.DMA((10,))],
+        [FACE, FACE_12, SIDE_12, ROW_12, ROW_12, SIDE, SIDE],
+        [SIDE, (4,) + FIELD, FIELD, pltpu.SemaphoreType.DMA((4,))],
         [pltpu.with_memory_space_constraint(v, pltpu.HBM) for v in (lattice_links, transform)],
         10**7,
-        pltpu.HBM,
-    )
-    g = [start, start]
-    packed = [sides[:2], sides[2:]]
+        hbm=True,
+    )
+    links = lattice_links
+    g = [transform, transform]
+    packed = [None, side]
     kept_far, kept_side = [None, None], [None, None]
-    th = swap(tp, "tc", even_odd)
     line = None
     for step in map(Step, range(2 * ITERS)):
         colour = step.colour
@@ -564,13 +589,25 @@
         yu = swap(lowp, "gy", lambda i: i - 1)
         yd = swap(highp, "gy", lambda i: i + 1)
         zh = swap(zp, "gz", even_odd)
-        (w,) = call(
-            functools.partial(local_kernel, colour, step.number == 0),
-            [FIELD],
-            [],
+        th = swap(tp, "tc", even_odd)
+        outs, scratch = [FIELD], []
+        if step.number == 0:
+            outs += [SIDE, SIDE]
+        if step.last:
+            outs += [(2,) + FIELD]
+            scratch = [pltpu.SemaphoreType.DMA(())]
+        w, *rest = call(
+            functools.partial(local_kernel, step),
+            outs,
+            scratch,
             [links, g[1 - colour]],
             3 * 10**7,
+            hbm_outs=(1,) if step.last else (),
         )
+        if step.number == 0:
+            packed[0] = rest
+        if step.last:
+            (begun,) = rest
         outs = [FACE, FACE]
         outs += [SIDE, SIDE] if step.keeps else []
         outs += [] if step.last else [FACE]
@@ -582,15 +619,14 @@
         if step.keeps:
             kept_side[colour] = [rest.pop(0), rest.pop(0)]
         if not step.last:
-            th = swap(rest.pop(0), "tc", even_odd)
+            tp = rest.pop(0)
         args = [links, g[colour], gn, wf, fh]
         args += [kept_far[colour]] if step.mode == TURN else []
         args += [rest.pop()] if colour == 1 else []
         args += [line] if line is not None and colour == 1 else []
-        args += [g[0]] if step.last else []
         args += packed[colour] if step.sends == WHOLE else []
         args += [rest.pop()] if step.sends == TURN else []
-        outs = [(2,) + FIELD] if step.last else [FIELD]
+        outs = [FACE] if step.last else [FIELD]
         outs += [FACE] if step.keeps else []
         if not step.last:
             outs += SENT[step.sends]
@@ -613,8 +649,16 @@
     for axis in AXES:
         count *= lax.axis_size(axis)
     parts = jnp.broadcast_to(line[None], (count, 1, 128))
-    parts = lax.all_to_all(parts, AXES, 0, 0, tiled=True)
-    (monitor,) = call(functools.partial(final_kernel, volume), [(2, ITERS)], [], [parts], 10**3)
+    parts = lax.all_to_all(parts, AXES, 0, 0, tiled=True).reshape(count // 8, 8, 128)
+    out, monitor = call(
+        functools.partial(final_kernel, volume),
+        [(2,) + FIELD, (2, ITERS)],
+        [(2, ITERS), pltpu.SemaphoreType.DMA((3,))],
+        [parts, gn, out, begun],
+        10**3,
+        hbm_outs=(0, 1),
+        aliases={3: 0},
+    )
     return (out, monitor)
 
 

time: 73.7 us -> 72.6 us (0.985)
  Pallas kernels: 12.3 us -> 11 us
    pallas_call x14, Pallas kernels: 12.3 us -> 11 us  [call(): pl.pallas_call(body, out_shape=[jax.ShapeDtypeStruct(o, F32) for o in out...]
  transfers between devices with their start and end apart: 20 -> 20, of which waited for: 4 -> 4; matrix products, arithmetic and copies ran while one was open for 0% -> 0% of each run, Pallas kernels for 11% -> 12%
where the time goes in v3:
time: 72.6 us; the launch traced here: 72.5 us
  starting transfers between devices  33.3 us (46%)
  blocking collectives  21.5 us (30%)
  Pallas kernels  11 us (15%)
  waiting for transfers between devices  5.64 us (8%)
  between operations  0.95 us (1%)
    ppermute x20, starting transfers between devices, swap(): lax.ppermute(value, axis, [(i, partner(i) % count) for i in range(count)])  33.3 us
    all_to_all x1, blocking collectives, shards(): lax.all_to_all(parts, AXES, 0, 0, tiled=True).reshape(count // 8, 8, 128)  21.5 us
    pallas_call x14, Pallas kernels, call(): pl.pallas_call(body, out_shape=[jax.ShapeDtypeStruct(o, F32) for o in out...  11 us
    ppermute x20, waiting for transfers between devices, swap(): lax.ppermute(value, axis, [(i, partner(i) % count) for i in range(count)])  5.64 us
  transfers between devices with their start and end apart: 20, of which 4 were waited for; matrix products, arithmetic and copies ran while one was open for 0% of the time, Pallas kernels for 12%

profile of v3, /device:TPU:1, one launch (start us, length us, event | category | flops | bytes accessed | tf_op | source)
XLA Modules:
  0.0 72.5 jit_solution(5387059819468505355)
XLA Ops:
  0.6 1.6 %shard_map.42 = (f32[18,8,256]{2,1,0:T(8,128)S(1)}, f32[12,8,256]{2,1,0:T(8,128)S(1)}, f32[12,8,128]{2,1,0:T(8,128)S(1)}, f32[6,8,128]{2,1,0:T(8,128)S(1)}, f32[...) custom-call(f32[2,4,18,2,8,256]{5,4,3,2,1,0:T(8,128)} %links.23, f32[2,18,2,8,256]{4,3,2,1,0:T(8,128)} %g.7), custom_call_target="tpu_custom_call" | custom-call | flops 10000000 | tf_op jit(solution)/shard_map/pallas_call | solution.py:516
  2.3 3.3 %collective-permute-start.3 = (f32[18,8,256]{2,1,0:T(8,128)S(1)}, f32[18,8,256]{2,1,0:T(8,128)S(1)}, u32[]{:S(2)}, u32[]{:S(2)}) collective-permute-start(f32[18,8,256]{2,1,0:T(8,128)S(1)} %get-tuple-element.59), channel_id=1, source_target_pairs={{0,8},{8,0},{1,9},{9,1},{2,10},{10,2},{3,11},{11,3},{4,12},{12,4},... | collective-permute-start | bytes 442376 | tf_op jit(solution)/shard_map/ppermute | solution.py:536
  5.6 2.2 %collective-permute-start.1 = (f32[6,8,128]{2,1,0:T(8,128)S(1)}, f32[6,8,128]{2,1,0:T(8,128)S(1)}, u32[]{:S(2)}, u32[]{:S(2)}) collective-permute-start(f32[6,8,128]{2,1,0:T(8,128)S(1)} %get-tuple-element.57), channel_id=1, source_target_pairs={{0,3},{1,0},{2,1},{3,2},{4,7},{5,4},{6,5},{7,6},{8,11},{9,8},{10,9... | collective-permute-start | bytes 73736 | tf_op jit(solution)/shard_map/ppermute | solution.py:536
  7.8 0.0 collective-permute-start.2
  7.8 3.0 %collective-permute-start.4 = (f32[12,8,256]{2,1,0:T(8,128)S(1)}, f32[12,8,256]{2,1,0:T(8,128)S(1)}, u32[]{:S(2)}, u32[]{:S(2)}) collective-permute-start(f32[12,8,256]{2,1,0:T(8,128)S(1)} %get-tuple-element.62), channel_id=1, source_target_pairs={{0,248},{8,16},{16,8},{24,32},{32,24},{40,48},{48,40},{56,64},{64,... | collective-permute-start | bytes 294920 | tf_op jit(solution)/shard_map/ppermute | solution.py:536
  10.8 1.2 %shard_map.41 = (f32[18,2,8,256]{3,2,1,0:T(8,128)S(1)}, f32[18,8,128]{2,1,0:T(8,128)S(1)}, f32[18,8,128]{2,1,0:T(8,128)S(1)}) custom-call(f32[2,4,18,2,8,256]{5,4,3,2,1,0:T(8,128)S(1)} %copy-done, f32[2,18,2,8,256]{4,3,2,1,0:T(8,128)S(1)} %copy-done.1), custom_call_target="tpu_custom_call" | custom-call | flops 30000000 | tf_op jit(solution)/shard_map/pallas_call | solution.py:516
  12.0 0.0 collective-permute-done.1.yu
  12.1 0.0 collective-permute-done.3.th
  12.1 0.6 shard_map.43
  12.6 5.2 %collective-permute-start.8 = (f32[18,8,256]{2,1,0:T(8,128)S(1)}, f32[18,8,256]{2,1,0:T(8,128)S(1)}, u32[]{:S(2)}, u32[]{:S(2)}) collective-permute-start(f32[18,8,256]{2,1,0:T(8,128)S(1)} %get-tuple-element.69), channel_id=1, source_target_pairs={{0,8},{8,0},{1,9},{9,1},{2,10},{10,2},{3,11},{11,3},{4,12},{12,4},... | collective-permute-start | bytes 442376 | tf_op jit(solution)/shard_map/ppermute | solution.py:536
  17.9 0.6 shard_map.44
  18.4 0.1 collective-permute-start.5
  18.5 0.3 collective-permute-start.9
  18.9 3.0 %collective-permute-start.6 = (f32[9,8,128]{2,1,0:T(8,128)S(1)}, f32[9,8,128]{2,1,0:T(8,128)S(1)}, u32[]{:S(2)}, u32[]{:S(2)}) collective-permute-start(f32[9,8,128]{2,1,0:T(8,128)S(1)} %get-tuple-element.67), channel_id=1, source_target_pairs={{0,3},{1,0},{2,1},{3,2},{4,7},{5,4},{6,5},{7,6},{8,11},{9,8},{10,9... | collective-permute-start | bytes 110600 | tf_op jit(solution)/shard_map/ppermute | solution.py:536
  21.8 0.0 collective-permute-start.7
  21.8 1.2 %shard_map.45.w = f32[18,2,8,256]{3,2,1,0:T(8,128)S(1)} custom-call(f32[2,4,18,2,8,256]{5,4,3,2,1,0:T(8,128)S(1)} %copy-done, f32[18,2,8,256]{3,2,1,0:T(8,128)S(1)} %get-tuple-element.63.gp.g), custom_call_target="tpu_custom_call" | custom-call | flops 30000000 | tf_op jit(solution)/shard_map/pallas_call | solution.py:516
  23.0 0.0 collective-permute-done.6.yu
  23.0 3.1 %collective-permute-done.7.yd = f32[9,8,128]{2,1,0:T(8,128)S(1)} collective-permute-done((f32[9,8,128]{2,1,0:T(8,128)S(1)}, f32[9,8,128]{2,1,0:T(8,128)S(1)}, u32[]{:S(2)}, u32[]{:S(2)}) %collective-permute-start.7) | collective-permute-done | bytes 36896 | tf_op jit(solution)/shard_map/ppermute | solution.py:536
  26.1 0.0 collective-permute-done.5.zh
  26.1 0.0 collective-permute-done.8.th
  26.1 0.6 shard_map.46
  26.8 6.9 %collective-permute-start.13 = (f32[18,8,256]{2,1,0:T(8,128)S(1)}, f32[18,8,256]{2,1,0:T(8,128)S(1)}, u32[]{:S(2)}, u32[]{:S(2)}) collective-permute-start(f32[18,8,256]{2,1,0:T(8,128)S(1)} %get-tuple-element.79), channel_id=1, source_target_pairs={{0,8},{8,0},{1,9},{9,1},{2,10},{10,2},{3,11},{11,3},{4,12},{12,4},... | collective-permute-start | bytes 442376 | tf_op jit(solution)/shard_map/ppermute | solution.py:536
  33.7 0.4 shard_map.47
  34.1 0.6 collective-permute-start.10
  34.7 0.0 collective-permute-start.14
  34.7 0.0 collective-permute-start.11
  34.7 1.5 %collective-permute-start.12 = (f32[6,8,128]{2,1,0:T(8,128)S(1)}, f32[6,8,128]{2,1,0:T(8,128)S(1)}, u32[]{:S(2)}, u32[]{:S(2)}) collective-permute-start(f32[6,8,128]{2,1,0:T(8,128)S(1)} %get-tuple-element.78), channel_id=1, source_target_pairs={{0,1},{1,2},{2,3},{3,0},{4,5},{5,6},{6,7},{7,4},{8,9},{9,10},{10,1... | collective-permute-start | bytes 73736 | tf_op jit(solution)/shard_map/ppermute | solution.py:536
  36.1 1.2 %shard_map.48.w = f32[18,2,8,256]{3,2,1,0:T(8,128)S(1)} custom-call(f32[2,4,18,2,8,256]{5,4,3,2,1,0:T(8,128)S(1)} %copy-done, f32[18,2,8,256]{3,2,1,0:T(8,128)S(1)} %get-tuple-element.75.gp.g), custom_call_target="tpu_custom_call" | custom-call | flops 30000000 | tf_op jit(solution)/shard_map/pallas_call | solution.py:516
  37.3 0.3 collective-permute-done.11.yu
  37.6 0.9 %collective-permute-done.12.yd = f32[6,8,128]{2,1,0:T(8,128)S(1)} collective-permute-done((f32[6,8,128]{2,1,0:T(8,128)S(1)}, f32[6,8,128]{2,1,0:T(8,128)S(1)}, u32[]{:S(2)}, u32[]{:S(2)}) %collective-permute-start.12) | collective-permute-done | bytes 24608 | tf_op jit(solution)/shard_map/ppermute | solution.py:536
  38.5 0.0 collective-permute-done.10.zh
  38.6 0.0 collective-permute-done.13.th
  38.6 0.5 shard_map.49
  39.1 4.1 %collective-permute-start.18 = (f32[18,8,256]{2,1,0:T(8,128)S(1)}, f32[18,8,256]{2,1,0:T(8,128)S(1)}, u32[]{:S(2)}, u32[]{:S(2)}) collective-permute-start(f32[18,8,256]{2,1,0:T(8,128)S(1)} %get-tuple-element.92), channel_id=1, source_target_pairs={{0,8},{8,0},{1,9},{9,1},{2,10},{10,2},{3,11},{11,3},{4,12},{12,4},... | collective-permute-start | bytes 442376 | tf_op jit(solution)/shard_map/ppermute | solution.py:536
  43.2 0.0 collective-permute-done.14.fh
  43.2 0.4 shard_map.50
  43.6 0.4 collective-permute-start.19
  44.1 1.2 %collective-permute-start.15 = (f32[12,8,128]{2,1,0:T(8,128)S(1)}, f32[12,8,128]{2,1,0:T(8,128)S(1)}, u32[]{:S(2)}, u32[]{:S(2)}) collective-permute-start(f32[12,8,128]{2,1,0:T(8,128)S(1)} %get-tuple-element.89), channel_id=1, source_target_pairs={{0,4},{4,0},{1,5},{5,1},{2,6},{6,2},{3,7},{7,3},{8,12},{12,8},{9,1... | collective-permute-start | bytes 147464 | tf_op jit(solution)/shard_map/ppermute | solution.py:536
  45.2 1.5 %collective-permute-start.17 = (f32[6,8,128]{2,1,0:T(8,128)S(1)}, f32[6,8,128]{2,1,0:T(8,128)S(1)}, u32[]{:S(2)}, u32[]{:S(2)}) collective-permute-start(f32[6,8,128]{2,1,0:T(8,128)S(1)} %get-tuple-element.91), channel_id=1, source_target_pairs={{0,1},{1,2},{2,3},{3,0},{4,5},{5,6},{6,7},{7,4},{8,9},{9,10},{10,1... | collective-permute-start | bytes 73736 | tf_op jit(solution)/shard_map/ppermute | solution.py:536
  46.7 1.2 %shard_map.51 = (f32[18,2,8,256]{3,2,1,0:T(8,128)S(1)}, f32[2,18,2,8,256]{4,3,2,1,0:T(8,128)}) custom-call(f32[2,4,18,2,8,256]{5,4,3,2,1,0:T(8,128)S(1)} %copy-done, f32[18,2,8,256]{3,2,1,0:T(8,128)S(1)} %get-tuple-element.87.gp), custom_call_target="tpu_custom_call" | custom-call | flops 30000000 | tf_op jit(solution)/shard_map/pallas_call | solution.py:516
  47.9 0.0 collective-permute-done.16.yu
  47.9 1.2 %collective-permute-done.17.yd = f32[6,8,128]{2,1,0:T(8,128)S(1)} collective-permute-done((f32[6,8,128]{2,1,0:T(8,128)S(1)}, f32[6,8,128]{2,1,0:T(8,128)S(1)}, u32[]{:S(2)}, u32[]{:S(2)}) %collective-permute-start.17) | collective-permute-done | bytes 24608 | tf_op jit(solution)/shard_map/ppermute | solution.py:536
  49.1 0.5 shard_map.52
  49.6 0.0 collective-permute-done.19.fh
  49.7 0.3 shard_map.53
  50.0 0.1 broadcast_in_dim.9
  50.1 21.5 %all_to_all.5 = f32[256,1,128]{2,1,0:T(1,128)S(1)} all-to-all(f32[256,1,128]{2,1,0:T(1,128)S(1)} %broadcast_in_dim.9), channel_id=1, replica_groups=mesh['tz'=8,'tx'=2,'tc'=2,'gz'=2,'gy'=4] {'tz','tx','tc','gz','gy'}, dimensions={0} | all-to-all | bytes 262144 | tf_op jit(solution)/shard_map/all_to_all | solution.py:652
  71.6 0.7 %shard_map.54 = (f32[2,18,2,8,256]{4,3,2,1,0:T(8,128)}, f32[2,2]{1,0:T(2,128)}) custom-call(f32[32,8,128]{2,1,0:T(8,128)S(1)} %bitcast.2, f32[18,8,256]{2,1,0:T(8,128)S(1)} %get-tuple-element.95.gn, f32[18,8,256]{2,1,0:T(8,128)S(1)} %get-tuple-element.102.gf, f32[2,18,2,8,256]{4,3,2,1,0:T(8,128)} %get-tuple-element.103.begun), custom_call_target="tpu_custom_call", output_to_operand_aliasing={{0}: (3, {})} | custom-call | flops 1000 | tf_op jit(solution)/shard_map/pallas_call | solution.py:516
  (12 shorter events, 0.0 us)
Async XLA Ops:
  0.6 10.2 %copy-start = (f32[2,4,18,2,8,256]{5,4,3,2,1,0:T(8,128)S(1)}, f32[2,4,18,2,8,256]{5,4,3,2,1,0:T(8,128)}, u32[]{:S(2)}) copy-start(f32[2,4,18,2,8,256]{5,4,3,2,1,0:T(8,128)} %links.23) | copy-start | bytes 7077892
  0.6 10.2 %copy-start.1 = (f32[2,18,2,8,256]{4,3,2,1,0:T(8,128)S(1)}, f32[2,18,2,8,256]{4,3,2,1,0:T(8,128)}, u32[]{:S(2)}) copy-start(f32[2,18,2,8,256]{4,3,2,1,0:T(8,128)} %g.7) | copy-start | bytes 1769476
  2.3 9.8 %collective-permute-start.3 = (f32[18,8,256]{2,1,0:T(8,128)S(1)}, f32[18,8,256]{2,1,0:T(8,128)S(1)}, u32[]{:S(2)}, u32[]{:S(2)}) collective-permute-start(f32[18,8,256]{2,1,0:T(8,128)S(1)} %get-tuple-element.59), channel_id=1, source_target_pairs={{0,8},{8,0},{1,9},{9,1},{2,10},{10,2},{3,11},{11,3},{4,12},{12,4},... | collective-permute-start | bytes 442376 | tf_op jit(solution)/shard_map/ppermute | solution.py:536
  5.6 6.5 %collective-permute-start = (f32[12,8,128]{2,1,0:T(8,128)S(1)}, f32[12,8,128]{2,1,0:T(8,128)S(1)}, u32[]{:S(2)}, u32[]{:S(2)}) collective-permute-start(f32[12,8,128]{2,1,0:T(8,128)S(1)} %get-tuple-element.56), channel_id=1, source_target_pairs={{0,4},{4,0},{1,5},{5,1},{2,6},{6,2},{3,7},{7,3},{8,12},{12,8},{9,1... | collective-permute-start | bytes 147464 | tf_op jit(solution)/shard_map/ppermute | solution.py:536
  5.6 6.5 %collective-permute-start.1 = (f32[6,8,128]{2,1,0:T(8,128)S(1)}, f32[6,8,128]{2,1,0:T(8,128)S(1)}, u32[]{:S(2)}, u32[]{:S(2)}) collective-permute-start(f32[6,8,128]{2,1,0:T(8,128)S(1)} %get-tuple-element.57), channel_id=1, source_target_pairs={{0,3},{1,0},{2,1},{3,2},{4,7},{5,4},{6,5},{7,6},{8,11},{9,8},{10,9... | collective-permute-start | bytes 73736 | tf_op jit(solution)/shard_map/ppermute | solution.py:536
  7.8 4.2 %collective-permute-start.2 = (f32[6,8,128]{2,1,0:T(8,128)S(1)}, f32[6,8,128]{2,1,0:T(8,128)S(1)}, u32[]{:S(2)}, u32[]{:S(2)}) collective-permute-start(f32[6,8,128]{2,1,0:T(8,128)S(1)} %get-tuple-element.58), channel_id=1, source_target_pairs={{0,1},{1,2},{2,3},{3,0},{4,5},{5,6},{6,7},{7,4},{8,9},{9,10},{10,1... | collective-permute-start | bytes 73736 | tf_op jit(solution)/shard_map/ppermute | solution.py:536
  7.8 10.1 %collective-permute-start.4 = (f32[12,8,256]{2,1,0:T(8,128)S(1)}, f32[12,8,256]{2,1,0:T(8,128)S(1)}, u32[]{:S(2)}, u32[]{:S(2)}) collective-permute-start(f32[12,8,256]{2,1,0:T(8,128)S(1)} %get-tuple-element.62), channel_id=1, source_target_pairs={{0,248},{8,16},{16,8},{24,32},{32,24},{40,48},{48,40},{56,64},{64,... | collective-permute-start | bytes 294920 | tf_op jit(solution)/shard_map/ppermute | solution.py:536
  12.6 13.5 %collective-permute-start.8 = (f32[18,8,256]{2,1,0:T(8,128)S(1)}, f32[18,8,256]{2,1,0:T(8,128)S(1)}, u32[]{:S(2)}, u32[]{:S(2)}) collective-permute-start(f32[18,8,256]{2,1,0:T(8,128)S(1)} %get-tuple-element.69), channel_id=1, source_target_pairs={{0,8},{8,0},{1,9},{9,1},{2,10},{10,2},{3,11},{11,3},{4,12},{12,4},... | collective-permute-start | bytes 442376 | tf_op jit(solution)/shard_map/ppermute | solution.py:536
  18.4 7.7 %collective-permute-start.5 = (f32[18,8,128]{2,1,0:T(8,128)S(1)}, f32[18,8,128]{2,1,0:T(8,128)S(1)}, u32[]{:S(2)}, u32[]{:S(2)}) collective-permute-start(f32[18,8,128]{2,1,0:T(8,128)S(1)} %get-tuple-element.66), channel_id=1, source_target_pairs={{0,4},{4,0},{1,5},{5,1},{2,6},{6,2},{3,7},{7,3},{8,12},{12,8},{9,1... | collective-permute-start | bytes 221192 | tf_op jit(solution)/shard_map/ppermute | solution.py:536
  18.5 15.1 %collective-permute-start.9 = (f32[18,8,256]{2,1,0:T(8,128)S(1)}, f32[18,8,256]{2,1,0:T(8,128)S(1)}, u32[]{:S(2)}, u32[]{:S(2)}) collective-permute-start(f32[18,8,256]{2,1,0:T(8,128)S(1)} %get-tuple-element.72), channel_id=1, source_target_pairs={{0,248},{8,16},{16,8},{24,32},{32,24},{40,48},{48,40},{56,64},{64,... | collective-permute-start | bytes 442376 | tf_op jit(solution)/shard_map/ppermute | solution.py:536
  18.9 4.1 %collective-permute-start.6 = (f32[9,8,128]{2,1,0:T(8,128)S(1)}, f32[9,8,128]{2,1,0:T(8,128)S(1)}, u32[]{:S(2)}, u32[]{:S(2)}) collective-permute-start(f32[9,8,128]{2,1,0:T(8,128)S(1)} %get-tuple-element.67), channel_id=1, source_target_pairs={{0,3},{1,0},{2,1},{3,2},{4,7},{5,4},{6,5},{7,6},{8,11},{9,8},{10,9... | collective-permute-start | bytes 110600 | tf_op jit(solution)/shard_map/ppermute | solution.py:536
  21.8 4.3 %collective-permute-start.7 = (f32[9,8,128]{2,1,0:T(8,128)S(1)}, f32[9,8,128]{2,1,0:T(8,128)S(1)}, u32[]{:S(2)}, u32[]{:S(2)}) collective-permute-start(f32[9,8,128]{2,1,0:T(8,128)S(1)} %get-tuple-element.68), channel_id=1, source_target_pairs={{0,1},{1,2},{2,3},{3,0},{4,5},{5,6},{6,7},{7,4},{8,9},{9,10},{10,1... | collective-permute-start | bytes 110600 | tf_op jit(solution)/shard_map/ppermute | solution.py:536
  26.8 11.8 %collective-permute-start.13 = (f32[18,8,256]{2,1,0:T(8,128)S(1)}, f32[18,8,256]{2,1,0:T(8,128)S(1)}, u32[]{:S(2)}, u32[]{:S(2)}) collective-permute-start(f32[18,8,256]{2,1,0:T(8,128)S(1)} %get-tuple-element.79), channel_id=1, source_target_pairs={{0,8},{8,0},{1,9},{9,1},{2,10},{10,2},{3,11},{11,3},{4,12},{12,4},... | collective-permute-start | bytes 442376 | tf_op jit(solution)/shard_map/ppermute | solution.py:536
  34.1 4.5 %collective-permute-start.10 = (f32[12,8,128]{2,1,0:T(8,128)S(1)}, f32[12,8,128]{2,1,0:T(8,128)S(1)}, u32[]{:S(2)}, u32[]{:S(2)}) collective-permute-start(f32[12,8,128]{2,1,0:T(8,128)S(1)} %get-tuple-element.76), channel_id=1, source_target_pairs={{0,4},{4,0},{1,5},{5,1},{2,6},{6,2},{3,7},{7,3},{8,12},{12,8},{9,1... | collective-permute-start | bytes 147464 | tf_op jit(solution)/shard_map/ppermute | solution.py:536
  34.7 8.6 %collective-permute-start.14 = (f32[12,8,256]{2,1,0:T(8,128)S(1)}, f32[12,8,256]{2,1,0:T(8,128)S(1)}, u32[]{:S(2)}, u32[]{:S(2)}) collective-permute-start(f32[12,8,256]{2,1,0:T(8,128)S(1)} %get-tuple-element.84), channel_id=1, source_target_pairs={{0,248},{8,16},{16,8},{24,32},{32,24},{40,48},{48,40},{56,64},{64,... | collective-permute-start | bytes 294920 | tf_op jit(solution)/shard_map/ppermute | solution.py:536
  34.7 3.0 %collective-permute-start.11 = (f32[6,8,128]{2,1,0:T(8,128)S(1)}, f32[6,8,128]{2,1,0:T(8,128)S(1)}, u32[]{:S(2)}, u32[]{:S(2)}) collective-permute-start(f32[6,8,128]{2,1,0:T(8,128)S(1)} %get-tuple-element.77), channel_id=1, source_target_pairs={{0,3},{1,0},{2,1},{3,2},{4,7},{5,4},{6,5},{7,6},{8,11},{9,8},{10,9... | collective-permute-start | bytes 73736 | tf_op jit(solution)/shard_map/ppermute | solution.py:536
  34.7 3.9 %collective-permute-start.12 = (f32[6,8,128]{2,1,0:T(8,128)S(1)}, f32[6,8,128]{2,1,0:T(8,128)S(1)}, u32[]{:S(2)}, u32[]{:S(2)}) collective-permute-start(f32[6,8,128]{2,1,0:T(8,128)S(1)} %get-tuple-element.78), channel_id=1, source_target_pairs={{0,1},{1,2},{2,3},{3,0},{4,5},{5,6},{6,7},{7,4},{8,9},{9,10},{10,1... | collective-permute-start | bytes 73736 | tf_op jit(solution)/shard_map/ppermute | solution.py:536
  39.1 10.0 %collective-permute-start.18 = (f32[18,8,256]{2,1,0:T(8,128)S(1)}, f32[18,8,256]{2,1,0:T(8,128)S(1)}, u32[]{:S(2)}, u32[]{:S(2)}) collective-permute-start(f32[18,8,256]{2,1,0:T(8,128)S(1)} %get-tuple-element.92), channel_id=1, source_target_pairs={{0,8},{8,0},{1,9},{9,1},{2,10},{10,2},{3,11},{11,3},{4,12},{12,4},... | collective-permute-start | bytes 442376 | tf_op jit(solution)/shard_map/ppermute | solution.py:536
  43.6 6.0 %collective-permute-start.19 = (f32[12,8,256]{2,1,0:T(8,128)S(1)}, f32[12,8,256]{2,1,0:T(8,128)S(1)}, u32[]{:S(2)}, u32[]{:S(2)}) collective-permute-start(f32[12,8,256]{2,1,0:T(8,128)S(1)} %get-tuple-element.97), channel_id=1, source_target_pairs={{0,248},{8,16},{16,8},{24,32},{32,24},{40,48},{48,40},{56,64},{64,... | collective-permute-start | bytes 294920 | tf_op jit(solution)/shard_map/ppermute | solution.py:536
  44.1 5.0 %collective-permute-start.15 = (f32[12,8,128]{2,1,0:T(8,128)S(1)}, f32[12,8,128]{2,1,0:T(8,128)S(1)}, u32[]{:S(2)}, u32[]{:S(2)}) collective-permute-start(f32[12,8,128]{2,1,0:T(8,128)S(1)} %get-tuple-element.89), channel_id=1, source_target_pairs={{0,4},{4,0},{1,5},{5,1},{2,6},{6,2},{3,7},{7,3},{8,12},{12,8},{9,1... | collective-permute-start | bytes 147464 | tf_op jit(solution)/shard_map/ppermute | solution.py:536
  45.2 2.7 %collective-permute-start.16 = (f32[6,8,128]{2,1,0:T(8,128)S(1)}, f32[6,8,128]{2,1,0:T(8,128)S(1)}, u32[]{:S(2)}, u32[]{:S(2)}) collective-permute-start(f32[6,8,128]{2,1,0:T(8,128)S(1)} %get-tuple-element.90), channel_id=1, source_target_pairs={{0,3},{1,0},{2,1},{3,2},{4,7},{5,4},{6,5},{7,6},{8,11},{9,8},{10,9... | collective-permute-start | bytes 73736 | tf_op jit(solution)/shard_map/ppermute | solution.py:536
  45.2 3.9 %collective-permute-start.17 = (f32[6,8,128]{2,1,0:T(8,128)S(1)}, f32[6,8,128]{2,1,0:T(8,128)S(1)}, u32[]{:S(2)}, u32[]{:S(2)}) collective-permute-start(f32[6,8,128]{2,1,0:T(8,128)S(1)} %get-tuple-element.91), channel_id=1, source_target_pairs={{0,1},{1,2},{2,3},{3,0},{4,5},{5,6},{6,7},{7,4},{8,9},{9,10},{10,1... | collective-permute-start | bytes 73736 | tf_op jit(solution)/shard_map/ppermute | solution.py:536

commit v4 on v3

--- a/solution.py
+++ b/solution.py
@@ -1,4 +1,5 @@
 import functools
+import types
 
 import jax
 import jax.numpy as jnp
@@ -136,7 +137,11 @@
         return turned([before[c] for c in range(18)], [sent(c) for c in range(12)])
     if mode == TWO_ROWS:
         full = third_row([sent(k) for k in range(12)])
+        if link is None:
+            return full
         return times_adjoint([None] * 18, lambda c: full[c], link)
+    if link is None:
+        return [sent(c) for c in range(18)]
     return times_adjoint([None] * 18, sent, link)
 
 
@@ -222,12 +227,9 @@
         highp[k] = jnp.where(lane < 64, pltpu.roll(a, 64, 1), b)
 
 
-def received_rows(c, yu, yd):
-    _, lane = iotas()
-    u, d = yu[c // 2], yd[c // 2]
-    if c % 2:
-        return jnp.where(lane < 64, pltpu.roll(u, 64, 1), d)
-    return jnp.where(lane < 64, u, pltpu.roll(d, 64, 1))
+def received(message, c):
+    tile = message[c // 2]
+    return pltpu.roll(tile, 64, 1) if c % 2 else tile
 
 
 def pack_y(core, g, upy, lowp, highp):
@@ -353,142 +355,125 @@
         copy.wait()
 
 
-def near_kernel(step, links, g, w, upz, upy, zh, yu, yd, th, *refs):
-    refs = list(refs)
-    before = [refs.pop(0), refs.pop(0)] if step.mode == TURN else [None, None]
-    gn, wf = refs.pop(0), refs.pop(0)
-    kept = [refs.pop(0), refs.pop(0)] if step.keeps else [None, None]
-    tp = None if step.last else refs.pop(0)
-    qn = refs.pop(0) if step.sends == TURN else None
-    sums = refs.pop(0) if step.colour == 1 else None
-    z_scr, y_scr = refs
-    own = links.at[step.colour]
-    if step.first:
-        g = g.at[step.colour]
+def half_kernel(step, h, r):
+    own = r.links.at[step.colour]
+    g = r.g.at[step.colour] if step.first else r.g
     core = lax.axis_index("tc")
     far, near = slices(core)
     row, lane = iotas()
-    part = behind(
-        step.mode, lambda c: zh[c], lambda c: pltpu.roll(upz[c], 4, 0), before[0]
+    if h == 0:
+        part = behind(
+            step.mode,
+            lambda c: r.zh[c],
+            lambda c: pltpu.roll(r.upz[c], 4, 0),
+            r.z_before if step.mode == TURN else None,
+        )
+        for c in range(18):
+            r.z_side[c] = part[c]
+        link = None
+        edge, shift = lane < 32, 0
+    else:
+        link = None if step.mode == TURN else (lambda c: pltpu.roll(r.upy[c], 64, 1))
+        edge, shift = lane >= 96, 96
+    y_side = behind(
+        step.mode,
+        lambda c: received(r.y, c),
+        link,
+        r.y_before if step.mode == TURN else None,
     )
-    for c in range(18):
-        z_scr[c] = part[c]
-        if kept[0] is not None:
-            kept[0][c] = part[c]
-    part = behind(
-        step.mode,
-        lambda c: received_rows(c, yu, yd),
-        lambda c: pltpu.roll(upy[c], 64, 1),
-        before[1],
-    )
-    for c in range(18):
-        v = part[c]
-        if kept[1] is not None:
-            kept[1][c] = v
-        for k in range(2):
-            y_scr[c, k, :, half(0)] = jnp.where(lane < 32, pltpu.roll(v, 64 - 32 * k, 1), 0.0)
-            y_scr[c, k, :, half(1)] = jnp.where(lane < 96, 0.0, pltpu.roll(v, 96 - 32 * k, 1))
-
-    def with_sides(k, s, h):
+    if step.keeps:
+        for c in range(18):
+            r.y_kept[c] = y_side[c]
+
+    def with_sides(k, s):
         side = []
         for c in range(18):
-            r = 2 * k + h
-            up = jnp.broadcast_to(z_scr[c, r : r + 1, :], (8, 128))
-            down = jnp.broadcast_to(z_scr[c, 4 + r : 5 + r, :], (8, 128))
-            edge = jnp.where(row == 7, up, jnp.where(row == 0, down, 0.0))
-            side.append(edge + y_scr[c, k, :, half(h)])
-        return plus_adjoint([w[c, s, :, half(h)] for c in range(18)], side)
+            n = 2 * k + h
+            up = jnp.broadcast_to(r.z_side[c, n : n + 1, :], (8, 128))
+            down = jnp.broadcast_to(r.z_side[c, 4 + n : 5 + n, :], (8, 128))
+            across = y_side[c]
+            if (shift - 32 * k) % 128:
+                across = pltpu.roll(across, (shift - 32 * k) % 128, 1)
+            across = jnp.where(edge, across, 0.0)
+            side.append(jnp.where(row == 7, up, jnp.where(row == 0, down, 0.0)) + across)
+        return plus_adjoint([r.w[c, s, :, half(h)] for c in range(18)], side)
 
     total = None
-    for h in range(2):
-        acc = with_sides(0, far, h)
+    for k, s in ((1, near), (0, far)):
+        acc = with_sides(k, s)
+        if k == 1:
+            link = crossing(own, h, core == 1)
+            acc = times_adjoint(acc, link, lambda c: r.th[c, :, half(h)])
+        else:
+            link = crossing(own, h, core == 0)
+            part = behind(
+                step.mode,
+                lambda c: r.fh[c, :, half(h)],
+                link,
+                r.f_before if step.mode == TURN else None,
+            )
+            if step.keeps:
+                for c in range(18):
+                    r.f_kept[c] = part[c]
+            acc = plus_adjoint(acc, part)
+        new, mat, turn = relax([g[c, s, :, half(h)] for c in range(18)], acc)
+        to = (r.new_f, r.new_n)[k]
         for c in range(18):
-            wf[c, :, half(h)] = acc[c]
-        link = crossing(own, h, core == 1)
-        acc = with_sides(1, near, h)
-        acc = times_adjoint(acc, link, lambda c: th[c, :, half(h)])
-        new, mat, turn = relax([g[c, near, :, half(h)] for c in range(18)], acc)
-        for c in range(18):
-            gn[c, :, half(h)] = new[c]
-        if tp is not None:
+            to[c] = new[c]
+        if not step.last and (k == 1 or step.sends == WHOLE):
             face = times(lambda c: new[c], link)
+            to = r.face_n if k == 1 else r.face_f
             for c in range(18):
-                tp[c, :, half(h)] = face[c]
-        if qn is not None:
-            for k in range(12):
-                qn[k, :, half(h)] = turn[k]
-        if sums is not None:
+                to[c] = face[c]
+        if step.sends == TURN:
+            to = (r.turn_f, r.turn_n)[k]
+            for c in range(12):
+                to[c] = turn[c]
+        if step.colour == 1:
             now = measures(mat)
             total = now if total is None else [a + b for a, b in zip(total, now)]
-    if sums is not None:
-        sums[0] = total[0]
-        sums[1] = total[1]
-
-
-def far_kernel(step, links, g, gn, wf, fh, *refs):
-    refs = list(refs)
-    before = refs.pop(0) if step.mode == TURN else None
-    near_sums = refs.pop(0) if step.colour == 1 else None
-    line = refs.pop(0) if step.colour == 1 and step.number > 1 else None
-    upz = refs.pop(0) if step.sends == WHOLE else None
-    upy = refs.pop(0) if step.sends == WHOLE else None
-    qn = refs.pop(0) if step.sends == TURN else None
-    out = refs.pop(0)
-    kept = refs.pop(0) if step.keeps else None
-    fp, zp, lowp, highp = [None] * 4 if step.last else [refs.pop(0) for _ in range(4)]
-    sums = refs.pop(0) if step.colour == 1 else None
-    own = links.at[step.colour]
-    if step.first:
-        g = g.at[step.colour]
-    core = lax.axis_index("tc")
-    far, near = slices(core)
-    total = None if sums is None else [near_sums[0], near_sums[1]]
-    for h in range(2):
-        link = crossing(own, h, core == 0)
-        part = behind(
-            step.mode,
-            lambda c: fh[c, :, half(h)],
-            link,
-            None if before is None else [before[c, :, half(h)] for c in range(18)],
-        )
-        if kept is not None:
-            for c in range(18):
-                kept[c, :, half(h)] = part[c]
-        acc = plus_adjoint([wf[c, :, half(h)] for c in range(18)], part)
-        new, mat, turn = relax([g[c, far, :, half(h)] for c in range(18)], acc)
-        for c in range(18):
-            if step.last:
-                out[c, :, half(h)] = new[c]
-            else:
-                out[c, far, :, half(h)] = new[c]
-        if step.sends == WHOLE:
-            face = times(lambda c: new[c], link)
-            for c in range(18):
-                fp[c, :, half(h)] = face[c]
-        if step.sends == TURN:
-            for k in range(12):
-                fp[k, :, half(h)] = turn[k]
-                pack_rows(k, 0, turn[k], h, zp)
-                pack_rows(k, 1, qn[k, :, half(h)], h, zp)
-        if sums is not None:
-            total = [a + b for a, b in zip(total, measures(mat))]
-    if not step.last:
-        for c in range(18):
-            out[c, near] = gn[c]
-        if step.sends == WHOLE:
-            pack_z(core, out, upz, zp, refs.pop(0))
-            pack_y(core, out, upy, lowp, highp)
-        else:
-            ends = [row_ends(lambda j, h: (fp, qn)[j][k, :, half(h)]) for k in range(12)]
-            send_rows(ends, lowp, highp)
-    if sums is not None:
-        lane = lax.broadcasted_iota(jnp.int32, (1, 128), 1)
-        line = jnp.zeros((1, 128), F32) if line is None else line[...]
+    if h == 0:
+        if step.colour == 1:
+            r.sums[0] = total[0]
+            r.sums[1] = total[1]
+        return
+    if step.colour == 1:
+        total = [total[0] + r.sums0[0], total[1] + r.sums0[1]]
+        place = lax.broadcasted_iota(jnp.int32, (1, 128), 1)
+        line = r.line_before[...] if step.number > 1 else jnp.zeros((1, 128), F32)
         for k in range(2):
             rows = jnp.sum(total[k], axis=0, keepdims=True)
             value = jnp.sum(rows, axis=1, keepdims=True)
-            line = jnp.where(lane == ITERS * k + step.number // 2, value, line)
-        sums[...] = line
+            line = jnp.where(place == ITERS * k + step.number // 2, value, line)
+        r.line[...] = line
+    for k, s in ((0, far), (1, near)):
+        for c in range(18):
+            for j, part in ((0, (r.new_f0, r.new_n0)[k]), (1, (r.new_f, r.new_n)[k])):
+                if step.last:
+                    (r.out_f, r.out_n)[k][c, :, half(j)] = part[c]
+                else:
+                    r.out[c, s, :, half(j)] = part[c]
+    if step.last:
+        return
+    for c in range(18):
+        r.tp[c, :, half(0)] = r.face_n0[c]
+        r.tp[c, :, half(1)] = r.face_n[c]
+        if step.sends == WHOLE:
+            r.fp[c, :, half(0)] = r.face_f0[c]
+            r.fp[c, :, half(1)] = r.face_f[c]
+    if step.sends == WHOLE:
+        pack_z(core, r.out, r.upz, r.zp, r.pack_scr)
+        pack_y(core, r.out, r.upy, r.lowp, r.highp)
+        return
+    turns = ((r.turn_f0, r.turn_f), (r.turn_n0, r.turn_n))
+    for c in range(12):
+        for k in range(2):
+            for j in range(2):
+                pack_rows(c, k, turns[k][j][c], j, r.zp)
+                if k == 0:
+                    r.fp[c, :, half(j)] = turns[k][j][c]
+    ends = [row_ends(lambda k, j: turns[k][j][c]) for c in range(12)]
+    send_rows(ends, r.lowp, r.highp)
 
 
 def final_kernel(volume, parts, gn, gf, begun, out, monitor, scr, sems):
@@ -531,6 +516,16 @@
     )(*args)
 
 
+def named(body, ins, outs, scratch):
+    names = list(ins) + list(outs) + list(scratch)
+
+    def kernel(*refs):
+        body(types.SimpleNamespace(**dict(zip(names, refs))))
+
+    results = call(kernel, list(outs.values()), list(scratch.values()), list(ins.values()), 10**7)
+    return dict(zip(outs, results))
+
+
 def swap(value, axis, partner):
     count = lax.axis_size(axis)
     return lax.ppermute(value, axis, [(i, partner(i) % count) for i in range(count)])
@@ -581,7 +576,7 @@
     links = lattice_links
     g = [transform, transform]
     packed = [None, side]
-    kept_far, kept_side = [None, None], [None, None]
+    kept = [None, None]
     line = None
     for step in map(Step, range(2 * ITERS)):
         colour = step.colour
@@ -608,43 +603,63 @@
             packed[0] = rest
         if step.last:
             (begun,) = rest
-        outs = [FACE, FACE]
-        outs += [SIDE, SIDE] if step.keeps else []
-        outs += [] if step.last else [FACE]
-        outs += [FACE_12] if step.sends == TURN else []
-        outs += [SUMS] if colour == 1 else []
-        args = [links, g[colour], w, *packed[colour], zh, yu, yd, th]
-        args += kept_side[colour] if step.mode == TURN else []
-        gn, wf, *rest = call(functools.partial(near_kernel, step), outs, [SIDE, FIELD], args, 10**7)
+        base = {"links": links, "g": g[colour], "w": w, "th": th, "fh": fh}
+        outs = {"new_f": SIDE, "new_n": SIDE}
         if step.keeps:
-            kept_side[colour] = [rest.pop(0), rest.pop(0)]
+            outs |= {"y_kept": SIDE, "f_kept": SIDE}
+        scratch = {}
         if not step.last:
-            tp = rest.pop(0)
-        args = [links, g[colour], gn, wf, fh]
-        args += [kept_far[colour]] if step.mode == TURN else []
-        args += [rest.pop()] if colour == 1 else []
-        args += [line] if line is not None and colour == 1 else []
-        args += packed[colour] if step.sends == WHOLE else []
-        args += [rest.pop()] if step.sends == TURN else []
-        outs = [FACE] if step.last else [FIELD]
-        outs += [FACE] if step.keeps else []
+            outs |= {"face_n": SIDE}
+        if step.sends == WHOLE:
+            outs |= {"face_f": SIDE}
+        if step.sends == TURN:
+            outs |= {"turn_f": SIDE_12, "turn_n": SIDE_12}
+        ins = base | {"zh": zh, "y": yd, "upz": packed[colour][0]}
+        if step.mode == TURN:
+            ins |= kept[colour][0]
+        left = named(
+            functools.partial(half_kernel, step, 0),
+            ins,
+            outs | {"z_side": SIDE} | ({"sums": SUMS} if colour == 1 else {}),
+            {},
+        )
+        ins = base | {"z_side": left["z_side"], "y": yu}
+        if step.mode == TURN:
+            ins |= kept[colour][1]
+        if step.mode != TURN or step.sends == WHOLE:
+            ins |= {"upy": packed[colour][1]}
+        if step.sends == WHOLE:
+            ins |= {"upz": packed[colour][0]}
+        ins |= {
+            name + "0": left[name]
+            for name in ("new_f", "new_n", "face_n", "face_f", "turn_f", "turn_n", "sums")
+            if name in left
+        }
+        if colour == 1 and line is not None:
+            ins |= {"line_before": line}
+        scratch = {k: v for k, v in outs.items() if not k.endswith("_kept")}
+        outs = {k: v for k, v in outs.items() if k.endswith("_kept")}
+        if step.last:
+            outs |= {"out_f": FACE, "out_n": FACE}
+        else:
+            outs |= {"out": FIELD, "tp": FACE}
+            outs |= dict(zip(("fp", "zp", "lowp", "highp"), SENT[step.sends]))
+        if colour == 1:
+            outs |= {"line": (1, 128)}
+        if step.sends == WHOLE:
+            scratch |= {"pack_scr": SIDE}
+        right = named(functools.partial(half_kernel, step, 1), ins, outs, scratch)
+        if step.keeps:
+            kept[colour] = [
+                {"y_before": left["y_kept"], "f_before": left["f_kept"], "z_before": left["z_side"]},
+                {"y_before": right["y_kept"], "f_before": right["f_kept"]},
+            ]
+        line = right.get("line", line)
         if not step.last:
-            outs += SENT[step.sends]
-        outs += [(1, 128)] if colour == 1 else []
-        out, *rest = call(
-            functools.partial(far_kernel, step),
-            outs,
-            [SIDE] if step.sends == WHOLE else [],
-            args,
-            10**7,
-        )
-        g[colour] = out
-        if step.keeps:
-            kept_far[colour] = rest.pop(0)
-        if not step.last:
-            fp, zp, lowp, highp, *rest = rest
-        if colour == 1:
-            (line,) = rest
+            g[colour] = right["out"]
+            tp, fp, zp, lowp, highp = (
+                right[k] for k in ("tp", "fp", "zp", "lowp", "highp")
+            )
     count = 1
     for axis in AXES:
         count *= lax.axis_size(axis)
@@ -654,7 +669,7 @@
         functools.partial(final_kernel, volume),
         [(2,) + FIELD, (2, ITERS)],
         [(2, ITERS), pltpu.SemaphoreType.DMA((3,))],
-        [parts, gn, out, begun],
+        [parts, right["out_n"], right["out_f"], begun],
         10**3,
         hbm_outs=(0, 1),
         aliases={3: 0},

time: 72.6 us -> 70 us (0.964)
  waiting for transfers between devices: 5.64 us -> 2.77 us
  blocking collectives: 21.5 us -> 22.9 us
  starting transfers between devices: 33.3 us -> 32.2 us
    ppermute x20, waiting for transfers between devices: 5.64 us -> 2.77 us  [swap(): lax.ppermute(value, axis, [(i, partner(i) % count) for i in range(count)])]
    all_to_all x1, blocking collectives: 21.5 us -> 22.9 us  [shards(): lax.all_to_all(parts, AXES, 0, 0, tiled=True).reshape(count // 8, 8, 128)]
    ppermute x20, starting transfers between devices: 33.3 us -> 32.2 us  [swap(): lax.ppermute(value, axis, [(i, partner(i) % count) for i in range(count)])]
  transfers between devices with their start and end apart: 20 -> 20, of which waited for: 4 -> 6; matrix products, arithmetic and copies ran while one was open for 0% -> 0% of each run, Pallas kernels for 12% -> 9%
where the time goes in v4:
time: 70 us; the launch traced here: 69.9 us
  starting transfers between devices  32.2 us (46%)
  blocking collectives  22.9 us (33%)
  Pallas kernels  11 us (16%)
  waiting for transfers between devices  2.77 us (4%)
  between operations  0.93 us (1%)
    ppermute x20, starting transfers between devices, swap(): lax.ppermute(value, axis, [(i, partner(i) % count) for i in range(count)])  32.2 us
    all_to_all x1, blocking collectives, shards(): lax.all_to_all(parts, AXES, 0, 0, tiled=True).reshape(count // 8, 8, 128)  22.9 us
    pallas_call x14, Pallas kernels, call(): pl.pallas_call(body, out_shape=[jax.ShapeDtypeStruct(o, F32) for o in out...  11 us
    ppermute x20, waiting for transfers between devices, swap(): lax.ppermute(value, axis, [(i, partner(i) % count) for i in range(count)])  2.77 us
  transfers between devices with their start and end apart: 20, of which 6 were waited for; matrix products, arithmetic and copies ran while one was open for 0% of the time, Pallas kernels for 9%

profile of v4, /device:TPU:1, one launch (start us, length us, event | category | flops | bytes accessed | tf_op | source)
XLA Modules:
  0.0 69.9 jit_solution(12287102015856131622)
XLA Ops:
  0.6 1.6 %shard_map.42 = (f32[18,8,256]{2,1,0:T(8,128)S(1)}, f32[12,8,256]{2,1,0:T(8,128)S(1)}, f32[12,8,128]{2,1,0:T(8,128)S(1)}, f32[6,8,128]{2,1,0:T(8,128)S(1)}, f32[...) custom-call(f32[2,4,18,2,8,256]{5,4,3,2,1,0:T(8,128)} %refs_0_.15, ...), custom_call_target="tpu_custom_call" | custom-call | flops 10000000 | tf_op jit(solution)/shard_map/pallas_call | solution.py:501
  2.3 3.3 %collective-permute-start = (f32[18,8,256]{2,1,0:T(8,128)S(1)}, f32[18,8,256]{2,1,0:T(8,128)S(1)}, u32[]{:S(2)}, u32[]{:S(2)}) collective-permute-start(f32[18,8,256]{2,1,0:T(8,128)S(1)} %get-tuple-element.67), channel_id=1, source_target_pairs={{0,8},{8,0},{1,9},{9,1},{2,10},{10,2},{3,11},{11,3},{4,12},{12,4},... | collective-permute-start | bytes 442376 | tf_op jit(solution)/shard_map/ppermute | solution.py:531
  5.6 1.0 %collective-permute-start.1 = (f32[12,8,256]{2,1,0:T(8,128)S(1)}, f32[12,8,256]{2,1,0:T(8,128)S(1)}, u32[]{:S(2)}, u32[]{:S(2)}) collective-permute-start(f32[12,8,256]{2,1,0:T(8,128)S(1)} %get-tuple-element.68), channel_id=1, source_target_pairs={{0,248},{8,16},{16,8},{24,32},{32,24},{40,48},{48,40},{56,64},{64,... | collective-permute-start | bytes 294920 | tf_op jit(solution)/shard_map/ppermute | solution.py:531
  6.6 0.3 collective-permute-start.2
  6.9 1.3 %collective-permute-start.3 = (f32[6,8,128]{2,1,0:T(8,128)S(1)}, f32[6,8,128]{2,1,0:T(8,128)S(1)}, u32[]{:S(2)}, u32[]{:S(2)}) collective-permute-start(f32[6,8,128]{2,1,0:T(8,128)S(1)} %get-tuple-element.70), channel_id=1, source_target_pairs={{0,1},{1,2},{2,3},{3,0},{4,5},{5,6},{6,7},{7,4},{8,9},{9,10},{10,1... | collective-permute-start | bytes 73736 | tf_op jit(solution)/shard_map/ppermute | solution.py:531
  8.2 1.4 %collective-permute-start.4 = (f32[6,8,128]{2,1,0:T(8,128)S(1)}, f32[6,8,128]{2,1,0:T(8,128)S(1)}, u32[]{:S(2)}, u32[]{:S(2)}) collective-permute-start(f32[6,8,128]{2,1,0:T(8,128)S(1)} %get-tuple-element.73), channel_id=1, source_target_pairs={{0,3},{1,0},{2,1},{3,2},{4,7},{5,4},{6,5},{7,6},{8,11},{9,8},{10,9... | collective-permute-start | bytes 73736 | tf_op jit(solution)/shard_map/ppermute | solution.py:531
  9.6 1.1 %shard_map.41 = (f32[18,2,8,256]{3,2,1,0:T(8,128)S(1)}, f32[18,8,128]{2,1,0:T(8,128)S(1)}, f32[18,8,128]{2,1,0:T(8,128)S(1)}) custom-call(f32[2,4,18,2,8,256]{5,4,3,2,1,0:T(8,128)S(1)} %copy-done, f32[2,18,2,8,256]{4,3,2,1,0:T(8,128)S(1)} %copy-done.1), custom_call_target="tpu_custom_call" | custom-call | flops 30000000 | tf_op jit(solution)/shard_map/pallas_call | solution.py:501
  10.8 0.1 collective-permute-done.3.refs_6_
  10.8 0.0 collective-permute-done.2.refs_5_
  10.8 0.4 collective-permute-done.1.refs_4_
  11.3 0.0 collective-permute-done.refs_3_
  11.3 0.5 shard_map.43
  11.8 0.0 collective-permute-done.4.refs_6_
  11.8 0.7 %shard_map.44 = (f32[18,8,128]{2,1,0:T(8,128)S(1)}, f32[18,8,128]{2,1,0:T(8,128)S(1)}, f32[18,2,8,256]{3,2,1,0:T(8,128)S(1)}, f32[18,8,256]{2,1,0:T(8,128)S(1)},...) custom-call(f32[2,4,18,2,8,256]{5,4,3,2,1,0:T(8,128)S(1)} %copy-done, ...), custom_call_target="tpu_custom_call" | custom-call | flops 10000000 | tf_op jit(solution)/shard_map/pallas_call | solution.py:501
  12.5 6.7 %collective-permute-start.5 = (f32[18,8,256]{2,1,0:T(8,128)S(1)}, f32[18,8,256]{2,1,0:T(8,128)S(1)}, u32[]{:S(2)}, u32[]{:S(2)}) collective-permute-start(f32[18,8,256]{2,1,0:T(8,128)S(1)} %get-tuple-element.80), channel_id=1, source_target_pairs={{0,8},{8,0},{1,9},{9,1},{2,10},{10,2},{3,11},{11,3},{4,12},{12,4},... | collective-permute-start | bytes 442376 | tf_op jit(solution)/shard_map/ppermute | solution.py:531
  19.2 1.2 %collective-permute-start.7 = (f32[18,8,128]{2,1,0:T(8,128)S(1)}, f32[18,8,128]{2,1,0:T(8,128)S(1)}, u32[]{:S(2)}, u32[]{:S(2)}) collective-permute-start(f32[18,8,128]{2,1,0:T(8,128)S(1)} %get-tuple-element.82), channel_id=1, source_target_pairs={{0,4},{4,0},{1,5},{5,1},{2,6},{6,2},{3,7},{7,3},{8,12},{12,8},{9,1... | collective-permute-start | bytes 221192 | tf_op jit(solution)/shard_map/ppermute | solution.py:531
  20.4 1.1 %collective-permute-start.8 = (f32[9,8,128]{2,1,0:T(8,128)S(1)}, f32[9,8,128]{2,1,0:T(8,128)S(1)}, u32[]{:S(2)}, u32[]{:S(2)}) collective-permute-start(f32[9,8,128]{2,1,0:T(8,128)S(1)} %get-tuple-element.83), channel_id=1, source_target_pairs={{0,1},{1,2},{2,3},{3,0},{4,5},{5,6},{6,7},{7,4},{8,9},{9,10},{10,1... | collective-permute-start | bytes 110600 | tf_op jit(solution)/shard_map/ppermute | solution.py:531
  21.5 1.5 %collective-permute-start.9 = (f32[9,8,128]{2,1,0:T(8,128)S(1)}, f32[9,8,128]{2,1,0:T(8,128)S(1)}, u32[]{:S(2)}, u32[]{:S(2)}) collective-permute-start(f32[9,8,128]{2,1,0:T(8,128)S(1)} %get-tuple-element.86), channel_id=1, source_target_pairs={{0,3},{1,0},{2,1},{3,2},{4,7},{5,4},{6,5},{7,6},{8,11},{9,8},{10,9... | collective-permute-start | bytes 110600 | tf_op jit(solution)/shard_map/ppermute | solution.py:531
  23.0 1.1 %shard_map.45.refs_2_ = f32[18,2,8,256]{3,2,1,0:T(8,128)S(1)} custom-call(f32[2,4,18,2,8,256]{5,4,3,2,1,0:T(8,128)S(1)} %copy-done, f32[18,2,8,256]{3,2,1,0:T(8,128)S(1)} %get-tuple-element.79.gp.refs_1_), custom_call_target="tpu_custom_call" | custom-call | flops 30000000 | tf_op jit(solution)/shard_map/pallas_call | solution.py:501
  24.1 0.2 collective-permute-done.8.refs_6_
  24.4 0.0 collective-permute-done.7.refs_5_
  24.4 0.0 collective-permute-done.5.refs_3_
  24.4 1.2 %collective-permute-done.6.refs_4_ = f32[18,8,256]{2,1,0:T(8,128)S(1)} collective-permute-done((f32[18,8,256]{2,1,0:T(8,128)S(1)}, f32[18,8,256]{2,1,0:T(8,128)S(1)}, u32[]{:S(2)}, u32[]{:S(2)}) %collective-permute-start.6) | collective-permute-done | bytes 147488 | tf_op jit(solution)/shard_map/ppermute | solution.py:531
  25.6 0.5 shard_map.46
  26.0 0.0 collective-permute-done.9.refs_6_
  26.0 0.6 shard_map.47
  26.6 2.1 %collective-permute-start.10 = (f32[18,8,256]{2,1,0:T(8,128)S(1)}, f32[18,8,256]{2,1,0:T(8,128)S(1)}, u32[]{:S(2)}, u32[]{:S(2)}) collective-permute-start(f32[18,8,256]{2,1,0:T(8,128)S(1)} %get-tuple-element.95), channel_id=1, source_target_pairs={{0,8},{8,0},{1,9},{9,1},{2,10},{10,2},{3,11},{11,3},{4,12},{12,4},... | collective-permute-start | bytes 442376 | tf_op jit(solution)/shard_map/ppermute | solution.py:531
  28.7 2.7 %collective-permute-start.11 = (f32[12,8,256]{2,1,0:T(8,128)S(1)}, f32[12,8,256]{2,1,0:T(8,128)S(1)}, u32[]{:S(2)}, u32[]{:S(2)}) collective-permute-start(f32[12,8,256]{2,1,0:T(8,128)S(1)} %get-tuple-element.96), channel_id=1, source_target_pairs={{0,248},{8,16},{16,8},{24,32},{32,24},{40,48},{48,40},{56,64},{64,... | collective-permute-start | bytes 294920 | tf_op jit(solution)/shard_map/ppermute | solution.py:531
  31.4 0.0 collective-permute-start.12
  31.4 1.1 %collective-permute-start.13 = (f32[6,8,128]{2,1,0:T(8,128)S(1)}, f32[6,8,128]{2,1,0:T(8,128)S(1)}, u32[]{:S(2)}, u32[]{:S(2)}) collective-permute-start(f32[6,8,128]{2,1,0:T(8,128)S(1)} %get-tuple-element.98), channel_id=1, source_target_pairs={{0,1},{1,2},{2,3},{3,0},{4,5},{5,6},{6,7},{7,4},{8,9},{9,10},{10,1... | collective-permute-start | bytes 73736 | tf_op jit(solution)/shard_map/ppermute | solution.py:531
  32.6 1.5 %collective-permute-start.14 = (f32[6,8,128]{2,1,0:T(8,128)S(1)}, f32[6,8,128]{2,1,0:T(8,128)S(1)}, u32[]{:S(2)}, u32[]{:S(2)}) collective-permute-start(f32[6,8,128]{2,1,0:T(8,128)S(1)} %get-tuple-element.102), channel_id=1, source_target_pairs={{0,3},{1,0},{2,1},{3,2},{4,7},{5,4},{6,5},{7,6},{8,11},{9,8},{10,9... | collective-permute-start | bytes 73736 | tf_op jit(solution)/shard_map/ppermute | solution.py:531
  34.1 1.1 %shard_map.48.refs_2_ = f32[18,2,8,256]{3,2,1,0:T(8,128)S(1)} custom-call(f32[2,4,18,2,8,256]{5,4,3,2,1,0:T(8,128)S(1)} %copy-done, f32[18,2,8,256]{3,2,1,0:T(8,128)S(1)} %get-tuple-element.94.gp.refs_1_), custom_call_target="tpu_custom_call" | custom-call | flops 30000000 | tf_op jit(solution)/shard_map/pallas_call | solution.py:501
  35.2 0.4 collective-permute-done.13.refs_6_
  35.6 0.0 collective-permute-done.12.refs_5_
  35.6 0.5 shard_map.49
  36.1 0.5 shard_map.50
  36.6 2.4 %collective-permute-start.15 = (f32[18,8,256]{2,1,0:T(8,128)S(1)}, f32[18,8,256]{2,1,0:T(8,128)S(1)}, u32[]{:S(2)}, u32[]{:S(2)}) collective-permute-start(f32[18,8,256]{2,1,0:T(8,128)S(1)} %get-tuple-element.112), channel_id=1, source_target_pairs={{0,8},{8,0},{1,9},{9,1},{2,10},{10,2},{3,11},{11,3},{4,12},{12,4},... | collective-permute-start | bytes 442376 | tf_op jit(solution)/shard_map/ppermute | solution.py:531
  39.0 1.2 %collective-permute-start.16 = (f32[12,8,256]{2,1,0:T(8,128)S(1)}, f32[12,8,256]{2,1,0:T(8,128)S(1)}, u32[]{:S(2)}, u32[]{:S(2)}) collective-permute-start(f32[12,8,256]{2,1,0:T(8,128)S(1)} %get-tuple-element.113), channel_id=1, source_target_pairs={{0,248},{8,16},{16,8},{24,32},{32,24},{40,48},{48,40},{56,64},{64,... | collective-permute-start | bytes 294920 | tf_op jit(solution)/shard_map/ppermute | solution.py:531
  40.3 0.5 collective-permute-start.17
  40.8 0.7 %collective-permute-start.18 = (f32[6,8,128]{2,1,0:T(8,128)S(1)}, f32[6,8,128]{2,1,0:T(8,128)S(1)}, u32[]{:S(2)}, u32[]{:S(2)}) collective-permute-start(f32[6,8,128]{2,1,0:T(8,128)S(1)} %get-tuple-element.115), channel_id=1, source_target_pairs={{0,1},{1,2},{2,3},{3,0},{4,5},{5,6},{6,7},{7,4},{8,9},{9,10},{10,1... | collective-permute-start | bytes 73736 | tf_op jit(solution)/shard_map/ppermute | solution.py:531
  41.5 2.0 %collective-permute-start.19 = (f32[6,8,128]{2,1,0:T(8,128)S(1)}, f32[6,8,128]{2,1,0:T(8,128)S(1)}, u32[]{:S(2)}, u32[]{:S(2)}) collective-permute-start(f32[6,8,128]{2,1,0:T(8,128)S(1)} %get-tuple-element.119), channel_id=1, source_target_pairs={{0,3},{1,0},{2,1},{3,2},{4,7},{5,4},{6,5},{7,6},{8,11},{9,8},{10,9... | collective-permute-start | bytes 73736 | tf_op jit(solution)/shard_map/ppermute | solution.py:531
  43.4 1.1 %shard_map.51 = (f32[18,2,8,256]{3,2,1,0:T(8,128)S(1)}, f32[2,18,2,8,256]{4,3,2,1,0:T(8,128)}) custom-call(f32[2,4,18,2,8,256]{5,4,3,2,1,0:T(8,128)S(1)} %copy-done, f32[18,2,8,256]{3,2,1,0:T(8,128)S(1)} %get-tuple-element.110.gp), custom_call_target="tpu_custom_call" | custom-call | flops 30000000 | tf_op jit(solution)/shard_map/pallas_call | solution.py:501
  44.5 0.4 collective-permute-done.18.refs_6_
  44.9 0.5 shard_map.52
  45.5 0.5 shard_map.53
  46.0 0.1 broadcast_in_dim.9
  46.1 22.9 %all_to_all.5 = f32[256,1,128]{2,1,0:T(1,128)S(1)} all-to-all(f32[256,1,128]{2,1,0:T(1,128)S(1)} %broadcast_in_dim.9), channel_id=1, replica_groups=mesh['tz'=8,'tx'=2,'tc'=2,'gz'=2,'gy'=4] {'tz','tx','tc','gz','gy'}, dimensions={0} | all-to-all | bytes 262144 | tf_op jit(solution)/shard_map/all_to_all | solution.py:667
  69.0 0.7 %shard_map.54 = (f32[2,18,2,8,256]{4,3,2,1,0:T(8,128)}, f32[2,2]{1,0:T(2,128)}) custom-call(f32[32,8,128]{2,1,0:T(8,128)S(1)} %bitcast.2, f32[18,8,256]{2,1,0:T(8,128)S(1)} %get-tuple-element.127.gn, f32[18,8,256]{2,1,0:T(8,128)S(1)} %get-tuple-element.128.gf, f32[2,18,2,8,256]{4,3,2,1,0:T(8,128)} %get-tuple-element.129.begun), custom_call_target="tpu_custom_call", output_to_operand_aliasing={{0}: (3, {})} | custom-call | flops 1000 | tf_op jit(solution)/shard_map/pallas_call | solution.py:501
  (12 shorter events, 0.0 us)
Async XLA Ops:
  0.6 9.0 %copy-start = (f32[2,4,18,2,8,256]{5,4,3,2,1,0:T(8,128)S(1)}, f32[2,4,18,2,8,256]{5,4,3,2,1,0:T(8,128)}, u32[]{:S(2)}) copy-start(f32[2,4,18,2,8,256]{5,4,3,2,1,0:T(8,128)} %refs_0_.15) | copy-start | bytes 7077892
  0.6 9.0 %copy-start.1 = (f32[2,18,2,8,256]{4,3,2,1,0:T(8,128)S(1)}, f32[2,18,2,8,256]{4,3,2,1,0:T(8,128)}, u32[]{:S(2)}) copy-start(f32[2,18,2,8,256]{4,3,2,1,0:T(8,128)} %refs_1_.7) | copy-start | bytes 1769476
  2.3 9.0 %collective-permute-start = (f32[18,8,256]{2,1,0:T(8,128)S(1)}, f32[18,8,256]{2,1,0:T(8,128)S(1)}, u32[]{:S(2)}, u32[]{:S(2)}) collective-permute-start(f32[18,8,256]{2,1,0:T(8,128)S(1)} %get-tuple-element.67), channel_id=1, source_target_pairs={{0,8},{8,0},{1,9},{9,1},{2,10},{10,2},{3,11},{11,3},{4,12},{12,4},... | collective-permute-start | bytes 442376 | tf_op jit(solution)/shard_map/ppermute | solution.py:531
  5.6 5.7 %collective-permute-start.1 = (f32[12,8,256]{2,1,0:T(8,128)S(1)}, f32[12,8,256]{2,1,0:T(8,128)S(1)}, u32[]{:S(2)}, u32[]{:S(2)}) collective-permute-start(f32[12,8,256]{2,1,0:T(8,128)S(1)} %get-tuple-element.68), channel_id=1, source_target_pairs={{0,248},{8,16},{16,8},{24,32},{32,24},{40,48},{48,40},{56,64},{64,... | collective-permute-start | bytes 294920 | tf_op jit(solution)/shard_map/ppermute | solution.py:531
  6.6 4.3 %collective-permute-start.2 = (f32[12,8,128]{2,1,0:T(8,128)S(1)}, f32[12,8,128]{2,1,0:T(8,128)S(1)}, u32[]{:S(2)}, u32[]{:S(2)}) collective-permute-start(f32[12,8,128]{2,1,0:T(8,128)S(1)} %get-tuple-element.69), channel_id=1, source_target_pairs={{0,4},{4,0},{1,5},{5,1},{2,6},{6,2},{3,7},{7,3},{8,12},{12,8},{9,1... | collective-permute-start | bytes 147464 | tf_op jit(solution)/shard_map/ppermute | solution.py:531
  6.9 3.9 %collective-permute-start.3 = (f32[6,8,128]{2,1,0:T(8,128)S(1)}, f32[6,8,128]{2,1,0:T(8,128)S(1)}, u32[]{:S(2)}, u32[]{:S(2)}) collective-permute-start(f32[6,8,128]{2,1,0:T(8,128)S(1)} %get-tuple-element.70), channel_id=1, source_target_pairs={{0,1},{1,2},{2,3},{3,0},{4,5},{5,6},{6,7},{7,4},{8,9},{9,10},{10,1... | collective-permute-start | bytes 73736 | tf_op jit(solution)/shard_map/ppermute | solution.py:531
  8.2 3.6 %collective-permute-start.4 = (f32[6,8,128]{2,1,0:T(8,128)S(1)}, f32[6,8,128]{2,1,0:T(8,128)S(1)}, u32[]{:S(2)}, u32[]{:S(2)}) collective-permute-start(f32[6,8,128]{2,1,0:T(8,128)S(1)} %get-tuple-element.73), channel_id=1, source_target_pairs={{0,3},{1,0},{2,1},{3,2},{4,7},{5,4},{6,5},{7,6},{8,11},{9,8},{10,9... | collective-permute-start | bytes 73736 | tf_op jit(solution)/shard_map/ppermute | solution.py:531
  12.5 11.9 %collective-permute-start.5 = (f32[18,8,256]{2,1,0:T(8,128)S(1)}, f32[18,8,256]{2,1,0:T(8,128)S(1)}, u32[]{:S(2)}, u32[]{:S(2)}) collective-permute-start(f32[18,8,256]{2,1,0:T(8,128)S(1)} %get-tuple-element.80), channel_id=1, source_target_pairs={{0,8},{8,0},{1,9},{9,1},{2,10},{10,2},{3,11},{11,3},{4,12},{12,4},... | collective-permute-start | bytes 442376 | tf_op jit(solution)/shard_map/ppermute | solution.py:531
  19.2 6.4 %collective-permute-start.6 = (f32[18,8,256]{2,1,0:T(8,128)S(1)}, f32[18,8,256]{2,1,0:T(8,128)S(1)}, u32[]{:S(2)}, u32[]{:S(2)}) collective-permute-start(f32[18,8,256]{2,1,0:T(8,128)S(1)} %get-tuple-element.81), channel_id=1, source_target_pairs={{0,248},{8,16},{16,8},{24,32},{32,24},{40,48},{48,40},{56,64},{64,... | collective-permute-start | bytes 442376 | tf_op jit(solution)/shard_map/ppermute | solution.py:531
  19.2 5.2 %collective-permute-start.7 = (f32[18,8,128]{2,1,0:T(8,128)S(1)}, f32[18,8,128]{2,1,0:T(8,128)S(1)}, u32[]{:S(2)}, u32[]{:S(2)}) collective-permute-start(f32[18,8,128]{2,1,0:T(8,128)S(1)} %get-tuple-element.82), channel_id=1, source_target_pairs={{0,4},{4,0},{1,5},{5,1},{2,6},{6,2},{3,7},{7,3},{8,12},{12,8},{9,1... | collective-permute-start | bytes 221192 | tf_op jit(solution)/shard_map/ppermute | solution.py:531
  20.4 4.0 %collective-permute-start.8 = (f32[9,8,128]{2,1,0:T(8,128)S(1)}, f32[9,8,128]{2,1,0:T(8,128)S(1)}, u32[]{:S(2)}, u32[]{:S(2)}) collective-permute-start(f32[9,8,128]{2,1,0:T(8,128)S(1)} %get-tuple-element.83), channel_id=1, source_target_pairs={{0,1},{1,2},{2,3},{3,0},{4,5},{5,6},{6,7},{7,4},{8,9},{9,10},{10,1... | collective-permute-start | bytes 110600 | tf_op jit(solution)/shard_map/ppermute | solution.py:531
  21.5 4.5 %collective-permute-start.9 = (f32[9,8,128]{2,1,0:T(8,128)S(1)}, f32[9,8,128]{2,1,0:T(8,128)S(1)}, u32[]{:S(2)}, u32[]{:S(2)}) collective-permute-start(f32[9,8,128]{2,1,0:T(8,128)S(1)} %get-tuple-element.86), channel_id=1, source_target_pairs={{0,3},{1,0},{2,1},{3,2},{4,7},{5,4},{6,5},{7,6},{8,11},{9,8},{10,9... | collective-permute-start | bytes 110600 | tf_op jit(solution)/shard_map/ppermute | solution.py:531
  26.6 9.0 %collective-permute-start.10 = (f32[18,8,256]{2,1,0:T(8,128)S(1)}, f32[18,8,256]{2,1,0:T(8,128)S(1)}, u32[]{:S(2)}, u32[]{:S(2)}) collective-permute-start(f32[18,8,256]{2,1,0:T(8,128)S(1)} %get-tuple-element.95), channel_id=1, source_target_pairs={{0,8},{8,0},{1,9},{9,1},{2,10},{10,2},{3,11},{11,3},{4,12},{12,4},... | collective-permute-start | bytes 442376 | tf_op jit(solution)/shard_map/ppermute | solution.py:531
  28.7 6.9 %collective-permute-start.11 = (f32[12,8,256]{2,1,0:T(8,128)S(1)}, f32[12,8,256]{2,1,0:T(8,128)S(1)}, u32[]{:S(2)}, u32[]{:S(2)}) collective-permute-start(f32[12,8,256]{2,1,0:T(8,128)S(1)} %get-tuple-element.96), channel_id=1, source_target_pairs={{0,248},{8,16},{16,8},{24,32},{32,24},{40,48},{48,40},{56,64},{64,... | collective-permute-start | bytes 294920 | tf_op jit(solution)/shard_map/ppermute | solution.py:531
  31.4 4.2 %collective-permute-start.12 = (f32[12,8,128]{2,1,0:T(8,128)S(1)}, f32[12,8,128]{2,1,0:T(8,128)S(1)}, u32[]{:S(2)}, u32[]{:S(2)}) collective-permute-start(f32[12,8,128]{2,1,0:T(8,128)S(1)} %get-tuple-element.97), channel_id=1, source_target_pairs={{0,4},{4,0},{1,5},{5,1},{2,6},{6,2},{3,7},{7,3},{8,12},{12,8},{9,1... | collective-permute-start | bytes 147464 | tf_op jit(solution)/shard_map/ppermute | solution.py:531
  31.4 4.2 %collective-permute-start.13 = (f32[6,8,128]{2,1,0:T(8,128)S(1)}, f32[6,8,128]{2,1,0:T(8,128)S(1)}, u32[]{:S(2)}, u32[]{:S(2)}) collective-permute-start(f32[6,8,128]{2,1,0:T(8,128)S(1)} %get-tuple-element.98), channel_id=1, source_target_pairs={{0,1},{1,2},{2,3},{3,0},{4,5},{5,6},{6,7},{7,4},{8,9},{9,10},{10,1... | collective-permute-start | bytes 73736 | tf_op jit(solution)/shard_map/ppermute | solution.py:531
  32.6 3.5 %collective-permute-start.14 = (f32[6,8,128]{2,1,0:T(8,128)S(1)}, f32[6,8,128]{2,1,0:T(8,128)S(1)}, u32[]{:S(2)}, u32[]{:S(2)}) collective-permute-start(f32[6,8,128]{2,1,0:T(8,128)S(1)} %get-tuple-element.102), channel_id=1, source_target_pairs={{0,3},{1,0},{2,1},{3,2},{4,7},{5,4},{6,5},{7,6},{8,11},{9,8},{10,9... | collective-permute-start | bytes 73736 | tf_op jit(solution)/shard_map/ppermute | solution.py:531
  36.6 8.3 %collective-permute-start.15 = (f32[18,8,256]{2,1,0:T(8,128)S(1)}, f32[18,8,256]{2,1,0:T(8,128)S(1)}, u32[]{:S(2)}, u32[]{:S(2)}) collective-permute-start(f32[18,8,256]{2,1,0:T(8,128)S(1)} %get-tuple-element.112), channel_id=1, source_target_pairs={{0,8},{8,0},{1,9},{9,1},{2,10},{10,2},{3,11},{11,3},{4,12},{12,4},... | collective-permute-start | bytes 442376 | tf_op jit(solution)/shard_map/ppermute | solution.py:531
  39.0 5.9 %collective-permute-start.16 = (f32[12,8,256]{2,1,0:T(8,128)S(1)}, f32[12,8,256]{2,1,0:T(8,128)S(1)}, u32[]{:S(2)}, u32[]{:S(2)}) collective-permute-start(f32[12,8,256]{2,1,0:T(8,128)S(1)} %get-tuple-element.113), channel_id=1, source_target_pairs={{0,248},{8,16},{16,8},{24,32},{32,24},{40,48},{48,40},{56,64},{64,... | collective-permute-start | bytes 294920 | tf_op jit(solution)/shard_map/ppermute | solution.py:531
  40.3 4.7 %collective-permute-start.17 = (f32[12,8,128]{2,1,0:T(8,128)S(1)}, f32[12,8,128]{2,1,0:T(8,128)S(1)}, u32[]{:S(2)}, u32[]{:S(2)}) collective-permute-start(f32[12,8,128]{2,1,0:T(8,128)S(1)} %get-tuple-element.114), channel_id=1, source_target_pairs={{0,4},{4,0},{1,5},{5,1},{2,6},{6,2},{3,7},{7,3},{8,12},{12,8},{9,1... | collective-permute-start | bytes 147464 | tf_op jit(solution)/shard_map/ppermute | solution.py:531
  40.8 4.2 %collective-permute-start.18 = (f32[6,8,128]{2,1,0:T(8,128)S(1)}, f32[6,8,128]{2,1,0:T(8,128)S(1)}, u32[]{:S(2)}, u32[]{:S(2)}) collective-permute-start(f32[6,8,128]{2,1,0:T(8,128)S(1)} %get-tuple-element.115), channel_id=1, source_target_pairs={{0,1},{1,2},{2,3},{3,0},{4,5},{5,6},{6,7},{7,4},{8,9},{9,10},{10,1... | collective-permute-start | bytes 73736 | tf_op jit(solution)/shard_map/ppermute | solution.py:531
  41.5 4.0 %collective-permute-start.19 = (f32[6,8,128]{2,1,0:T(8,128)S(1)}, f32[6,8,128]{2,1,0:T(8,128)S(1)}, u32[]{:S(2)}, u32[]{:S(2)}) collective-permute-start(f32[6,8,128]{2,1,0:T(8,128)S(1)} %get-tuple-element.119), channel_id=1, source_target_pairs={{0,3},{1,0},{2,1},{3,2},{4,7},{5,4},{6,5},{7,6},{8,11},{9,8},{10,9... | collective-permute-start | bytes 73736 | tf_op jit(solution)/shard_map/ppermute | solution.py:531

commit v5 on v4

--- a/solution.py
+++ b/solution.py
@@ -34,38 +34,37 @@
     return pl.ds(128 * h, 128)
 
 
+def three_products(left, right, sign):
+    out = [[None] * 9 for _ in R3]
+    for k in R3:
+        lr = [left(i, k, 0) for i in R3]
+        li = [left(i, k, 1) for i in R3]
+        rr = [right(j, k, 0) for j in R3]
+        ri = [right(j, k, 1) for j in R3]
+        ls = [x + y for x, y in zip(lr, li)]
+        rs = [x + y if sign > 0 else x - y for x, y in zip(rr, ri)]
+        for n, (x, y) in enumerate(((lr, rr), (li, ri), (ls, rs))):
+            for i in R3:
+                for j in R3:
+                    term = x[i] * y[j]
+                    old = out[n][re(i, j)]
+                    out[n][re(i, j)] = term if old is None else old + term
+    return out
+
+
 def times_adjoint(acc, left, right):
-    out = list(acc)
-    for k in R3:
-        lr = [left(re(i, k)) for i in R3]
-        li = [left(im(i, k)) for i in R3]
-        rr = [right(re(j, k)) for j in R3]
-        ri = [right(im(j, k)) for j in R3]
-        for i in R3:
-            for j in R3:
-                tr = lr[i] * rr[j] + li[i] * ri[j]
-                ti = li[i] * rr[j] - lr[i] * ri[j]
-                a, b = re(i, j), im(i, j)
-                out[a] = tr if out[a] is None else out[a] + tr
-                out[b] = ti if out[b] is None else out[b] + ti
-    return out
+    p, q, s = three_products(
+        lambda i, k, n: left(9 * n + re(i, k)), lambda j, k, n: right(9 * n + re(j, k)), -1
+    )
+    out = [x + y for x, y in zip(p, q)] + [z - (x - y) for x, y, z in zip(p, q, s)]
+    return [v if a is None else a + v for a, v in zip(acc, out)]
 
 
 def times(left, right):
-    out = [None] * 18
-    for k in R3:
-        lr = [left(re(i, k)) for i in R3]
-        li = [left(im(i, k)) for i in R3]
-        rr = [right(re(k, j)) for j in R3]
-        ri = [right(im(k, j)) for j in R3]
-        for i in R3:
-            for j in R3:
-                tr = lr[i] * rr[j] - li[i] * ri[j]
-                ti = lr[i] * ri[j] + li[i] * rr[j]
-                a, b = re(i, j), im(i, j)
-                out[a] = tr if out[a] is None else out[a] + tr
-                out[b] = ti if out[b] is None else out[b] + ti
-    return out
+    p, q, s = three_products(
+        lambda i, k, n: left(9 * n + re(i, k)), lambda j, k, n: right(9 * n + re(k, j)), 1
+    )
+    return [x - y for x, y in zip(p, q)] + [z - (x + y) for x, y, z in zip(p, q, s)]
 
 
 def plus_adjoint(acc, mat):
@@ -403,7 +402,16 @@
         acc = with_sides(k, s)
         if k == 1:
             link = crossing(own, h, core == 1)
-            acc = times_adjoint(acc, link, lambda c: r.th[c, :, half(h)])
+            part = behind(
+                WHOLE if step.mode == TWO_ROWS else step.mode,
+                lambda c: r.th[c, :, half(h)],
+                link,
+                r.t_before if step.mode == TURN else None,
+            )
+            if step.keeps:
+                for c in range(18):
+                    r.t_kept[c] = part[c]
+            acc = plus_adjoint(acc, part)
         else:
             link = crossing(own, h, core == 0)
             part = behind(
@@ -420,7 +428,7 @@
         to = (r.new_f, r.new_n)[k]
         for c in range(18):
             to[c] = new[c]
-        if not step.last and (k == 1 or step.sends == WHOLE):
+        if step.sends == WHOLE:
             face = times(lambda c: new[c], link)
             to = r.face_n if k == 1 else r.face_f
             for c in range(18):
@@ -455,13 +463,12 @@
                     r.out[c, s, :, half(j)] = part[c]
     if step.last:
         return
-    for c in range(18):
-        r.tp[c, :, half(0)] = r.face_n0[c]
-        r.tp[c, :, half(1)] = r.face_n[c]
-        if step.sends == WHOLE:
+    if step.sends == WHOLE:
+        for c in range(18):
+            r.tp[c, :, half(0)] = r.face_n0[c]
+            r.tp[c, :, half(1)] = r.face_n[c]
             r.fp[c, :, half(0)] = r.face_f0[c]
             r.fp[c, :, half(1)] = r.face_f[c]
-    if step.sends == WHOLE:
         pack_z(core, r.out, r.upz, r.zp, r.pack_scr)
         pack_y(core, r.out, r.upy, r.lowp, r.highp)
         return
@@ -470,8 +477,7 @@
         for k in range(2):
             for j in range(2):
                 pack_rows(c, k, turns[k][j][c], j, r.zp)
-                if k == 0:
-                    r.fp[c, :, half(j)] = turns[k][j][c]
+                (r.fp, r.tp)[k][c, :, half(j)] = turns[k][j][c]
     ends = [row_ends(lambda k, j: turns[k][j][c]) for c in range(12)]
     send_rows(ends, r.lowp, r.highp)
 
@@ -606,12 +612,9 @@
         base = {"links": links, "g": g[colour], "w": w, "th": th, "fh": fh}
         outs = {"new_f": SIDE, "new_n": SIDE}
         if step.keeps:
-            outs |= {"y_kept": SIDE, "f_kept": SIDE}
-        scratch = {}
-        if not step.last:
-            outs |= {"face_n": SIDE}
+            outs |= {"y_kept": SIDE, "f_kept": SIDE, "t_kept": SIDE}
         if step.sends == WHOLE:
-            outs |= {"face_f": SIDE}
+            outs |= {"face_f": SIDE, "face_n": SIDE}
         if step.sends == TURN:
             outs |= {"turn_f": SIDE_12, "turn_n": SIDE_12}
         ins = base | {"zh": zh, "y": yd, "upz": packed[colour][0]}
@@ -642,7 +645,7 @@
         if step.last:
             outs |= {"out_f": FACE, "out_n": FACE}
         else:
-            outs |= {"out": FIELD, "tp": FACE}
+            outs |= {"out": FIELD, "tp": SENT[step.sends][0]}
             outs |= dict(zip(("fp", "zp", "lowp", "highp"), SENT[step.sends]))
         if colour == 1:
             outs |= {"line": (1, 128)}
@@ -651,9 +654,10 @@
         right = named(functools.partial(half_kernel, step, 1), ins, outs, scratch)
         if step.keeps:
             kept[colour] = [
-                {"y_before": left["y_kept"], "f_before": left["f_kept"], "z_before": left["z_side"]},
-                {"y_before": right["y_kept"], "f_before": right["f_kept"]},
+                {name + "_before": part[name + "_kept"] for name in "yft"}
+                for part in (left, right)
             ]
+            kept[colour][0]["z_before"] = left["z_side"]
         line = right.get("line", line)
         if not step.last:
             g[colour] = right["out"]

time: 70 us -> 69.8 us (level)
  transfers between devices with their start and end apart: 20 -> 20, of which waited for: 6 -> 4; matrix products, arithmetic and copies ran while one was open for 0% -> 0% of each run, Pallas kernels for 9% -> 10%
where the time goes in v5:
time: 69.8 us; the launch traced here: 69.7 us
  starting transfers between devices  32.1 us (46%)
  blocking collectives  22.7 us (33%)
  Pallas kernels  11.5 us (16%)
  waiting for transfers between devices  2.32 us (3%)
  between operations  0.96 us (1%)
    ppermute x20, starting transfers between devices, swap(): lax.ppermute(value, axis, [(i, partner(i) % count) for i in range(count)])  32.1 us
    all_to_all x1, blocking collectives, shards(): lax.all_to_all(parts, AXES, 0, 0, tiled=True).reshape(count // 8, 8, 128)  22.7 us
    pallas_call x14, Pallas kernels, call(): pl.pallas_call(body, out_shape=[jax.ShapeDtypeStruct(o, F32) for o in out...  11.5 us
    ppermute x20, waiting for transfers between devices, swap(): lax.ppermute(value, axis, [(i, partner(i) % count) for i in range(count)])  2.32 us
  transfers between devices with their start and end apart: 20, of which 4 were waited for; matrix products, arithmetic and copies ran while one was open for 0% of the time, Pallas kernels for 10%

profile of v5, /device:TPU:1, one launch (start us, length us, event | category | flops | bytes accessed | tf_op | source)
XLA Modules:
  0.0 69.7 jit_solution(13442378766038576090)
XLA Ops:
  0.6 1.6 %shard_map.42 = (f32[18,8,256]{2,1,0:T(8,128)S(1)}, f32[12,8,256]{2,1,0:T(8,128)S(1)}, f32[12,8,128]{2,1,0:T(8,128)S(1)}, f32[6,8,128]{2,1,0:T(8,128)S(1)}, f32[...) custom-call(f32[2,4,18,2,8,256]{5,4,3,2,1,0:T(8,128)} %refs_0_.15, ...), custom_call_target="tpu_custom_call" | custom-call | flops 10000000 | tf_op jit(solution)/shard_map/pallas_call | solution.py:507
  2.3 3.3 %collective-permute-start = (f32[18,8,256]{2,1,0:T(8,128)S(1)}, f32[18,8,256]{2,1,0:T(8,128)S(1)}, u32[]{:S(2)}, u32[]{:S(2)}) collective-permute-start(f32[18,8,256]{2,1,0:T(8,128)S(1)} %get-tuple-element.69), channel_id=1, source_target_pairs={{0,8},{8,0},{1,9},{9,1},{2,10},{10,2},{3,11},{11,3},{4,12},{12,4},... | collective-permute-start | bytes 442376 | tf_op jit(solution)/shard_map/ppermute | solution.py:537
  5.6 1.0 %collective-permute-start.1 = (f32[12,8,256]{2,1,0:T(8,128)S(1)}, f32[12,8,256]{2,1,0:T(8,128)S(1)}, u32[]{:S(2)}, u32[]{:S(2)}) collective-permute-start(f32[12,8,256]{2,1,0:T(8,128)S(1)} %get-tuple-element.70), channel_id=1, source_target_pairs={{0,248},{8,16},{16,8},{24,32},{32,24},{40,48},{48,40},{56,64},{64,... | collective-permute-start | bytes 294920 | tf_op jit(solution)/shard_map/ppermute | solution.py:537
  6.6 0.3 collective-permute-start.2
  6.9 1.3 %collective-permute-start.3 = (f32[6,8,128]{2,1,0:T(8,128)S(1)}, f32[6,8,128]{2,1,0:T(8,128)S(1)}, u32[]{:S(2)}, u32[]{:S(2)}) collective-permute-start(f32[6,8,128]{2,1,0:T(8,128)S(1)} %get-tuple-element.72), channel_id=1, source_target_pairs={{0,1},{1,2},{2,3},{3,0},{4,5},{5,6},{6,7},{7,4},{8,9},{9,10},{10,1... | collective-permute-start | bytes 73736 | tf_op jit(solution)/shard_map/ppermute | solution.py:537
  8.2 1.4 %collective-permute-start.4 = (f32[6,8,128]{2,1,0:T(8,128)S(1)}, f32[6,8,128]{2,1,0:T(8,128)S(1)}, u32[]{:S(2)}, u32[]{:S(2)}) collective-permute-start(f32[6,8,128]{2,1,0:T(8,128)S(1)} %get-tuple-element.75), channel_id=1, source_target_pairs={{0,3},{1,0},{2,1},{3,2},{4,7},{5,4},{6,5},{7,6},{8,11},{9,8},{10,9... | collective-permute-start | bytes 73736 | tf_op jit(solution)/shard_map/ppermute | solution.py:537
  9.6 1.2 %shard_map.41 = (f32[18,2,8,256]{3,2,1,0:T(8,128)S(1)}, f32[18,8,128]{2,1,0:T(8,128)S(1)}, f32[18,8,128]{2,1,0:T(8,128)S(1)}) custom-call(f32[2,4,18,2,8,256]{5,4,3,2,1,0:T(8,128)S(1)} %copy-done, f32[2,18,2,8,256]{4,3,2,1,0:T(8,128)S(1)} %copy-done.1), custom_call_target="tpu_custom_call" | custom-call | flops 30000000 | tf_op jit(solution)/shard_map/pallas_call | solution.py:507
  10.8 0.0 collective-permute-done.3.refs_6_
  10.8 0.0 collective-permute-done.2.refs_5_
  10.8 0.4 collective-permute-done.1.refs_4_
  11.3 0.4 shard_map.43
  11.7 0.7 shard_map.44
  12.4 6.7 %collective-permute-start.5 = (f32[18,8,256]{2,1,0:T(8,128)S(1)}, f32[18,8,256]{2,1,0:T(8,128)S(1)}, u32[]{:S(2)}, u32[]{:S(2)}) collective-permute-start(f32[18,8,256]{2,1,0:T(8,128)S(1)} %get-tuple-element.82), channel_id=1, source_target_pairs={{0,8},{8,0},{1,9},{9,1},{2,10},{10,2},{3,11},{11,3},{4,12},{12,4},... | collective-permute-start | bytes 442376 | tf_op jit(solution)/shard_map/ppermute | solution.py:537
  19.1 1.2 %collective-permute-start.7 = (f32[18,8,128]{2,1,0:T(8,128)S(1)}, f32[18,8,128]{2,1,0:T(8,128)S(1)}, u32[]{:S(2)}, u32[]{:S(2)}) collective-permute-start(f32[18,8,128]{2,1,0:T(8,128)S(1)} %get-tuple-element.84), channel_id=1, source_target_pairs={{0,4},{4,0},{1,5},{5,1},{2,6},{6,2},{3,7},{7,3},{8,12},{12,8},{9,1... | collective-permute-start | bytes 221192 | tf_op jit(solution)/shard_map/ppermute | solution.py:537
  20.3 1.2 %collective-permute-start.8 = (f32[9,8,128]{2,1,0:T(8,128)S(1)}, f32[9,8,128]{2,1,0:T(8,128)S(1)}, u32[]{:S(2)}, u32[]{:S(2)}) collective-permute-start(f32[9,8,128]{2,1,0:T(8,128)S(1)} %get-tuple-element.85), channel_id=1, source_target_pairs={{0,1},{1,2},{2,3},{3,0},{4,5},{5,6},{6,7},{7,4},{8,9},{9,10},{10,1... | collective-permute-start | bytes 110600 | tf_op jit(solution)/shard_map/ppermute | solution.py:537
  21.5 1.5 %collective-permute-start.9 = (f32[9,8,128]{2,1,0:T(8,128)S(1)}, f32[9,8,128]{2,1,0:T(8,128)S(1)}, u32[]{:S(2)}, u32[]{:S(2)}) collective-permute-start(f32[9,8,128]{2,1,0:T(8,128)S(1)} %get-tuple-element.88), channel_id=1, source_target_pairs={{0,3},{1,0},{2,1},{3,2},{4,7},{5,4},{6,5},{7,6},{8,11},{9,8},{10,9... | collective-permute-start | bytes 110600 | tf_op jit(solution)/shard_map/ppermute | solution.py:537
  23.0 1.1 %shard_map.45.refs_2_ = f32[18,2,8,256]{3,2,1,0:T(8,128)S(1)} custom-call(f32[2,4,18,2,8,256]{5,4,3,2,1,0:T(8,128)S(1)} %copy-done, f32[18,2,8,256]{3,2,1,0:T(8,128)S(1)} %get-tuple-element.81.gp.refs_1_), custom_call_target="tpu_custom_call" | custom-call | flops 30000000 | tf_op jit(solution)/shard_map/pallas_call | solution.py:507
  24.1 0.2 collective-permute-done.8.refs_6_
  24.3 0.0 collective-permute-done.7.refs_5_
  24.3 1.2 %collective-permute-done.6.refs_4_ = f32[18,8,256]{2,1,0:T(8,128)S(1)} collective-permute-done((f32[18,8,256]{2,1,0:T(8,128)S(1)}, f32[18,8,256]{2,1,0:T(8,128)S(1)}, u32[]{:S(2)}, u32[]{:S(2)}) %collective-permute-start.6) | collective-permute-done | bytes 147488 | tf_op jit(solution)/shard_map/ppermute | solution.py:537
  25.5 0.4 shard_map.46
  25.9 0.0 collective-permute-done.9.refs_6_
  25.9 0.6 shard_map.47
  26.5 2.1 %collective-permute-start.10 = (f32[12,8,256]{2,1,0:T(8,128)S(1)}, f32[12,8,256]{2,1,0:T(8,128)S(1)}, u32[]{:S(2)}, u32[]{:S(2)}) collective-permute-start(f32[12,8,256]{2,1,0:T(8,128)S(1)} %get-tuple-element.96), channel_id=1, source_target_pairs={{0,8},{8,0},{1,9},{9,1},{2,10},{10,2},{3,11},{11,3},{4,12},{12,4},... | collective-permute-start | bytes 294920 | tf_op jit(solution)/shard_map/ppermute | solution.py:537
  28.6 2.5 %collective-permute-start.11 = (f32[12,8,256]{2,1,0:T(8,128)S(1)}, f32[12,8,256]{2,1,0:T(8,128)S(1)}, u32[]{:S(2)}, u32[]{:S(2)}) collective-permute-start(f32[12,8,256]{2,1,0:T(8,128)S(1)} %get-tuple-element.97), channel_id=1, source_target_pairs={{0,248},{8,16},{16,8},{24,32},{32,24},{40,48},{48,40},{56,64},{64,... | collective-permute-start | bytes 294920 | tf_op jit(solution)/shard_map/ppermute | solution.py:537
  31.1 0.0 collective-permute-start.12
  31.1 1.2 %collective-permute-start.13 = (f32[6,8,128]{2,1,0:T(8,128)S(1)}, f32[6,8,128]{2,1,0:T(8,128)S(1)}, u32[]{:S(2)}, u32[]{:S(2)}) collective-permute-start(f32[6,8,128]{2,1,0:T(8,128)S(1)} %get-tuple-element.99), channel_id=1, source_target_pairs={{0,1},{1,2},{2,3},{3,0},{4,5},{5,6},{6,7},{7,4},{8,9},{9,10},{10,1... | collective-permute-start | bytes 73736 | tf_op jit(solution)/shard_map/ppermute | solution.py:537
  32.3 1.5 %collective-permute-start.14 = (f32[6,8,128]{2,1,0:T(8,128)S(1)}, f32[6,8,128]{2,1,0:T(8,128)S(1)}, u32[]{:S(2)}, u32[]{:S(2)}) collective-permute-start(f32[6,8,128]{2,1,0:T(8,128)S(1)} %get-tuple-element.104), channel_id=1, source_target_pairs={{0,3},{1,0},{2,1},{3,2},{4,7},{5,4},{6,5},{7,6},{8,11},{9,8},{10,9... | collective-permute-start | bytes 73736 | tf_op jit(solution)/shard_map/ppermute | solution.py:537
  33.8 1.1 %shard_map.48.refs_2_ = f32[18,2,8,256]{3,2,1,0:T(8,128)S(1)} custom-call(f32[2,4,18,2,8,256]{5,4,3,2,1,0:T(8,128)S(1)} %copy-done, f32[18,2,8,256]{3,2,1,0:T(8,128)S(1)} %get-tuple-element.95.gp.refs_1_), custom_call_target="tpu_custom_call" | custom-call | flops 30000000 | tf_op jit(solution)/shard_map/pallas_call | solution.py:507
  34.9 0.4 collective-permute-done.13.refs_6_
  35.3 0.0 collective-permute-done.10.refs_3_
  35.3 0.0 collective-permute-done.11.refs_4_
  35.3 0.4 shard_map.49
  35.8 0.5 shard_map.50
  36.3 2.5 %collective-permute-start.15 = (f32[12,8,256]{2,1,0:T(8,128)S(1)}, f32[12,8,256]{2,1,0:T(8,128)S(1)}, u32[]{:S(2)}, u32[]{:S(2)}) collective-permute-start(f32[12,8,256]{2,1,0:T(8,128)S(1)} %get-tuple-element.114), channel_id=1, source_target_pairs={{0,8},{8,0},{1,9},{9,1},{2,10},{10,2},{3,11},{11,3},{4,12},{12,4},... | collective-permute-start | bytes 294920 | tf_op jit(solution)/shard_map/ppermute | solution.py:537
  38.8 1.2 %collective-permute-start.16 = (f32[12,8,256]{2,1,0:T(8,128)S(1)}, f32[12,8,256]{2,1,0:T(8,128)S(1)}, u32[]{:S(2)}, u32[]{:S(2)}) collective-permute-start(f32[12,8,256]{2,1,0:T(8,128)S(1)} %get-tuple-element.115), channel_id=1, source_target_pairs={{0,248},{8,16},{16,8},{24,32},{32,24},{40,48},{48,40},{56,64},{64,... | collective-permute-start | bytes 294920 | tf_op jit(solution)/shard_map/ppermute | solution.py:537
  40.1 0.5 collective-permute-start.17
  40.6 0.8 %collective-permute-start.18 = (f32[6,8,128]{2,1,0:T(8,128)S(1)}, f32[6,8,128]{2,1,0:T(8,128)S(1)}, u32[]{:S(2)}, u32[]{:S(2)}) collective-permute-start(f32[6,8,128]{2,1,0:T(8,128)S(1)} %get-tuple-element.117), channel_id=1, source_target_pairs={{0,1},{1,2},{2,3},{3,0},{4,5},{5,6},{6,7},{7,4},{8,9},{9,10},{10,1... | collective-permute-start | bytes 73736 | tf_op jit(solution)/shard_map/ppermute | solution.py:537
  41.3 1.9 %collective-permute-start.19 = (f32[6,8,128]{2,1,0:T(8,128)S(1)}, f32[6,8,128]{2,1,0:T(8,128)S(1)}, u32[]{:S(2)}, u32[]{:S(2)}) collective-permute-start(f32[6,8,128]{2,1,0:T(8,128)S(1)} %get-tuple-element.122), channel_id=1, source_target_pairs={{0,3},{1,0},{2,1},{3,2},{4,7},{5,4},{6,5},{7,6},{8,11},{9,8},{10,9... | collective-permute-start | bytes 73736 | tf_op jit(solution)/shard_map/ppermute | solution.py:537
  43.2 1.7 %shard_map.51 = (f32[18,2,8,256]{3,2,1,0:T(8,128)S(1)}, f32[2,18,2,8,256]{4,3,2,1,0:T(8,128)}) custom-call(f32[2,4,18,2,8,256]{5,4,3,2,1,0:T(8,128)S(1)} %copy-done, f32[18,2,8,256]{3,2,1,0:T(8,128)S(1)} %get-tuple-element.112.gp), custom_call_target="tpu_custom_call" | custom-call | flops 30000000 | tf_op jit(solution)/shard_map/pallas_call | solution.py:507
  44.9 0.0 collective-permute-done.18.refs_6_
  44.9 0.0 collective-permute-done.15.refs_3_
  45.0 0.0 collective-permute-done.16.refs_4_
  45.0 0.5 shard_map.52
  45.5 0.5 shard_map.53
  46.0 0.1 broadcast_in_dim.9
  46.1 22.7 %all_to_all.5 = f32[256,1,128]{2,1,0:T(1,128)S(1)} all-to-all(f32[256,1,128]{2,1,0:T(1,128)S(1)} %broadcast_in_dim.9), channel_id=1, replica_groups=mesh['tz'=8,'tx'=2,'tc'=2,'gz'=2,'gy'=4] {'tz','tx','tc','gz','gy'}, dimensions={0} | all-to-all | bytes 262144 | tf_op jit(solution)/shard_map/all_to_all | solution.py:671
  68.8 0.7 %shard_map.54 = (f32[2,18,2,8,256]{4,3,2,1,0:T(8,128)}, f32[2,2]{1,0:T(2,128)}) custom-call(f32[32,8,128]{2,1,0:T(8,128)S(1)} %bitcast.2, f32[18,8,256]{2,1,0:T(8,128)S(1)} %get-tuple-element.131.gn, f32[18,8,256]{2,1,0:T(8,128)S(1)} %get-tuple-element.132.gf, f32[2,18,2,8,256]{4,3,2,1,0:T(8,128)} %get-tuple-element.133.begun), custom_call_target="tpu_custom_call", output_to_operand_aliasing={{0}: (3, {})} | custom-call | flops 1000 | tf_op jit(solution)/shard_map/pallas_call | solution.py:507
  (12 shorter events, 0.0 us)
Async XLA Ops:
  0.6 9.0 %copy-start = (f32[2,4,18,2,8,256]{5,4,3,2,1,0:T(8,128)S(1)}, f32[2,4,18,2,8,256]{5,4,3,2,1,0:T(8,128)}, u32[]{:S(2)}) copy-start(f32[2,4,18,2,8,256]{5,4,3,2,1,0:T(8,128)} %refs_0_.15) | copy-start | bytes 7077892
  0.6 9.0 %copy-start.1 = (f32[2,18,2,8,256]{4,3,2,1,0:T(8,128)S(1)}, f32[2,18,2,8,256]{4,3,2,1,0:T(8,128)}, u32[]{:S(2)}) copy-start(f32[2,18,2,8,256]{4,3,2,1,0:T(8,128)} %refs_1_.7) | copy-start | bytes 1769476
  2.3 9.0 %collective-permute-start = (f32[18,8,256]{2,1,0:T(8,128)S(1)}, f32[18,8,256]{2,1,0:T(8,128)S(1)}, u32[]{:S(2)}, u32[]{:S(2)}) collective-permute-start(f32[18,8,256]{2,1,0:T(8,128)S(1)} %get-tuple-element.69), channel_id=1, source_target_pairs={{0,8},{8,0},{1,9},{9,1},{2,10},{10,2},{3,11},{11,3},{4,12},{12,4},... | collective-permute-start | bytes 442376 | tf_op jit(solution)/shard_map/ppermute | solution.py:537
  5.6 5.7 %collective-permute-start.1 = (f32[12,8,256]{2,1,0:T(8,128)S(1)}, f32[12,8,256]{2,1,0:T(8,128)S(1)}, u32[]{:S(2)}, u32[]{:S(2)}) collective-permute-start(f32[12,8,256]{2,1,0:T(8,128)S(1)} %get-tuple-element.70), channel_id=1, source_target_pairs={{0,248},{8,16},{16,8},{24,32},{32,24},{40,48},{48,40},{56,64},{64,... | collective-permute-start | bytes 294920 | tf_op jit(solution)/shard_map/ppermute | solution.py:537
  6.6 4.3 %collective-permute-start.2 = (f32[12,8,128]{2,1,0:T(8,128)S(1)}, f32[12,8,128]{2,1,0:T(8,128)S(1)}, u32[]{:S(2)}, u32[]{:S(2)}) collective-permute-start(f32[12,8,128]{2,1,0:T(8,128)S(1)} %get-tuple-element.71), channel_id=1, source_target_pairs={{0,4},{4,0},{1,5},{5,1},{2,6},{6,2},{3,7},{7,3},{8,12},{12,8},{9,1... | collective-permute-start | bytes 147464 | tf_op jit(solution)/shard_map/ppermute | solution.py:537
  6.9 3.9 %collective-permute-start.3 = (f32[6,8,128]{2,1,0:T(8,128)S(1)}, f32[6,8,128]{2,1,0:T(8,128)S(1)}, u32[]{:S(2)}, u32[]{:S(2)}) collective-permute-start(f32[6,8,128]{2,1,0:T(8,128)S(1)} %get-tuple-element.72), channel_id=1, source_target_pairs={{0,1},{1,2},{2,3},{3,0},{4,5},{5,6},{6,7},{7,4},{8,9},{9,10},{10,1... | collective-permute-start | bytes 73736 | tf_op jit(solution)/shard_map/ppermute | solution.py:537
  8.2 3.5 %collective-permute-start.4 = (f32[6,8,128]{2,1,0:T(8,128)S(1)}, f32[6,8,128]{2,1,0:T(8,128)S(1)}, u32[]{:S(2)}, u32[]{:S(2)}) collective-permute-start(f32[6,8,128]{2,1,0:T(8,128)S(1)} %get-tuple-element.75), channel_id=1, source_target_pairs={{0,3},{1,0},{2,1},{3,2},{4,7},{5,4},{6,5},{7,6},{8,11},{9,8},{10,9... | collective-permute-start | bytes 73736 | tf_op jit(solution)/shard_map/ppermute | solution.py:537
  12.4 11.9 %collective-permute-start.5 = (f32[18,8,256]{2,1,0:T(8,128)S(1)}, f32[18,8,256]{2,1,0:T(8,128)S(1)}, u32[]{:S(2)}, u32[]{:S(2)}) collective-permute-start(f32[18,8,256]{2,1,0:T(8,128)S(1)} %get-tuple-element.82), channel_id=1, source_target_pairs={{0,8},{8,0},{1,9},{9,1},{2,10},{10,2},{3,11},{11,3},{4,12},{12,4},... | collective-permute-start | bytes 442376 | tf_op jit(solution)/shard_map/ppermute | solution.py:537
  19.1 6.4 %collective-permute-start.6 = (f32[18,8,256]{2,1,0:T(8,128)S(1)}, f32[18,8,256]{2,1,0:T(8,128)S(1)}, u32[]{:S(2)}, u32[]{:S(2)}) collective-permute-start(f32[18,8,256]{2,1,0:T(8,128)S(1)} %get-tuple-element.83), channel_id=1, source_target_pairs={{0,248},{8,16},{16,8},{24,32},{32,24},{40,48},{48,40},{56,64},{64,... | collective-permute-start | bytes 442376 | tf_op jit(solution)/shard_map/ppermute | solution.py:537
  19.1 5.2 %collective-permute-start.7 = (f32[18,8,128]{2,1,0:T(8,128)S(1)}, f32[18,8,128]{2,1,0:T(8,128)S(1)}, u32[]{:S(2)}, u32[]{:S(2)}) collective-permute-start(f32[18,8,128]{2,1,0:T(8,128)S(1)} %get-tuple-element.84), channel_id=1, source_target_pairs={{0,4},{4,0},{1,5},{5,1},{2,6},{6,2},{3,7},{7,3},{8,12},{12,8},{9,1... | collective-permute-start | bytes 221192 | tf_op jit(solution)/shard_map/ppermute | solution.py:537
  20.3 4.0 %collective-permute-start.8 = (f32[9,8,128]{2,1,0:T(8,128)S(1)}, f32[9,8,128]{2,1,0:T(8,128)S(1)}, u32[]{:S(2)}, u32[]{:S(2)}) collective-permute-start(f32[9,8,128]{2,1,0:T(8,128)S(1)} %get-tuple-element.85), channel_id=1, source_target_pairs={{0,1},{1,2},{2,3},{3,0},{4,5},{5,6},{6,7},{7,4},{8,9},{9,10},{10,1... | collective-permute-start | bytes 110600 | tf_op jit(solution)/shard_map/ppermute | solution.py:537
  21.5 4.5 %collective-permute-start.9 = (f32[9,8,128]{2,1,0:T(8,128)S(1)}, f32[9,8,128]{2,1,0:T(8,128)S(1)}, u32[]{:S(2)}, u32[]{:S(2)}) collective-permute-start(f32[9,8,128]{2,1,0:T(8,128)S(1)} %get-tuple-element.88), channel_id=1, source_target_pairs={{0,3},{1,0},{2,1},{3,2},{4,7},{5,4},{6,5},{7,6},{8,11},{9,8},{10,9... | collective-permute-start | bytes 110600 | tf_op jit(solution)/shard_map/ppermute | solution.py:537
  26.5 8.8 %collective-permute-start.10 = (f32[12,8,256]{2,1,0:T(8,128)S(1)}, f32[12,8,256]{2,1,0:T(8,128)S(1)}, u32[]{:S(2)}, u32[]{:S(2)}) collective-permute-start(f32[12,8,256]{2,1,0:T(8,128)S(1)} %get-tuple-element.96), channel_id=1, source_target_pairs={{0,8},{8,0},{1,9},{9,1},{2,10},{10,2},{3,11},{11,3},{4,12},{12,4},... | collective-permute-start | bytes 294920 | tf_op jit(solution)/shard_map/ppermute | solution.py:537
  28.6 6.7 %collective-permute-start.11 = (f32[12,8,256]{2,1,0:T(8,128)S(1)}, f32[12,8,256]{2,1,0:T(8,128)S(1)}, u32[]{:S(2)}, u32[]{:S(2)}) collective-permute-start(f32[12,8,256]{2,1,0:T(8,128)S(1)} %get-tuple-element.97), channel_id=1, source_target_pairs={{0,248},{8,16},{16,8},{24,32},{32,24},{40,48},{48,40},{56,64},{64,... | collective-permute-start | bytes 294920 | tf_op jit(solution)/shard_map/ppermute | solution.py:537
  31.1 4.2 %collective-permute-start.12 = (f32[12,8,128]{2,1,0:T(8,128)S(1)}, f32[12,8,128]{2,1,0:T(8,128)S(1)}, u32[]{:S(2)}, u32[]{:S(2)}) collective-permute-start(f32[12,8,128]{2,1,0:T(8,128)S(1)} %get-tuple-element.98), channel_id=1, source_target_pairs={{0,4},{4,0},{1,5},{5,1},{2,6},{6,2},{3,7},{7,3},{8,12},{12,8},{9,1... | collective-permute-start | bytes 147464 | tf_op jit(solution)/shard_map/ppermute | solution.py:537
  31.1 4.2 %collective-permute-start.13 = (f32[6,8,128]{2,1,0:T(8,128)S(1)}, f32[6,8,128]{2,1,0:T(8,128)S(1)}, u32[]{:S(2)}, u32[]{:S(2)}) collective-permute-start(f32[6,8,128]{2,1,0:T(8,128)S(1)} %get-tuple-element.99), channel_id=1, source_target_pairs={{0,1},{1,2},{2,3},{3,0},{4,5},{5,6},{6,7},{7,4},{8,9},{9,10},{10,1... | collective-permute-start | bytes 73736 | tf_op jit(solution)/shard_map/ppermute | solution.py:537
  32.3 3.5 %collective-permute-start.14 = (f32[6,8,128]{2,1,0:T(8,128)S(1)}, f32[6,8,128]{2,1,0:T(8,128)S(1)}, u32[]{:S(2)}, u32[]{:S(2)}) collective-permute-start(f32[6,8,128]{2,1,0:T(8,128)S(1)} %get-tuple-element.104), channel_id=1, source_target_pairs={{0,3},{1,0},{2,1},{3,2},{4,7},{5,4},{6,5},{7,6},{8,11},{9,8},{10,9... | collective-permute-start | bytes 73736 | tf_op jit(solution)/shard_map/ppermute | solution.py:537
  36.3 8.7 %collective-permute-start.15 = (f32[12,8,256]{2,1,0:T(8,128)S(1)}, f32[12,8,256]{2,1,0:T(8,128)S(1)}, u32[]{:S(2)}, u32[]{:S(2)}) collective-permute-start(f32[12,8,256]{2,1,0:T(8,128)S(1)} %get-tuple-element.114), channel_id=1, source_target_pairs={{0,8},{8,0},{1,9},{9,1},{2,10},{10,2},{3,11},{11,3},{4,12},{12,4},... | collective-permute-start | bytes 294920 | tf_op jit(solution)/shard_map/ppermute | solution.py:537
  38.8 6.1 %collective-permute-start.16 = (f32[12,8,256]{2,1,0:T(8,128)S(1)}, f32[12,8,256]{2,1,0:T(8,128)S(1)}, u32[]{:S(2)}, u32[]{:S(2)}) collective-permute-start(f32[12,8,256]{2,1,0:T(8,128)S(1)} %get-tuple-element.115), channel_id=1, source_target_pairs={{0,248},{8,16},{16,8},{24,32},{32,24},{40,48},{48,40},{56,64},{64,... | collective-permute-start | bytes 294920 | tf_op jit(solution)/shard_map/ppermute | solution.py:537
  40.1 4.9 %collective-permute-start.17 = (f32[12,8,128]{2,1,0:T(8,128)S(1)}, f32[12,8,128]{2,1,0:T(8,128)S(1)}, u32[]{:S(2)}, u32[]{:S(2)}) collective-permute-start(f32[12,8,128]{2,1,0:T(8,128)S(1)} %get-tuple-element.116), channel_id=1, source_target_pairs={{0,4},{4,0},{1,5},{5,1},{2,6},{6,2},{3,7},{7,3},{8,12},{12,8},{9,1... | collective-permute-start | bytes 147464 | tf_op jit(solution)/shard_map/ppermute | solution.py:537
  40.6 4.4 %collective-permute-start.18 = (f32[6,8,128]{2,1,0:T(8,128)S(1)}, f32[6,8,128]{2,1,0:T(8,128)S(1)}, u32[]{:S(2)}, u32[]{:S(2)}) collective-permute-start(f32[6,8,128]{2,1,0:T(8,128)S(1)} %get-tuple-element.117), channel_id=1, source_target_pairs={{0,1},{1,2},{2,3},{3,0},{4,5},{5,6},{6,7},{7,4},{8,9},{9,10},{10,1... | collective-permute-start | bytes 73736 | tf_op jit(solution)/shard_map/ppermute | solution.py:537
  41.3 4.1 %collective-permute-start.19 = (f32[6,8,128]{2,1,0:T(8,128)S(1)}, f32[6,8,128]{2,1,0:T(8,128)S(1)}, u32[]{:S(2)}, u32[]{:S(2)}) collective-permute-start(f32[6,8,128]{2,1,0:T(8,128)S(1)} %get-tuple-element.122), channel_id=1, source_target_pairs={{0,3},{1,0},{2,1},{3,2},{4,7},{5,4},{6,5},{7,6},{8,11},{9,8},{10,9... | collective-permute-start | bytes 73736 | tf_op jit(solution)/shard_map/ppermute | solution.py:537

commit v6 on v5

--- a/solution.py
+++ b/solution.py
@@ -34,8 +34,9 @@
     return pl.ds(128 * h, 128)
 
 
-def three_products(left, right, sign):
-    out = [[None] * 9 for _ in R3]
+def three_products(left, right, sign, out=None):
+    if out is None:
+        out = [[None] * 9 for _ in R3]
     for k in R3:
         lr = [left(i, k, 0) for i in R3]
         li = [left(i, k, 1) for i in R3]
@@ -52,10 +53,16 @@
     return out
 
 
-def times_adjoint(acc, left, right):
-    p, q, s = three_products(
-        lambda i, k, n: left(9 * n + re(i, k)), lambda j, k, n: right(9 * n + re(j, k)), -1
-    )
+def times_adjoint(acc, *pairs):
+    sums = None
+    for left, right in zip(pairs[::2], pairs[1::2]):
+        sums = three_products(
+            lambda i, k, n: left(9 * n + re(i, k)),
+            lambda j, k, n: right(9 * n + re(j, k)),
+            -1,
+            sums,
+        )
+    p, q, s = sums
     out = [x + y for x, y in zip(p, q)] + [z - (x - y) for x, y, z in zip(p, q, s)]
     return [v if a is None else a + v for a, v in zip(acc, out)]
 
@@ -315,7 +322,6 @@
                 moved = jnp.where(column == 31, pltpu.roll(v, 31, 1), pltpu.roll(v, 127, 1))
                 return jnp.where(stays, v, moved)
 
-            acc = times_adjoint(acc, lambda c: own[0, c, s, :, half(h)], ahead_x)
 
             def ahead_y(c):
                 a = pltpu.roll(gp[c, s, :, half(1)], 96, 1)
@@ -323,12 +329,16 @@
                     return jnp.where(lane >= 96, a, pltpu.roll(tile(c), 96, 1))
                 return jnp.where(lane >= 96, 0.0, a)
 
-            acc = times_adjoint(acc, lambda c: own[1, c, s, :, half(h)], ahead_y)
 
             def ahead_z(c):
                 return jnp.where(row == 7, 0.0, pltpu.roll(tile(c), 7, 0))
 
-            acc = times_adjoint(acc, lambda c: own[2, c, s, :, half(h)], ahead_z)
+            ahead = []
+            for mu, value in enumerate((ahead_x, ahead_y, ahead_z)):
+                ahead += [lambda c, mu=mu: own[mu, c, s, :, half(h)], value]
+            if s == 0:
+                ahead += [lambda c: own[3, c, 0, :, half(h)], lambda c: gp[c, 1, :, half(h)]]
+            acc = times_adjoint(acc, *ahead)
             back = times(tile, lambda c: other[0, c, s, :, half(h)])
             shifted = []
             for v in back:
@@ -337,13 +347,7 @@
             acc = plus_adjoint(acc, shifted)
             back = times(tile, lambda c: other[2, c, s, :, half(h)])
             acc = plus_adjoint(acc, [jnp.where(row == 0, 0.0, pltpu.roll(v, 1, 0)) for v in back])
-            if s == 0:
-                acc = times_adjoint(
-                    acc,
-                    lambda c: own[3, c, 0, :, half(h)],
-                    lambda c: gp[c, 1, :, half(h)],
-                )
-            else:
+            if s == 1:
                 back = times(
                     lambda c: gp[c, 0, :, half(h)], lambda c: other[3, c, 0, :, half(h)]
                 )

time: 69.8 us -> 69.8 us (level)
  transfers between devices with their start and end apart: 20 -> 20, of which waited for: 4 -> 5; matrix products, arithmetic and copies ran while one was open for 0% -> 0% of each run, Pallas kernels for 10% -> 9%
where the time goes in v6:
time: 69.8 us; the launch traced here: 69.7 us
  starting transfers between devices  32.1 us (46%)
  blocking collectives  22.7 us (33%)
  Pallas kernels  11.2 us (16%)
  waiting for transfers between devices  2.57 us (4%)
  between operations  0.97 us (1%)
    ppermute x20, starting transfers between devices, swap(): lax.ppermute(value, axis, [(i, partner(i) % count) for i in range(count)])  32.1 us
    all_to_all x1, blocking collectives, shards(): lax.all_to_all(parts, AXES, 0, 0, tiled=True).reshape(count // 8, 8, 128)  22.7 us
    pallas_call x14, Pallas kernels, call(): pl.pallas_call(body, out_shape=[jax.ShapeDtypeStruct(o, F32) for o in out...  11.2 us
    ppermute x20, waiting for transfers between devices, swap(): lax.ppermute(value, axis, [(i, partner(i) % count) for i in range(count)])  2.57 us
  transfers between devices with their start and end apart: 20, of which 5 were waited for; matrix products, arithmetic and copies ran while one was open for 0% of the time, Pallas kernels for 9%

profile of v6, /device:TPU:1, one launch (start us, length us, event | category | flops | bytes accessed | tf_op | source)
XLA Modules:
  0.0 69.7 jit_solution(5378050859183289869)
XLA Ops:
  0.6 1.6 %shard_map.42 = (f32[18,8,256]{2,1,0:T(8,128)S(1)}, f32[12,8,256]{2,1,0:T(8,128)S(1)}, f32[12,8,128]{2,1,0:T(8,128)S(1)}, f32[6,8,128]{2,1,0:T(8,128)S(1)}, f32[...) custom-call(f32[2,4,18,2,8,256]{5,4,3,2,1,0:T(8,128)} %refs_0_.15, ...), custom_call_target="tpu_custom_call" | custom-call | flops 10000000 | tf_op jit(solution)/shard_map/pallas_call | solution.py:511
  2.3 3.3 %collective-permute-start = (f32[18,8,256]{2,1,0:T(8,128)S(1)}, f32[18,8,256]{2,1,0:T(8,128)S(1)}, u32[]{:S(2)}, u32[]{:S(2)}) collective-permute-start(f32[18,8,256]{2,1,0:T(8,128)S(1)} %get-tuple-element.69), channel_id=1, source_target_pairs={{0,8},{8,0},{1,9},{9,1},{2,10},{10,2},{3,11},{11,3},{4,12},{12,4},... | collective-permute-start | bytes 442376 | tf_op jit(solution)/shard_map/ppermute | solution.py:541
  5.6 1.0 %collective-permute-start.1 = (f32[12,8,256]{2,1,0:T(8,128)S(1)}, f32[12,8,256]{2,1,0:T(8,128)S(1)}, u32[]{:S(2)}, u32[]{:S(2)}) collective-permute-start(f32[12,8,256]{2,1,0:T(8,128)S(1)} %get-tuple-element.70), channel_id=1, source_target_pairs={{0,248},{8,16},{16,8},{24,32},{32,24},{40,48},{48,40},{56,64},{64,... | collective-permute-start | bytes 294920 | tf_op jit(solution)/shard_map/ppermute | solution.py:541
  6.6 0.3 collective-permute-start.2
  6.9 1.3 %collective-permute-start.3 = (f32[6,8,128]{2,1,0:T(8,128)S(1)}, f32[6,8,128]{2,1,0:T(8,128)S(1)}, u32[]{:S(2)}, u32[]{:S(2)}) collective-permute-start(f32[6,8,128]{2,1,0:T(8,128)S(1)} %get-tuple-element.72), channel_id=1, source_target_pairs={{0,1},{1,2},{2,3},{3,0},{4,5},{5,6},{6,7},{7,4},{8,9},{9,10},{10,1... | collective-permute-start | bytes 73736 | tf_op jit(solution)/shard_map/ppermute | solution.py:541
  8.2 1.4 %collective-permute-start.4 = (f32[6,8,128]{2,1,0:T(8,128)S(1)}, f32[6,8,128]{2,1,0:T(8,128)S(1)}, u32[]{:S(2)}, u32[]{:S(2)}) collective-permute-start(f32[6,8,128]{2,1,0:T(8,128)S(1)} %get-tuple-element.75), channel_id=1, source_target_pairs={{0,3},{1,0},{2,1},{3,2},{4,7},{5,4},{6,5},{7,6},{8,11},{9,8},{10,9... | collective-permute-start | bytes 73736 | tf_op jit(solution)/shard_map/ppermute | solution.py:541
  9.6 1.1 %shard_map.41 = (f32[18,2,8,256]{3,2,1,0:T(8,128)S(1)}, f32[18,8,128]{2,1,0:T(8,128)S(1)}, f32[18,8,128]{2,1,0:T(8,128)S(1)}) custom-call(f32[2,4,18,2,8,256]{5,4,3,2,1,0:T(8,128)S(1)} %copy-done, f32[2,18,2,8,256]{4,3,2,1,0:T(8,128)S(1)} %copy-done.1), custom_call_target="tpu_custom_call" | custom-call | flops 30000000 | tf_op jit(solution)/shard_map/pallas_call | solution.py:511
  10.7 0.1 collective-permute-done.3.refs_6_
  10.8 0.0 collective-permute-done.2.refs_5_
  10.8 0.4 collective-permute-done.1.refs_4_
  11.3 0.0 collective-permute-done.refs_3_
  11.3 0.4 shard_map.43
  11.7 0.7 shard_map.44
  12.4 6.7 %collective-permute-start.5 = (f32[18,8,256]{2,1,0:T(8,128)S(1)}, f32[18,8,256]{2,1,0:T(8,128)S(1)}, u32[]{:S(2)}, u32[]{:S(2)}) collective-permute-start(f32[18,8,256]{2,1,0:T(8,128)S(1)} %get-tuple-element.82), channel_id=1, source_target_pairs={{0,8},{8,0},{1,9},{9,1},{2,10},{10,2},{3,11},{11,3},{4,12},{12,4},... | collective-permute-start | bytes 442376 | tf_op jit(solution)/shard_map/ppermute | solution.py:541
  19.1 1.2 %collective-permute-start.7 = (f32[18,8,128]{2,1,0:T(8,128)S(1)}, f32[18,8,128]{2,1,0:T(8,128)S(1)}, u32[]{:S(2)}, u32[]{:S(2)}) collective-permute-start(f32[18,8,128]{2,1,0:T(8,128)S(1)} %get-tuple-element.84), channel_id=1, source_target_pairs={{0,4},{4,0},{1,5},{5,1},{2,6},{6,2},{3,7},{7,3},{8,12},{12,8},{9,1... | collective-permute-start | bytes 221192 | tf_op jit(solution)/shard_map/ppermute | solution.py:541
  20.3 1.2 %collective-permute-start.8 = (f32[9,8,128]{2,1,0:T(8,128)S(1)}, f32[9,8,128]{2,1,0:T(8,128)S(1)}, u32[]{:S(2)}, u32[]{:S(2)}) collective-permute-start(f32[9,8,128]{2,1,0:T(8,128)S(1)} %get-tuple-element.85), channel_id=1, source_target_pairs={{0,1},{1,2},{2,3},{3,0},{4,5},{5,6},{6,7},{7,4},{8,9},{9,10},{10,1... | collective-permute-start | bytes 110600 | tf_op jit(solution)/shard_map/ppermute | solution.py:541
  21.5 1.5 %collective-permute-start.9 = (f32[9,8,128]{2,1,0:T(8,128)S(1)}, f32[9,8,128]{2,1,0:T(8,128)S(1)}, u32[]{:S(2)}, u32[]{:S(2)}) collective-permute-start(f32[9,8,128]{2,1,0:T(8,128)S(1)} %get-tuple-element.88), channel_id=1, source_target_pairs={{0,3},{1,0},{2,1},{3,2},{4,7},{5,4},{6,5},{7,6},{8,11},{9,8},{10,9... | collective-permute-start | bytes 110600 | tf_op jit(solution)/shard_map/ppermute | solution.py:541
  23.0 1.0 %shard_map.45.refs_2_ = f32[18,2,8,256]{3,2,1,0:T(8,128)S(1)} custom-call(f32[2,4,18,2,8,256]{5,4,3,2,1,0:T(8,128)S(1)} %copy-done, f32[18,2,8,256]{3,2,1,0:T(8,128)S(1)} %get-tuple-element.81.gp.refs_1_), custom_call_target="tpu_custom_call" | custom-call | flops 30000000 | tf_op jit(solution)/shard_map/pallas_call | solution.py:511
  24.0 0.3 collective-permute-done.8.refs_6_
  24.3 0.0 collective-permute-done.7.refs_5_
  24.3 1.2 %collective-permute-done.6.refs_4_ = f32[18,8,256]{2,1,0:T(8,128)S(1)} collective-permute-done((f32[18,8,256]{2,1,0:T(8,128)S(1)}, f32[18,8,256]{2,1,0:T(8,128)S(1)}, u32[]{:S(2)}, u32[]{:S(2)}) %collective-permute-start.6) | collective-permute-done | bytes 147488 | tf_op jit(solution)/shard_map/ppermute | solution.py:541
  25.5 0.4 shard_map.46
  25.9 0.0 collective-permute-done.9.refs_6_
  25.9 0.6 shard_map.47
  26.5 2.1 %collective-permute-start.10 = (f32[12,8,256]{2,1,0:T(8,128)S(1)}, f32[12,8,256]{2,1,0:T(8,128)S(1)}, u32[]{:S(2)}, u32[]{:S(2)}) collective-permute-start(f32[12,8,256]{2,1,0:T(8,128)S(1)} %get-tuple-element.96), channel_id=1, source_target_pairs={{0,8},{8,0},{1,9},{9,1},{2,10},{10,2},{3,11},{11,3},{4,12},{12,4},... | collective-permute-start | bytes 294920 | tf_op jit(solution)/shard_map/ppermute | solution.py:541
  28.6 2.5 %collective-permute-start.11 = (f32[12,8,256]{2,1,0:T(8,128)S(1)}, f32[12,8,256]{2,1,0:T(8,128)S(1)}, u32[]{:S(2)}, u32[]{:S(2)}) collective-permute-start(f32[12,8,256]{2,1,0:T(8,128)S(1)} %get-tuple-element.97), channel_id=1, source_target_pairs={{0,248},{8,16},{16,8},{24,32},{32,24},{40,48},{48,40},{56,64},{64,... | collective-permute-start | bytes 294920 | tf_op jit(solution)/shard_map/ppermute | solution.py:541
  31.1 0.0 collective-permute-start.12
  31.1 1.2 %collective-permute-start.13 = (f32[6,8,128]{2,1,0:T(8,128)S(1)}, f32[6,8,128]{2,1,0:T(8,128)S(1)}, u32[]{:S(2)}, u32[]{:S(2)}) collective-permute-start(f32[6,8,128]{2,1,0:T(8,128)S(1)} %get-tuple-element.99), channel_id=1, source_target_pairs={{0,1},{1,2},{2,3},{3,0},{4,5},{5,6},{6,7},{7,4},{8,9},{9,10},{10,1... | collective-permute-start | bytes 73736 | tf_op jit(solution)/shard_map/ppermute | solution.py:541
  32.3 1.5 %collective-permute-start.14 = (f32[6,8,128]{2,1,0:T(8,128)S(1)}, f32[6,8,128]{2,1,0:T(8,128)S(1)}, u32[]{:S(2)}, u32[]{:S(2)}) collective-permute-start(f32[6,8,128]{2,1,0:T(8,128)S(1)} %get-tuple-element.104), channel_id=1, source_target_pairs={{0,3},{1,0},{2,1},{3,2},{4,7},{5,4},{6,5},{7,6},{8,11},{9,8},{10,9... | collective-permute-start | bytes 73736 | tf_op jit(solution)/shard_map/ppermute | solution.py:541
  33.8 1.0 %shard_map.48.refs_2_ = f32[18,2,8,256]{3,2,1,0:T(8,128)S(1)} custom-call(f32[2,4,18,2,8,256]{5,4,3,2,1,0:T(8,128)S(1)} %copy-done, f32[18,2,8,256]{3,2,1,0:T(8,128)S(1)} %get-tuple-element.95.gp.refs_1_), custom_call_target="tpu_custom_call" | custom-call | flops 30000000 | tf_op jit(solution)/shard_map/pallas_call | solution.py:511
  34.8 0.5 collective-permute-done.13.refs_6_
  35.3 0.0 collective-permute-done.10.refs_3_
  35.3 0.0 collective-permute-done.11.refs_4_
  35.3 0.4 shard_map.49
  35.8 0.5 shard_map.50
  36.3 2.5 %collective-permute-start.15 = (f32[12,8,256]{2,1,0:T(8,128)S(1)}, f32[12,8,256]{2,1,0:T(8,128)S(1)}, u32[]{:S(2)}, u32[]{:S(2)}) collective-permute-start(f32[12,8,256]{2,1,0:T(8,128)S(1)} %get-tuple-element.114), channel_id=1, source_target_pairs={{0,8},{8,0},{1,9},{9,1},{2,10},{10,2},{3,11},{11,3},{4,12},{12,4},... | collective-permute-start | bytes 294920 | tf_op jit(solution)/shard_map/ppermute | solution.py:541
  38.8 1.2 %collective-permute-start.16 = (f32[12,8,256]{2,1,0:T(8,128)S(1)}, f32[12,8,256]{2,1,0:T(8,128)S(1)}, u32[]{:S(2)}, u32[]{:S(2)}) collective-permute-start(f32[12,8,256]{2,1,0:T(8,128)S(1)} %get-tuple-element.115), channel_id=1, source_target_pairs={{0,248},{8,16},{16,8},{24,32},{32,24},{40,48},{48,40},{56,64},{64,... | collective-permute-start | bytes 294920 | tf_op jit(solution)/shard_map/ppermute | solution.py:541
  40.1 0.5 collective-permute-start.17
  40.6 0.8 %collective-permute-start.18 = (f32[6,8,128]{2,1,0:T(8,128)S(1)}, f32[6,8,128]{2,1,0:T(8,128)S(1)}, u32[]{:S(2)}, u32[]{:S(2)}) collective-permute-start(f32[6,8,128]{2,1,0:T(8,128)S(1)} %get-tuple-element.117), channel_id=1, source_target_pairs={{0,1},{1,2},{2,3},{3,0},{4,5},{5,6},{6,7},{7,4},{8,9},{9,10},{10,1... | collective-permute-start | bytes 73736 | tf_op jit(solution)/shard_map/ppermute | solution.py:541
  41.3 1.9 %collective-permute-start.19 = (f32[6,8,128]{2,1,0:T(8,128)S(1)}, f32[6,8,128]{2,1,0:T(8,128)S(1)}, u32[]{:S(2)}, u32[]{:S(2)}) collective-permute-start(f32[6,8,128]{2,1,0:T(8,128)S(1)} %get-tuple-element.122), channel_id=1, source_target_pairs={{0,3},{1,0},{2,1},{3,2},{4,7},{5,4},{6,5},{7,6},{8,11},{9,8},{10,9... | collective-permute-start | bytes 73736 | tf_op jit(solution)/shard_map/ppermute | solution.py:541
  43.2 1.6 %shard_map.51 = (f32[18,2,8,256]{3,2,1,0:T(8,128)S(1)}, f32[2,18,2,8,256]{4,3,2,1,0:T(8,128)}) custom-call(f32[2,4,18,2,8,256]{5,4,3,2,1,0:T(8,128)S(1)} %copy-done, f32[18,2,8,256]{3,2,1,0:T(8,128)S(1)} %get-tuple-element.112.gp), custom_call_target="tpu_custom_call" | custom-call | flops 30000000 | tf_op jit(solution)/shard_map/pallas_call | solution.py:511
  44.9 0.0 collective-permute-done.17.refs_5_
  44.9 0.0 collective-permute-done.15.refs_3_
  44.9 0.5 shard_map.52
  45.4 0.5 shard_map.53
  45.9 0.1 broadcast_in_dim.9
  46.0 22.7 %all_to_all.5 = f32[256,1,128]{2,1,0:T(1,128)S(1)} all-to-all(f32[256,1,128]{2,1,0:T(1,128)S(1)} %broadcast_in_dim.9), channel_id=1, replica_groups=mesh['tz'=8,'tx'=2,'tc'=2,'gz'=2,'gy'=4] {'tz','tx','tc','gz','gy'}, dimensions={0} | all-to-all | bytes 262144 | tf_op jit(solution)/shard_map/all_to_all | solution.py:675
  68.8 0.7 %shard_map.54 = (f32[2,18,2,8,256]{4,3,2,1,0:T(8,128)}, f32[2,2]{1,0:T(2,128)}) custom-call(f32[32,8,128]{2,1,0:T(8,128)S(1)} %bitcast.2, f32[18,8,256]{2,1,0:T(8,128)S(1)} %get-tuple-element.131.gn, f32[18,8,256]{2,1,0:T(8,128)S(1)} %get-tuple-element.132.gf, f32[2,18,2,8,256]{4,3,2,1,0:T(8,128)} %get-tuple-element.133.begun), custom_call_target="tpu_custom_call", output_to_operand_aliasing={{0}: (3, {})} | custom-call | flops 1000 | tf_op jit(solution)/shard_map/pallas_call | solution.py:511
  (12 shorter events, 0.0 us)
Async XLA Ops:
  0.6 9.0 %copy-start = (f32[2,4,18,2,8,256]{5,4,3,2,1,0:T(8,128)S(1)}, f32[2,4,18,2,8,256]{5,4,3,2,1,0:T(8,128)}, u32[]{:S(2)}) copy-start(f32[2,4,18,2,8,256]{5,4,3,2,1,0:T(8,128)} %refs_0_.15) | copy-start | bytes 7077892
  0.6 9.0 %copy-start.1 = (f32[2,18,2,8,256]{4,3,2,1,0:T(8,128)S(1)}, f32[2,18,2,8,256]{4,3,2,1,0:T(8,128)}, u32[]{:S(2)}) copy-start(f32[2,18,2,8,256]{4,3,2,1,0:T(8,128)} %refs_1_.7) | copy-start | bytes 1769476
  2.3 9.0 %collective-permute-start = (f32[18,8,256]{2,1,0:T(8,128)S(1)}, f32[18,8,256]{2,1,0:T(8,128)S(1)}, u32[]{:S(2)}, u32[]{:S(2)}) collective-permute-start(f32[18,8,256]{2,1,0:T(8,128)S(1)} %get-tuple-element.69), channel_id=1, source_target_pairs={{0,8},{8,0},{1,9},{9,1},{2,10},{10,2},{3,11},{11,3},{4,12},{12,4},... | collective-permute-start | bytes 442376 | tf_op jit(solution)/shard_map/ppermute | solution.py:541
  5.6 5.7 %collective-permute-start.1 = (f32[12,8,256]{2,1,0:T(8,128)S(1)}, f32[12,8,256]{2,1,0:T(8,128)S(1)}, u32[]{:S(2)}, u32[]{:S(2)}) collective-permute-start(f32[12,8,256]{2,1,0:T(8,128)S(1)} %get-tuple-element.70), channel_id=1, source_target_pairs={{0,248},{8,16},{16,8},{24,32},{32,24},{40,48},{48,40},{56,64},{64,... | collective-permute-start | bytes 294920 | tf_op jit(solution)/shard_map/ppermute | solution.py:541
  6.6 4.3 %collective-permute-start.2 = (f32[12,8,128]{2,1,0:T(8,128)S(1)}, f32[12,8,128]{2,1,0:T(8,128)S(1)}, u32[]{:S(2)}, u32[]{:S(2)}) collective-permute-start(f32[12,8,128]{2,1,0:T(8,128)S(1)} %get-tuple-element.71), channel_id=1, source_target_pairs={{0,4},{4,0},{1,5},{5,1},{2,6},{6,2},{3,7},{7,3},{8,12},{12,8},{9,1... | collective-permute-start | bytes 147464 | tf_op jit(solution)/shard_map/ppermute | solution.py:541
  6.9 3.9 %collective-permute-start.3 = (f32[6,8,128]{2,1,0:T(8,128)S(1)}, f32[6,8,128]{2,1,0:T(8,128)S(1)}, u32[]{:S(2)}, u32[]{:S(2)}) collective-permute-start(f32[6,8,128]{2,1,0:T(8,128)S(1)} %get-tuple-element.72), channel_id=1, source_target_pairs={{0,1},{1,2},{2,3},{3,0},{4,5},{5,6},{6,7},{7,4},{8,9},{9,10},{10,1... | collective-permute-start | bytes 73736 | tf_op jit(solution)/shard_map/ppermute | solution.py:541
  8.2 3.5 %collective-permute-start.4 = (f32[6,8,128]{2,1,0:T(8,128)S(1)}, f32[6,8,128]{2,1,0:T(8,128)S(1)}, u32[]{:S(2)}, u32[]{:S(2)}) collective-permute-start(f32[6,8,128]{2,1,0:T(8,128)S(1)} %get-tuple-element.75), channel_id=1, source_target_pairs={{0,3},{1,0},{2,1},{3,2},{4,7},{5,4},{6,5},{7,6},{8,11},{9,8},{10,9... | collective-permute-start | bytes 73736 | tf_op jit(solution)/shard_map/ppermute | solution.py:541
  12.4 11.9 %collective-permute-start.5 = (f32[18,8,256]{2,1,0:T(8,128)S(1)}, f32[18,8,256]{2,1,0:T(8,128)S(1)}, u32[]{:S(2)}, u32[]{:S(2)}) collective-permute-start(f32[18,8,256]{2,1,0:T(8,128)S(1)} %get-tuple-element.82), channel_id=1, source_target_pairs={{0,8},{8,0},{1,9},{9,1},{2,10},{10,2},{3,11},{11,3},{4,12},{12,4},... | collective-permute-start | bytes 442376 | tf_op jit(solution)/shard_map/ppermute | solution.py:541
  19.1 6.4 %collective-permute-start.6 = (f32[18,8,256]{2,1,0:T(8,128)S(1)}, f32[18,8,256]{2,1,0:T(8,128)S(1)}, u32[]{:S(2)}, u32[]{:S(2)}) collective-permute-start(f32[18,8,256]{2,1,0:T(8,128)S(1)} %get-tuple-element.83), channel_id=1, source_target_pairs={{0,248},{8,16},{16,8},{24,32},{32,24},{40,48},{48,40},{56,64},{64,... | collective-permute-start | bytes 442376 | tf_op jit(solution)/shard_map/ppermute | solution.py:541
  19.1 5.2 %collective-permute-start.7 = (f32[18,8,128]{2,1,0:T(8,128)S(1)}, f32[18,8,128]{2,1,0:T(8,128)S(1)}, u32[]{:S(2)}, u32[]{:S(2)}) collective-permute-start(f32[18,8,128]{2,1,0:T(8,128)S(1)} %get-tuple-element.84), channel_id=1, source_target_pairs={{0,4},{4,0},{1,5},{5,1},{2,6},{6,2},{3,7},{7,3},{8,12},{12,8},{9,1... | collective-permute-start | bytes 221192 | tf_op jit(solution)/shard_map/ppermute | solution.py:541
  20.3 4.0 %collective-permute-start.8 = (f32[9,8,128]{2,1,0:T(8,128)S(1)}, f32[9,8,128]{2,1,0:T(8,128)S(1)}, u32[]{:S(2)}, u32[]{:S(2)}) collective-permute-start(f32[9,8,128]{2,1,0:T(8,128)S(1)} %get-tuple-element.85), channel_id=1, source_target_pairs={{0,1},{1,2},{2,3},{3,0},{4,5},{5,6},{6,7},{7,4},{8,9},{9,10},{10,1... | collective-permute-start | bytes 110600 | tf_op jit(solution)/shard_map/ppermute | solution.py:541
  21.5 4.5 %collective-permute-start.9 = (f32[9,8,128]{2,1,0:T(8,128)S(1)}, f32[9,8,128]{2,1,0:T(8,128)S(1)}, u32[]{:S(2)}, u32[]{:S(2)}) collective-permute-start(f32[9,8,128]{2,1,0:T(8,128)S(1)} %get-tuple-element.88), channel_id=1, source_target_pairs={{0,3},{1,0},{2,1},{3,2},{4,7},{5,4},{6,5},{7,6},{8,11},{9,8},{10,9... | collective-permute-start | bytes 110600 | tf_op jit(solution)/shard_map/ppermute | solution.py:541
  26.5 8.8 %collective-permute-start.10 = (f32[12,8,256]{2,1,0:T(8,128)S(1)}, f32[12,8,256]{2,1,0:T(8,128)S(1)}, u32[]{:S(2)}, u32[]{:S(2)}) collective-permute-start(f32[12,8,256]{2,1,0:T(8,128)S(1)} %get-tuple-element.96), channel_id=1, source_target_pairs={{0,8},{8,0},{1,9},{9,1},{2,10},{10,2},{3,11},{11,3},{4,12},{12,4},... | collective-permute-start | bytes 294920 | tf_op jit(solution)/shard_map/ppermute | solution.py:541
  28.6 6.7 %collective-permute-start.11 = (f32[12,8,256]{2,1,0:T(8,128)S(1)}, f32[12,8,256]{2,1,0:T(8,128)S(1)}, u32[]{:S(2)}, u32[]{:S(2)}) collective-permute-start(f32[12,8,256]{2,1,0:T(8,128)S(1)} %get-tuple-element.97), channel_id=1, source_target_pairs={{0,248},{8,16},{16,8},{24,32},{32,24},{40,48},{48,40},{56,64},{64,... | collective-permute-start | bytes 294920 | tf_op jit(solution)/shard_map/ppermute | solution.py:541
  31.1 4.2 %collective-permute-start.12 = (f32[12,8,128]{2,1,0:T(8,128)S(1)}, f32[12,8,128]{2,1,0:T(8,128)S(1)}, u32[]{:S(2)}, u32[]{:S(2)}) collective-permute-start(f32[12,8,128]{2,1,0:T(8,128)S(1)} %get-tuple-element.98), channel_id=1, source_target_pairs={{0,4},{4,0},{1,5},{5,1},{2,6},{6,2},{3,7},{7,3},{8,12},{12,8},{9,1... | collective-permute-start | bytes 147464 | tf_op jit(solution)/shard_map/ppermute | solution.py:541
  31.1 4.2 %collective-permute-start.13 = (f32[6,8,128]{2,1,0:T(8,128)S(1)}, f32[6,8,128]{2,1,0:T(8,128)S(1)}, u32[]{:S(2)}, u32[]{:S(2)}) collective-permute-start(f32[6,8,128]{2,1,0:T(8,128)S(1)} %get-tuple-element.99), channel_id=1, source_target_pairs={{0,1},{1,2},{2,3},{3,0},{4,5},{5,6},{6,7},{7,4},{8,9},{9,10},{10,1... | collective-permute-start | bytes 73736 | tf_op jit(solution)/shard_map/ppermute | solution.py:541
  32.3 3.5 %collective-permute-start.14 = (f32[6,8,128]{2,1,0:T(8,128)S(1)}, f32[6,8,128]{2,1,0:T(8,128)S(1)}, u32[]{:S(2)}, u32[]{:S(2)}) collective-permute-start(f32[6,8,128]{2,1,0:T(8,128)S(1)} %get-tuple-element.104), channel_id=1, source_target_pairs={{0,3},{1,0},{2,1},{3,2},{4,7},{5,4},{6,5},{7,6},{8,11},{9,8},{10,9... | collective-permute-start | bytes 73736 | tf_op jit(solution)/shard_map/ppermute | solution.py:541
  36.3 8.6 %collective-permute-start.15 = (f32[12,8,256]{2,1,0:T(8,128)S(1)}, f32[12,8,256]{2,1,0:T(8,128)S(1)}, u32[]{:S(2)}, u32[]{:S(2)}) collective-permute-start(f32[12,8,256]{2,1,0:T(8,128)S(1)} %get-tuple-element.114), channel_id=1, source_target_pairs={{0,8},{8,0},{1,9},{9,1},{2,10},{10,2},{3,11},{11,3},{4,12},{12,4},... | collective-permute-start | bytes 294920 | tf_op jit(solution)/shard_map/ppermute | solution.py:541
  38.8 6.1 %collective-permute-start.16 = (f32[12,8,256]{2,1,0:T(8,128)S(1)}, f32[12,8,256]{2,1,0:T(8,128)S(1)}, u32[]{:S(2)}, u32[]{:S(2)}) collective-permute-start(f32[12,8,256]{2,1,0:T(8,128)S(1)} %get-tuple-element.115), channel_id=1, source_target_pairs={{0,248},{8,16},{16,8},{24,32},{32,24},{40,48},{48,40},{56,64},{64,... | collective-permute-start | bytes 294920 | tf_op jit(solution)/shard_map/ppermute | solution.py:541
  40.1 4.8 %collective-permute-start.17 = (f32[12,8,128]{2,1,0:T(8,128)S(1)}, f32[12,8,128]{2,1,0:T(8,128)S(1)}, u32[]{:S(2)}, u32[]{:S(2)}) collective-permute-start(f32[12,8,128]{2,1,0:T(8,128)S(1)} %get-tuple-element.116), channel_id=1, source_target_pairs={{0,4},{4,0},{1,5},{5,1},{2,6},{6,2},{3,7},{7,3},{8,12},{12,8},{9,1... | collective-permute-start | bytes 147464 | tf_op jit(solution)/shard_map/ppermute | solution.py:541
  40.6 4.3 %collective-permute-start.18 = (f32[6,8,128]{2,1,0:T(8,128)S(1)}, f32[6,8,128]{2,1,0:T(8,128)S(1)}, u32[]{:S(2)}, u32[]{:S(2)}) collective-permute-start(f32[6,8,128]{2,1,0:T(8,128)S(1)} %get-tuple-element.117), channel_id=1, source_target_pairs={{0,1},{1,2},{2,3},{3,0},{4,5},{5,6},{6,7},{7,4},{8,9},{9,10},{10,1... | collective-permute-start | bytes 73736 | tf_op jit(solution)/shard_map/ppermute | solution.py:541
  41.3 4.1 %collective-permute-start.19 = (f32[6,8,128]{2,1,0:T(8,128)S(1)}, f32[6,8,128]{2,1,0:T(8,128)S(1)}, u32[]{:S(2)}, u32[]{:S(2)}) collective-permute-start(f32[6,8,128]{2,1,0:T(8,128)S(1)} %get-tuple-element.122), channel_id=1, source_target_pairs={{0,3},{1,0},{2,1},{3,2},{4,7},{5,4},{6,5},{7,6},{8,11},{9,8},{10,9... | collective-permute-start | bytes 73736 | tf_op jit(solution)/shard_map/ppermute | solution.py:541
